TPU v7x, 32 devices: a whole 2x2x4 slice. The times are simulated.
32 devices in a mesh: row: 8 (over z, core), col: 4 (over y, x).
Axes of the slice: x: 2, y: 2, z: 4, core: 2. Of those that a mesh axis runs over, the one named last changes fastest.
Arguments:
- substrate: float32 [1024, 1024], P('row', 'col'), may hold values from 0.05 to 0.95
- activator: float32 [1024, 1024], P('row', 'col'), may hold values from 0 to 0.45
Outputs:
- substrate_section: float32 [1024, 1024], P('row', 'col')
- activator_section: float32 [1024, 1024], P('row', 'col')
All inputs are finite; a program needn't handle non-finite values.
Results may differ from a plain program's by a relative error of at most 0.00023.
Values sent between devices are 32-bit elements; how exact they have to be, the bound alone decides.
No kernel may reach another device: no remote copies, remote signals or barrier semaphores. Data moves between devices by JAX's collectives and lax.ppermute only.
A program may use at most 64 MiB of HBM per device.

v0:
```python
import math

import jax
import jax.numpy as jnp
import numpy as np
from jax import lax
from jax.experimental import pallas as pl
from jax.experimental.pallas import tpu as pltpu
from jax.sharding import PartitionSpec as P

FEED_RATE = 0.037
KILL_RATE = 0.06
TIME_STEP = 8.0
SUBSTRATE_DIFFUSION = 4e-07
ACTIVATOR_DIFFUSION = 2e-07
LANES = 128
SUBLANES = 8
VMEM = pl.BlockSpec(memory_space=pltpu.VMEM)
SMEM = pl.BlockSpec(memory_space=pltpu.SMEM)


def basis_matrices(total):
    radix = total // LANES
    b = np.arange(LANES, dtype=np.int64)[:, None]
    k2 = np.arange(LANES, dtype=np.int64)[None, :]

    def angles(k1):
        return (b * (k1 + radix * k2) % total) * (2.0 * np.pi / total)

    matrices = np.zeros((radix // 2, 2 * LANES, 2 * LANES))
    for half, k1 in enumerate((0, radix // 2)):
        theta = angles(k1)
        part = slice(half * LANES, (half + 1) * LANES)
        matrices[0, part, part] = np.cos(theta) + np.sin(theta)
    for k1 in range(1, radix // 2):
        cosine, sine = np.cos(angles(k1)), np.sin(angles(k1))
        matrices[k1] = np.block([[cosine, -sine], [sine, cosine]])
    return matrices


def split_constant(matrices):
    high = matrices.astype(jnp.bfloat16)
    low = (matrices - high.astype(np.float64)).astype(jnp.bfloat16)
    return jnp.asarray(high), jnp.asarray(low)


def split_value(values):
    high = values.astype(jnp.bfloat16)
    low = (values - high.astype(jnp.float32)).astype(jnp.bfloat16)
    return high, low


def dot(left, right):
    return jnp.dot(left, right, preferred_element_type=jnp.float32)


def dot_pairs(left, right):
    return dot(left[0], right[0]) + (dot(left[0], right[1]) + dot(left[1], right[0]))


def turn(value, k, period, sign):
    real, imag = value
    if k == 0:
        return value
    if 4 * k == period:
        return (-sign * imag, sign * real) if imag is not None else (None, sign * real)
    cosine, sine = math.cos(2.0 * math.pi * k / period), sign * math.sin(2.0 * math.pi * k / period)
    if imag is None:
        return (real * cosine, real * sine)
    if 8 * k == period:
        return ((real - sign * imag) * cosine, (imag + sign * real) * cosine)
    return (real * cosine - imag * sine, real * sine + imag * cosine)


def plus(left, right):
    if left is None or right is None:
        return left if right is None else right
    return left + right


def minus(left, right):
    if right is None:
        return left
    return -right if left is None else left - right


def real_dft(values):
    n = len(values)
    if n == 1:
        return [(values[0], None)]
    even, odd = real_dft(values[0::2]), real_dft(values[1::2])
    out = [None] * (n // 2 + 1)
    for k in range(n // 4 + 1):
        turned = turn(odd[k], k, n, -1.0)
        if n // 2 - k != k:
            out[n // 2 - k] = (minus(even[k][0], turned[0]), minus(turned[1], even[k][1]))
        out[k] = (plus(even[k][0], turned[0]), plus(even[k][1], turned[1]))
    return out


def real_dft_transposed(spectrum):
    n = 2 * (len(spectrum) - 1)
    if n == 0:
        return [spectrum[0][0]]
    even, odd = [], []
    for k in range(n // 4 + 1):
        near, far = spectrum[k], spectrum[n // 2 - k]
        if k == 0:
            even.append((near[0] + far[0], None))
            odd.append((near[0] - far[0], None))
        elif 4 * k == n:
            even.append((near[0], None))
            odd.append((-near[1], None))
        else:
            even.append((near[0] + far[0], near[1] - far[1]))
            odd.append(turn((near[0] - far[0], near[1] + far[1]), k, n, 1.0))
    out = [None] * n
    out[0::2] = real_dft_transposed(even)
    out[1::2] = real_dft_transposed(odd)
    return out


def paired(spectrum, axis):
    half = len(spectrum) - 1
    rows = [(spectrum[0][0], spectrum[half][0])] + spectrum[1:half]
    return [jnp.concatenate(row, axis=axis) for row in rows]


def unpaired(products, axis):
    def halves(value):
        return lax.slice_in_dim(value, 0, LANES, axis=axis), lax.slice_in_dim(value, LANES, 2 * LANES, axis=axis)

    parts = [halves(value) for value in products]
    first, last = parts[0]
    return [(first, None)] + parts[1:] + [(last, None)]


def lane_chunk(shape, width):
    return lax.broadcasted_iota(jnp.int32, shape, len(shape) - 1) // width


def pick_chunks(pieces, width):
    chunk = lane_chunk(pieces[0].shape, width)
    out = pieces[-1]
    for index in range(len(pieces) - 2, -1, -1):
        out = jnp.where(chunk == index, pieces[index], out)
    return out


def rolled(value, chunks, width):
    shift = chunks * width % LANES
    return pltpu.roll(value, shift, 1) if shift else value


def wave_squares(k1, k2, total):
    radix = total // LANES
    wave = k1 + radix * k2
    signed = jnp.where(2 * wave < total, wave, wave - total).astype(jnp.float32)
    angular = (2.0 * math.pi) * signed
    return angular * angular


def tables_kernel(total_rows, total_cols, width, device_ref, growth_ref, forcing_ref):
    radix = total_rows // LANES
    chunks = LANES // width
    device = device_ref[0]
    tile, place = device // chunks, device % chunks
    lane = lax.broadcasted_iota(jnp.int32, (1, LANES), 1)
    col_class = jnp.where(tile == 0, 0, jnp.where(tile == 1, total_cols // LANES // 2, tile // 2))
    col_squares = wave_squares(col_class, place * width + lane % width, total_cols)
    col_scale = jnp.where(tile < 2, 1.0 / total_cols, 2.0 / total_cols).astype(jnp.float32)
    first = lane < width
    diffusion = jnp.where(first, SUBSTRATE_DIFFUSION, ACTIVATOR_DIFFUSION).astype(jnp.float32)
    decay = jnp.where(first, FEED_RATE, FEED_RATE + KILL_RATE).astype(jnp.float32)
    sign = jnp.where(first, -1.0, 1.0).astype(jnp.float32)
    k2 = lax.broadcasted_iota(jnp.int32, (LANES, LANES), 0)
    for index in range(radix // 2):
        for half in range(2):
            k1 = half * (radix // 2) if index == 0 else index
            scale = col_scale * ((1.0 if index == 0 else 2.0) / total_rows)
            linear = -diffusion * (wave_squares(k1, k2, total_rows) + col_squares) - decay
            growth = jnp.exp(linear * (0.5 * TIME_STEP))
            rows = slice(half * LANES, (half + 1) * LANES)
            growth_ref[index, rows, :] = growth * scale
            forcing_ref[index, rows, :] = (growth - 1.0) / linear * (scale * sign)


def forward_kernel(packed, place_ref, *refs):
    *block_refs, high_ref, low_ref, out_ref, buffer_ref = refs
    count = len(block_refs)
    place = place_ref[0]
    for step, block_ref in enumerate(block_refs):
        buffer_ref[place ^ step] = block_ref[...]
    cols = buffer_ref.shape[-1]
    height = buffer_ref.shape[2]
    tiles = []
    for source in range(count):
        for tile in range(cols // LANES):
            part = slice(tile * LANES, (tile + 1) * LANES)
            substrate = buffer_ref[source, 0, :, part]
            activator = buffer_ref[source, 1, :, part]
            tiles.append(jnp.concatenate([substrate, activator, substrate * activator * activator], axis=0))
    operands = paired(real_dft(tiles), 1)
    for index, operand in enumerate(operands):
        product = dot_pairs(split_value(operand), (high_ref[index], low_ref[index]))
        for half in range(2):
            tile = 2 * index + half
            spectrum = product[:, half * LANES : (half + 1) * LANES]
            if not packed:
                out_ref[tile] = spectrum
                continue
            width = LANES // count
            turns = [rolled(spectrum, shift, width) for shift in range(count)]
            for chunk in range(count):
                for field in range(3):
                    base = field * height
                    pieces = [
                        turns[(group - chunk) % count][base + group * SUBLANES : base + (group + 1) * SUBLANES]
                        for group in range(count)
                    ]
                    out_ref[tile * count + chunk, field * SUBLANES : (field + 1) * SUBLANES, :] = pick_chunks(
                        pieces, width
                    )


def advance_kernel(packed, count, *refs):
    if packed:
        in_ref, growth_ref, forcing_ref, high_ref, low_ref, high_t_ref, low_t_ref, out_ref = refs
        width = LANES // count
        radix = in_ref.shape[0] // count
        tiles = []
        for band in range(radix):
            own_rows, source_rows = [], []
            for source in range(count):
                block = in_ref[band * count + source]
                turns = [
                    [rolled(block[field * SUBLANES : (field + 1) * SUBLANES], -shift, width) for shift in range(count)]
                    for field in range(3)
                ]
                low_half = lane_chunk((SUBLANES, LANES), width) == 0
                for group in range(count):
                    near, next_near = group, (group - 1) % count
                    own_rows.append(jnp.where(low_half, turns[0][near], turns[1][next_near]))
                    source_rows.append(jnp.where(low_half, turns[2][near], turns[2][next_near]))
            own = jnp.concatenate(own_rows, axis=0)
            tiles.append(jnp.concatenate([own, jnp.concatenate(source_rows, axis=0)], axis=1))
    else:
        own_ref, source_ref, growth_ref, forcing_ref, high_ref, low_ref, high_t_ref, low_t_ref, out_ref = refs
        radix = own_ref.shape[0]
        tiles = [jnp.concatenate([own_ref[band], source_ref[band]], axis=1) for band in range(radix)]
    operands = paired(real_dft(tiles), 0)
    products = []
    for index, operand in enumerate(operands):
        spectrum = dot_pairs((high_t_ref[index], low_t_ref[index]), split_value(operand))
        advanced = growth_ref[index] * spectrum[:, :LANES] + forcing_ref[index] * spectrum[:, LANES:]
        products.append(dot_pairs((high_ref[index], low_ref[index]), split_value(advanced)))
    bands = real_dft_transposed(unpaired(products, 0))
    for band, value in enumerate(bands):
        if not packed:
            out_ref[band] = value
            continue
        height = LANES // count
        for target in range(count):
            for field in range(2):
                pieces = [
                    rolled(
                        value[target * height + group * SUBLANES : target * height + (group + 1) * SUBLANES],
                        group - field,
                        width,
                    )
                    for group in range(count)
                ]
                out_ref[band * count + target, field * SUBLANES : (field + 1) * SUBLANES, :] = pick_chunks(
                    pieces, width
                )


def inverse_kernel(packed, count, shift, place_ref, in_ref, high_t_ref, low_t_ref, out_ref):
    place = place_ref[0]
    radix = 2 * high_t_ref.shape[0]
    height = out_ref.shape[2]
    cols = out_ref.shape[3]
    tiles = []
    for tile in range(radix):
        if not packed:
            tiles.append(in_ref[tile])
            continue
        width = LANES // count
        turns = [[rolled(in_ref[tile * count + chunk], step, width) for step in range(count)] for chunk in range(count)]
        rows = []
        for field in range(2):
            part = slice(field * SUBLANES, (field + 1) * SUBLANES)
            for group in range(count):
                rows.append(
                    pick_chunks([turns[chunk][(chunk - group) % count][part] for chunk in range(count)], width)
                )
        tiles.append(jnp.concatenate(rows, axis=0))
    products = []
    for index in range(radix // 2):
        operand = jnp.concatenate([tiles[2 * index], tiles[2 * index + 1]], axis=1)
        products.append(dot_pairs(split_value(operand), (high_t_ref[index], low_t_ref[index])))
    values = real_dft_transposed(unpaired(products, 1))
    per_target = cols // LANES
    for index, value in enumerate(values):
        target, tile = index // per_target, index % per_target
        part = slice(tile * LANES, (tile + 1) * LANES)
        out_ref[place ^ target, 0, :, part] = value[:height] + shift
        out_ref[place ^ target, 1, :, part] = value[height:]


def call(kernel, out_shape, specs, operands, scratch=()):
    return pl.pallas_call(
        kernel,
        out_shape=out_shape,
        in_specs=specs,
        out_specs=jax.tree.map(lambda _: VMEM, out_shape),
        scratch_shapes=list(scratch),
    )(*operands)


def float_shape(*shape):
    return jax.ShapeDtypeStruct(shape, jnp.float32)


def swap_blocks(blocks):
    count = len(blocks)
    return [blocks[0]] + [
        lax.ppermute(blocks[step], "col", [(s, s ^ step) for s in range(count)]) for step in range(1, count)
    ]


def on_device(substrate, activator):
    row_count, col_count = substrate.shape
    bands, count = lax.axis_size("row"), lax.axis_size("col")
    total_rows, total_cols = row_count * bands, col_count * count
    height = row_count // count
    radix = total_cols // LANES
    width = total_cols // (bands * count)
    assert row_count == LANES and total_rows == total_cols and count & (count - 1) == 0
    packed = height == SUBLANES * count and width * count == LANES
    place = lax.axis_index("col")
    places = place[None].astype(jnp.int32)
    devices = (lax.axis_index("row") * count + place)[None].astype(jnp.int32)
    matrices = basis_matrices(total_rows)
    high, low = split_constant(matrices)
    high_t, low_t = split_constant(np.swapaxes(matrices, 1, 2))

    fields = jnp.stack([substrate, activator]).reshape(2, count, height, col_count)
    blocks = swap_blocks(
        [lax.dynamic_index_in_dim(fields, place ^ step, 1, keepdims=False) for step in range(count)]
    )
    growth, forcing = call(
        lambda *refs: tables_kernel(total_rows, total_cols, width, *refs),
        [float_shape(radix // 2, 2 * LANES, LANES)] * 2,
        [SMEM],
        (devices,),
    )
    spectra = call(
        lambda *refs: forward_kernel(packed, *refs),
        float_shape(bands * count, 3 * SUBLANES, LANES) if packed else float_shape(radix, 3 * height, LANES),
        [SMEM] + [VMEM] * (count + 2),
        (places, *blocks, high, low),
        [pltpu.VMEM((count, 2, height, col_count), jnp.float32)],
    )
    axes = ("row", "col")
    if packed:
        spectra = (lax.all_to_all(spectra, axes, 0, 0, tiled=True),)
    else:
        spectra = spectra.reshape(radix, 3, height, LANES // width, width)
        spectra = jnp.transpose(spectra, (0, 3, 1, 2, 4)).reshape(bands * count, -1)
        spectra = lax.all_to_all(spectra, axes, 0, 0, tiled=True)
        spectra = jnp.transpose(spectra.reshape(bands, count, 3, height, width), (2, 0, 1, 3, 4))
        spectra = spectra.reshape(3, bands, row_count, width)
        rest = jnp.zeros((bands, row_count, LANES - 2 * width), jnp.float32)
        spectra = (
            jnp.concatenate([spectra[0], spectra[1], rest], axis=2),
            jnp.concatenate([spectra[2], spectra[2], rest], axis=2),
        )
    advanced = call(
        lambda *refs: advance_kernel(packed, count, *refs),
        float_shape(bands * count, 2 * SUBLANES, LANES) if packed else float_shape(bands, row_count, LANES),
        [VMEM] * (len(spectra) + 6),
        (*spectra, growth, forcing, high, low, high_t, low_t),
    )
    if packed:
        advanced = lax.all_to_all(advanced, axes, 0, 0, tiled=True)
    else:
        advanced = advanced[:, :, : 2 * width].reshape(bands, count, height, 2, width)
        advanced = jnp.transpose(advanced, (0, 1, 3, 2, 4)).reshape(bands * count, -1)
        advanced = lax.all_to_all(advanced, axes, 0, 0, tiled=True)
        advanced = jnp.transpose(advanced.reshape(radix, LANES // width, 2, height, width), (0, 2, 3, 1, 4))
        advanced = advanced.reshape(radix, 2 * height, LANES)
    shift = FEED_RATE * math.expm1(-FEED_RATE * 0.5 * TIME_STEP) / -FEED_RATE
    values = call(
        lambda *refs: inverse_kernel(packed, count, shift, *refs),
        float_shape(count, 2, height, col_count),
        [SMEM] + [VMEM] * 3,
        (places, advanced, high_t, low_t),
    )
    blocks = swap_blocks([values[step] for step in range(count)])
    out = jnp.zeros((2, count, height, col_count), jnp.float32)
    for step, block in enumerate(blocks):
        out = lax.dynamic_update_index_in_dim(out, block, place ^ step, 1)
    out = out.reshape(2, row_count, col_count)
    return (out[0], out[1])


def solution(mesh):
    in_specs = (P("row", "col"), P("row", "col"))
    out_specs = (P("row", "col"), P("row", "col"))
    return jax.shard_map(
        on_device, mesh=mesh, in_specs=in_specs, out_specs=out_specs, check_vma=False
    )
```

profile of v0, /device:TPU:0, one launch (start us, length us, event | category | flops | bytes accessed | tf_op | source)
XLA Modules:
  0.0 64.2 jit_solution(8522630979795609690)
XLA Ops:
  0.7 1.5 %fusion.1 = (f32[2,32,256]{2,1,0:T(8,128)S(1)}, f32[2,32,256]{2,1,0:T(8,128)}, f32[2,32,256]{2,1,0:T(8,128)S(1)}, f32[2,32,256]{2,1,0:T(8,128)S(1)}) fusion(s32[]{:T(128)S(6)} %select_n.21, f32[1,4,32,256]{3,2,0,1:T(8,128)} %bitcast.36, f32[1,4,32,256]{3,2,0,1:T(8,128)} %bitcast.37, s32[]{:T(128)S(6)} %select_n.18, s32[]{:T(128)S(6)} %select_n.19, ...), kind=kLoop, calls=%fused_computation.9 | loop fusion | flops 65536 | bytes 524304 | tf_op jit(solution)/shard_map/jit(dynamic_index_in_dim)/squeeze | solution.py:350
  2.2 3.0 %collective-permute-start = (f32[2,32,256]{2,1,0:T(8,128)S(1)}, f32[2,32,256]{2,1,0:T(8,128)S(1)}, u32[]{:S(2)}, u32[]{:S(2)}) collective-permute-start(f32[2,32,256]{2,1,0:T(8,128)S(1)} %get-tuple-element.13), channel_id=1, source_target_pairs={{0,1},{1,0},{2,3},{3,2},{4,5},{5,4},{6,7},{7,6},{8,9},{9,8},{10,11... | collective-permute-start | bytes 196616 | tf_op jit(solution)/shard_map/ppermute | solution.py:328
  5.2 1.5 %collective-permute-start.1 = (f32[2,32,256]{2,1,0:T(8,128)S(1)}, f32[2,32,256]{2,1,0:T(8,128)S(1)}, u32[]{:S(2)}, u32[]{:S(2)}) collective-permute-start(f32[2,32,256]{2,1,0:T(8,128)S(1)} %get-tuple-element.14), channel_id=1, source_target_pairs={{0,2},{1,3},{2,0},{3,1},{4,6},{5,7},{6,4},{7,5},{8,10},{9,11},{10,... | collective-permute-start | bytes 196616 | tf_op jit(solution)/shard_map/ppermute | solution.py:328
  6.7 0.0 collective-permute-start.2
  6.7 0.9 %collective-permute-done.refs_2_ = f32[2,32,256]{2,1,0:T(8,128)S(1)} collective-permute-done((f32[2,32,256]{2,1,0:T(8,128)S(1)}, f32[2,32,256]{2,1,0:T(8,128)S(1)}, u32[]{:S(2)}, u32[]{:S(2)}) %collective-permute-start) | collective-permute-done | bytes 65568 | tf_op jit(solution)/shard_map/ppermute | solution.py:328
  7.5 0.0 copy-start.1
  7.5 1.9 %collective-permute-done.1.refs_3_ = f32[2,32,256]{2,1,0:T(8,128)S(1)} collective-permute-done((f32[2,32,256]{2,1,0:T(8,128)S(1)}, f32[2,32,256]{2,1,0:T(8,128)S(1)}, u32[]{:S(2)}, u32[]{:S(2)}) %collective-permute-start.1) | collective-permute-done | bytes 65568 | tf_op jit(solution)/shard_map/ppermute | solution.py:328
  9.4 0.0 copy-start.2
  9.4 2.4 %collective-permute-done.2.refs_4_ = f32[2,32,256]{2,1,0:T(8,128)S(1)} collective-permute-done((f32[2,32,256]{2,1,0:T(8,128)S(1)}, f32[2,32,256]{2,1,0:T(8,128)S(1)}, u32[]{:S(2)}, u32[]{:S(2)}) %collective-permute-start.2) | collective-permute-done | bytes 65568 | tf_op jit(solution)/shard_map/ppermute | solution.py:328
  11.8 0.0 copy-start.3
  11.8 0.0 copy-done.1
  11.8 0.0 copy-done.2
  11.8 0.6 copy-done.3
  12.5 2.8 %shard_map.77 = f32[32,24,128]{2,1,0:T(8,128)} custom-call(s32[1]{0:T(128)} %bitcast.refs_0_, f32[2,32,256]{2,1,0:T(8,128)} %get-tuple-element.12.refs_1_, f32[2,32,256]{2,1,0:T(8,128)} %copy-done.1, f32[2,32,256]{2,1,0:T(8,128)} %copy-done.2, f32[2,32,256]{2,1,0:T(8,128)} %copy-done.3, bf16[4,256,256]{2,1,0:T(8,128)(2,1)} %constant.48.clone.refs_5_.refs_3_, ...), custom_call_target="tpu_custom_call" | custom-call | tf_op jit(solution)/shard_map/pallas_call | solution.py:312
  15.2 4.0 %all-to-all-start = ((f32[32,24,128]{2,1,0:T(8,128)}), f32[32,24,128]{2,1,0:T(8,128)S(1)}, u32[]{:S(2)}, u32[]{:S(2)}) async-start(f32[32,24,128]{2,1,0:T(8,128)} %shard_map.77), calls=%async_computation | async-start | bytes 786432 | tf_op jit(solution)/shard_map/all_to_all | solution.py:367
  19.2 1.2 %shard_map.78 = (f32[4,256,128]{2,1,0:T(8,128)}, f32[4,256,128]{2,1,0:T(8,128)}) custom-call(s32[1]{0:T(128)} %bitcast.9.refs_0_), custom_call_target="tpu_custom_call" | custom-call | tf_op jit(solution)/shard_map/pallas_call | solution.py:312
  20.4 12.4 %all-to-all-done.refs_0_ = f32[32,24,128]{2,1,0:T(8,128)S(1)} async-done(((f32[32,24,128]{2,1,0:T(8,128)}), f32[32,24,128]{2,1,0:T(8,128)S(1)}, u32[]{:S(2)}, u32[]{:S(2)}) %all-to-all-start) | async-done | bytes 393248 | tf_op jit(solution)/shard_map/all_to_all | solution.py:367
  32.8 0.0 copy-start
  32.8 0.8 %copy-done = f32[32,24,128]{2,1,0:T(8,128)} copy-done((f32[32,24,128]{2,1,0:T(8,128)}, f32[32,24,128]{2,1,0:T(8,128)S(1)}, u32[]{:S(2)}) %copy-start) | copy-done | bytes 393240
  33.6 4.8 %shard_map.79 = f32[32,16,128]{2,1,0:T(8,128)} custom-call(f32[32,24,128]{2,1,0:T(8,128)} %copy-done, f32[4,256,128]{2,1,0:T(8,128)} %get-tuple-element.4.refs_1_, f32[4,256,128]{2,1,0:T(8,128)} %get-tuple-element.5.refs_2_, bf16[4,256,256]{2,1,0:T(8,128)(2,1)} %constant.48.clone.refs_5_.refs_3_, bf16[4,256,256]{2,1,0:T(8,128)(2,1)} %constant.49.clone.refs_6_.refs_4_, ...), custom_call_target="tpu_custom_call" | custom-call | tf_op jit(solution)/shard_map/pallas_call | solution.py:312
  38.4 14.2 %all_to_all.10.refs_1_ = f32[32,16,128]{2,1,0:T(8,128)} all-to-all(f32[32,16,128]{2,1,0:T(8,128)} %shard_map.79), channel_id=1, replica_groups=mesh['row'=8,'col'=4] {'row','col'}, dimensions={0} | all-to-all | bytes 524288 | tf_op jit(solution)/shard_map/all_to_all | solution.py:386
  52.6 2.5 %shard_map.80 = f32[4,2,32,256]{3,2,1,0:T(8,128)} custom-call(s32[1]{0:T(128)} %bitcast.refs_0_, f32[32,16,128]{2,1,0:T(8,128)} %all_to_all.10.refs_1_, bf16[4,256,256]{2,1,0:T(8,128)(2,1)} %constant.50.clone.refs_5_.refs_2_, bf16[4,256,256]{2,1,0:T(8,128)(2,1)} %constant.51.clone.refs_6_.refs_3_), custom_call_target="tpu_custom_call" | custom-call | tf_op jit(solution)/shard_map/pallas_call | solution.py:312
  55.0 0.9 %slice_bitcast_fusion = (f32[2,32,256]{2,1,0:T(8,128)S(1)}, f32[2,32,256]{2,1,0:T(8,128)S(1)}, f32[2,32,256]{2,1,0:T(8,128)S(1)}) fusion(f32[4,2,32,256]{3,2,1,0:T(8,128)} %shard_map.80), kind=kLoop, calls=%fused_computation.16 | loop fusion | bytes 393216 | tf_op jit(solution)/shard_map/squeeze | solution.py:400
  56.0 0.1 collective-permute-start.3
  56.1 0.9 %fusion.8 = f32[2,4,32,256]{3,2,0,1:T(8,128)S(1)} fusion(f32[2,4,32,256]{3,2,0,1:T(8,128)S(1)} %broadcast_in_dim.22, s32[]{:T(128)S(6)} %select_n.18, f32[4,2,32,256]{3,2,1,0:T(8,128)} %shard_map.80), kind=kLoop, calls=%fused_computation.20 | loop fusion | bytes 131076 | tf_op jit(solution)/shard_map/jit(dynamic_update_index_in_dim)/dynamic_update_slice | solution.py:403
  56.9 1.4 %collective-permute-start.4 = (f32[2,32,256]{2,1,0:T(8,128)S(1)}, f32[2,32,256]{2,1,0:T(8,128)S(1)}, u32[]{:S(2)}, u32[]{:S(2)}) collective-permute-start(f32[2,32,256]{2,1,0:T(8,128)S(1)} %get-tuple-element.9), channel_id=1, source_target_pairs={{0,2},{1,3},{2,0},{3,1},{4,6},{5,7},{6,4},{7,5},{8,10},{9,11},{10,... | collective-permute-start | bytes 196616 | tf_op jit(solution)/shard_map/ppermute | solution.py:328
  58.3 2.1 %collective-permute-start.5 = (f32[2,32,256]{2,1,0:T(8,128)S(1)}, f32[2,32,256]{2,1,0:T(8,128)S(1)}, u32[]{:S(2)}, u32[]{:S(2)}) collective-permute-start(f32[2,32,256]{2,1,0:T(8,128)S(1)} %get-tuple-element.8), channel_id=1, source_target_pairs={{0,3},{1,2},{2,1},{3,0},{4,7},{5,6},{6,5},{7,4},{8,11},{9,10},{10,... | collective-permute-start | bytes 196616 | tf_op jit(solution)/shard_map/ppermute | solution.py:328
  60.4 0.0 collective-permute-done.3
  60.4 1.5 %collective-permute-done.4 = f32[2,32,256]{2,1,0:T(8,128)S(1)} collective-permute-done((f32[2,32,256]{2,1,0:T(8,128)S(1)}, f32[2,32,256]{2,1,0:T(8,128)S(1)}, u32[]{:S(2)}, u32[]{:S(2)}) %collective-permute-start.4) | collective-permute-done | bytes 65568 | tf_op jit(solution)/shard_map/ppermute | solution.py:328
  61.9 1.5 %collective-permute-done.5 = f32[2,32,256]{2,1,0:T(8,128)S(1)} collective-permute-done((f32[2,32,256]{2,1,0:T(8,128)S(1)}, f32[2,32,256]{2,1,0:T(8,128)S(1)}, u32[]{:S(2)}, u32[]{:S(2)}) %collective-permute-start.5) | collective-permute-done | bytes 65568 | tf_op jit(solution)/shard_map/ppermute | solution.py:328
  63.5 0.7 %fusion.9 = (f32[1,4,32,256]{3,2,1,0:T(8,128)}, f32[1,4,32,256]{3,2,1,0:T(8,128)}) fusion(f32[2,4,32,256]{3,2,1,0:T(8,128)S(1)} %bitcast_dynamic-update-slice_fusion), kind=kLoop, calls=%fused_computation.24 | loop fusion | bytes 524288 | tf_op jit(solution)/shard_map/slice | solution.py:405
  (5 shorter events, 0.1 us)
Async XLA Ops:
  2.2 5.3 %collective-permute-start = (f32[2,32,256]{2,1,0:T(8,128)S(1)}, f32[2,32,256]{2,1,0:T(8,128)S(1)}, u32[]{:S(2)}, u32[]{:S(2)}) collective-permute-start(f32[2,32,256]{2,1,0:T(8,128)S(1)} %get-tuple-element.13), channel_id=1, source_target_pairs={{0,1},{1,0},{2,3},{3,2},{4,5},{5,4},{6,7},{7,6},{8,9},{9,8},{10,11... | collective-permute-start | bytes 196616 | tf_op jit(solution)/shard_map/ppermute | solution.py:328
  5.2 4.3 %collective-permute-start.1 = (f32[2,32,256]{2,1,0:T(8,128)S(1)}, f32[2,32,256]{2,1,0:T(8,128)S(1)}, u32[]{:S(2)}, u32[]{:S(2)}) collective-permute-start(f32[2,32,256]{2,1,0:T(8,128)S(1)} %get-tuple-element.14), channel_id=1, source_target_pairs={{0,2},{1,3},{2,0},{3,1},{4,6},{5,7},{6,4},{7,5},{8,10},{9,11},{10,... | collective-permute-start | bytes 196616 | tf_op jit(solution)/shard_map/ppermute | solution.py:328
  6.7 5.2 %collective-permute-start.2 = (f32[2,32,256]{2,1,0:T(8,128)S(1)}, f32[2,32,256]{2,1,0:T(8,128)S(1)}, u32[]{:S(2)}, u32[]{:S(2)}) collective-permute-start(f32[2,32,256]{2,1,0:T(8,128)S(1)} %get-tuple-element.11), channel_id=1, source_target_pairs={{0,3},{1,2},{2,1},{3,0},{4,7},{5,6},{6,5},{7,4},{8,11},{9,10},{10,... | collective-permute-start | bytes 196616 | tf_op jit(solution)/shard_map/ppermute | solution.py:328
  7.5 4.3 %copy-start.1 = (f32[2,32,256]{2,1,0:T(8,128)}, f32[2,32,256]{2,1,0:T(8,128)S(1)}, u32[]{:S(2)}) copy-start(f32[2,32,256]{2,1,0:T(8,128)S(1)} %collective-permute-done.refs_2_) | copy-start | bytes 196612
  9.4 2.4 %copy-start.2 = (f32[2,32,256]{2,1,0:T(8,128)}, f32[2,32,256]{2,1,0:T(8,128)S(1)}, u32[]{:S(2)}) copy-start(f32[2,32,256]{2,1,0:T(8,128)S(1)} %collective-permute-done.1.refs_3_) | copy-start | bytes 196612
  11.8 0.6 copy-start.3
  15.2 17.6 %all-to-all-start = ((f32[32,24,128]{2,1,0:T(8,128)}), f32[32,24,128]{2,1,0:T(8,128)S(1)}, u32[]{:S(2)}, u32[]{:S(2)}) async-start(f32[32,24,128]{2,1,0:T(8,128)} %shard_map.77), calls=%async_computation | async-start | bytes 786432 | tf_op jit(solution)/shard_map/all_to_all | solution.py:367
  32.8 0.8 %copy-start = (f32[32,24,128]{2,1,0:T(8,128)}, f32[32,24,128]{2,1,0:T(8,128)S(1)}, u32[]{:S(2)}) copy-start(f32[32,24,128]{2,1,0:T(8,128)S(1)} %all-to-all-done.refs_0_) | copy-start | bytes 1179652
  56.0 4.4 %collective-permute-start.3 = (f32[2,32,256]{2,1,0:T(8,128)S(1)}, f32[2,32,256]{2,1,0:T(8,128)S(1)}, u32[]{:S(2)}, u32[]{:S(2)}) collective-permute-start(f32[2,32,256]{2,1,0:T(8,128)S(1)} %get-tuple-element.10), channel_id=1, source_target_pairs={{0,1},{1,0},{2,3},{3,2},{4,5},{5,4},{6,7},{7,6},{8,9},{9,8},{10,11... | collective-permute-start | bytes 196616 | tf_op jit(solution)/shard_map/ppermute | solution.py:328
  56.9 5.0 %collective-permute-start.4 = (f32[2,32,256]{2,1,0:T(8,128)S(1)}, f32[2,32,256]{2,1,0:T(8,128)S(1)}, u32[]{:S(2)}, u32[]{:S(2)}) collective-permute-start(f32[2,32,256]{2,1,0:T(8,128)S(1)} %get-tuple-element.9), channel_id=1, source_target_pairs={{0,2},{1,3},{2,0},{3,1},{4,6},{5,7},{6,4},{7,5},{8,10},{9,11},{10,... | collective-permute-start | bytes 196616 | tf_op jit(solution)/shard_map/ppermute | solution.py:328
  58.3 5.2 %collective-permute-start.5 = (f32[2,32,256]{2,1,0:T(8,128)S(1)}, f32[2,32,256]{2,1,0:T(8,128)S(1)}, u32[]{:S(2)}, u32[]{:S(2)}) collective-permute-start(f32[2,32,256]{2,1,0:T(8,128)S(1)} %get-tuple-element.8), channel_id=1, source_target_pairs={{0,3},{1,2},{2,1},{3,0},{4,7},{5,6},{6,5},{7,4},{8,11},{9,10},{10,... | collective-permute-start | bytes 196616 | tf_op jit(solution)/shard_map/ppermute | solution.py:328
where the time goes:
time: 64.7 us; the launch traced here: 64.2 us
  waiting for transfers between devices  20.6 us (32%)
  blocking collectives  14.2 us (22%)
  starting transfers between devices  12 us (19%)
  Pallas kernels  11.2 us (17%)
  local copies, waits for them, and re-layouts  3.93 us (6%)
  other arithmetic  1.53 us (2%)
  between operations  0.72 us (1%)
    all_to_all x1, blocking collectives, on_device(): advanced = lax.all_to_all(advanced, axes, 0, 0, tiled=True)  14.2 us
    all_to_all x1, waiting for transfers between devices, on_device(): spectra = (lax.all_to_all(spectra, axes, 0, 0, tiled=True),)  12.4 us
    pallas_call x4, Pallas kernels, call(): pl.pallas_call(kernel, out_shape=out_shape, in_specs=specs, out_specs=jax...  11.2 us
    ppermute x6, waiting for transfers between devices, swap_blocks(): lax.ppermute(blocks[step], 'col', [(s, s ^ step) for s in range(count)])  8.17 us
    ppermute x6, starting transfers between devices, swap_blocks(): lax.ppermute(blocks[step], 'col', [(s, s ^ step) for s in range(count)])  8.03 us
    all_to_all x1, starting transfers between devices, on_device(): spectra = (lax.all_to_all(spectra, axes, 0, 0, tiled=True),)  3.97 us
    squeeze x1, other arithmetic, on_device(): lax.dynamic_index_in_dim(fields, place ^ step, 1, keepdims=False)  1.53 us
    unnamed x8, local copies, waits for them, and re-layouts  1.39 us
  transfers between devices with their start and end apart: 7, of which 6 were waited for; matrix products, arithmetic and copies ran while one was open for 1% of the time, Pallas kernels for 2%

commit v1 on v0

--- a/solution.py
+++ b/solution.py
@@ -15,6 +15,7 @@
 ACTIVATOR_DIFFUSION = 2e-07
 LANES = 128
 SUBLANES = 8
+VMEM_LIMIT = 36 << 20
 VMEM = pl.BlockSpec(memory_space=pltpu.VMEM)
 SMEM = pl.BlockSpec(memory_space=pltpu.SMEM)
 
@@ -186,7 +187,7 @@
 
 
 def forward_kernel(packed, place_ref, *refs):
-    *block_refs, high_ref, low_ref, out_ref, buffer_ref = refs
+    *block_refs, high_ref, low_ref, _, out_ref, buffer_ref = refs
     count = len(block_refs)
     place = place_ref[0]
     for step, block_ref in enumerate(block_refs):
@@ -315,6 +316,7 @@
         in_specs=specs,
         out_specs=jax.tree.map(lambda _: VMEM, out_shape),
         scratch_shapes=list(scratch),
+        compiler_params=pltpu.CompilerParams(vmem_limit_bytes=VMEM_LIMIT),
     )(*operands)
 
 
@@ -358,8 +360,8 @@
     spectra = call(
         lambda *refs: forward_kernel(packed, *refs),
         float_shape(bands * count, 3 * SUBLANES, LANES) if packed else float_shape(radix, 3 * height, LANES),
-        [SMEM] + [VMEM] * (count + 2),
-        (places, *blocks, high, low),
+        [SMEM] + [VMEM] * (count + 2) + [pl.BlockSpec(memory_space=pl.ANY)],
+        (places, *blocks, high, low, growth),
         [pltpu.VMEM((count, 2, height, col_count), jnp.float32)],
     )
     axes = ("row", "col")

time: 64.7 us -> 53.8 us (0.83)
  blocking collectives: 14.2 us -> 30.3 us
  waiting for transfers between devices: 20.6 us -> 7.94 us
  Pallas kernels: 11.2 us -> 3.54 us
  starting transfers between devices: 12 us -> 8.18 us
  local copies, waits for them, and re-layouts: 3.93 us -> 1.87 us
    all_to_all x0 -> x1, blocking collectives: none -> 17.4 us  [on_device(): spectra = (lax.all_to_all(spectra, axes, 0, 0, tiled=True),)]
    all_to_all x1 -> x0, waiting for transfers between devices: 12.4 us -> none  [on_device(): spectra = (lax.all_to_all(spectra, axes, 0, 0, tiled=True),)]
    pallas_call x4, Pallas kernels: 11.2 us -> 3.54 us  [call(): pl.pallas_call(kernel, out_shape=out_shape, in_specs=specs, out_specs=jax...]
    all_to_all x1 -> x0, starting transfers between devices: 3.97 us -> none  [on_device(): spectra = (lax.all_to_all(spectra, axes, 0, 0, tiled=True),)]
    all_to_all x1, blocking collectives: 14.2 us -> 12.9 us  [on_device(): advanced = lax.all_to_all(advanced, axes, 0, 0, tiled=True)]
    squeeze x1, local copies, waits for them, and re-layouts: 0.92 us -> 0.02 us  [on_device(): blocks = swap_blocks([values[step] for step in range(count)])]
    dynamic_update_slice x5, local copies, waits for them, and re-layouts: 0.89 us -> 0.05 us  [on_device(): out = lax.dynamic_update_index_in_dim(out, block, place ^ step, 1)]
    unnamed x8 -> x10, local copies, waits for them, and re-layouts: 1.39 us -> 1.06 us
  transfers between devices with their start and end apart: 7 -> 6, of which waited for: 6 -> 6; matrix products, arithmetic and copies ran while one was open for 1% -> 0% of each run, Pallas kernels for 2% -> 0%
where the time goes in v1:
time: 53.8 us; the launch traced here: 53.5 us
  blocking collectives  30.3 us (56%)
  starting transfers between devices  8.18 us (15%)
  waiting for transfers between devices  7.94 us (15%)
  Pallas kernels  3.54 us (7%)
  local copies, waits for them, and re-layouts  1.87 us (3%)
  other arithmetic  0.95 us (2%)
  between operations  0.76 us (1%)
    all_to_all x1, blocking collectives, on_device(): spectra = (lax.all_to_all(spectra, axes, 0, 0, tiled=True),)  17.4 us
    all_to_all x1, blocking collectives, on_device(): advanced = lax.all_to_all(advanced, axes, 0, 0, tiled=True)  12.9 us
    ppermute x6, starting transfers between devices, swap_blocks(): lax.ppermute(blocks[step], 'col', [(s, s ^ step) for s in range(count)])  8.18 us
    ppermute x6, waiting for transfers between devices, swap_blocks(): lax.ppermute(blocks[step], 'col', [(s, s ^ step) for s in range(count)])  7.94 us
    pallas_call x4, Pallas kernels, call(): pl.pallas_call(kernel, out_shape=out_shape, in_specs=specs, out_specs=jax...  3.54 us
  transfers between devices with their start and end apart: 6, of which 6 were waited for; matrix products, arithmetic and copies ran while one was open for 0% of the time, Pallas kernels for 0%

profile of v1, /device:TPU:0, one launch (start us, length us, event | category | flops | bytes accessed | tf_op | source)
XLA Modules:
  0.0 53.5 jit_solution(7542648350027538070)
XLA Ops:
  0.6 0.0 copy-start
  0.7 1.0 %fusion.1 = (f32[2,32,256]{2,1,0:T(8,128)S(1)}, f32[2,32,256]{2,1,0:T(8,128)S(1)}, f32[2,32,256]{2,1,0:T(8,128)S(1)}, f32[2,32,256]{2,1,0:T(8,128)S(1)}) fusion(s32[]{:T(128)S(6)} %select_n.21, f32[1,4,32,256]{3,2,0,1:T(8,128)} %bitcast.36, f32[1,4,32,256]{3,2,0,1:T(8,128)} %bitcast.37, s32[]{:T(128)S(6)} %select_n.18, s32[]{:T(128)S(6)} %select_n.19, ...), kind=kLoop, calls=%fused_computation.9 | loop fusion | flops 65536 | bytes 524304 | tf_op jit(solution)/shard_map/jit(dynamic_index_in_dim)/squeeze | solution.py:352
  1.6 3.0 %collective-permute-start = (f32[2,32,256]{2,1,0:T(8,128)S(1)}, f32[2,32,256]{2,1,0:T(8,128)S(1)}, u32[]{:S(2)}, u32[]{:S(2)}) collective-permute-start(f32[2,32,256]{2,1,0:T(8,128)S(1)} %get-tuple-element.13), channel_id=1, source_target_pairs={{0,1},{1,0},{2,3},{3,2},{4,5},{5,4},{6,7},{7,6},{8,9},{9,8},{10,11... | collective-permute-start | bytes 196616 | tf_op jit(solution)/shard_map/ppermute | solution.py:330
  4.7 1.5 %collective-permute-start.1 = (f32[2,32,256]{2,1,0:T(8,128)S(1)}, f32[2,32,256]{2,1,0:T(8,128)S(1)}, u32[]{:S(2)}, u32[]{:S(2)}) collective-permute-start(f32[2,32,256]{2,1,0:T(8,128)S(1)} %get-tuple-element.14), channel_id=1, source_target_pairs={{0,2},{1,3},{2,0},{3,1},{4,6},{5,7},{6,4},{7,5},{8,10},{9,11},{10,... | collective-permute-start | bytes 196616 | tf_op jit(solution)/shard_map/ppermute | solution.py:330
  6.2 0.0 collective-permute-start.2
  6.2 0.2 shard_map.77
  6.4 0.6 %collective-permute-done.refs_2_ = f32[2,32,256]{2,1,0:T(8,128)S(1)} collective-permute-done((f32[2,32,256]{2,1,0:T(8,128)S(1)}, f32[2,32,256]{2,1,0:T(8,128)S(1)}, u32[]{:S(2)}, u32[]{:S(2)}) %collective-permute-start) | collective-permute-done | bytes 65568 | tf_op jit(solution)/shard_map/ppermute | solution.py:330
  7.0 1.9 %collective-permute-done.1.refs_3_ = f32[2,32,256]{2,1,0:T(8,128)S(1)} collective-permute-done((f32[2,32,256]{2,1,0:T(8,128)S(1)}, f32[2,32,256]{2,1,0:T(8,128)S(1)}, u32[]{:S(2)}, u32[]{:S(2)}) %collective-permute-start.1) | collective-permute-done | bytes 65568 | tf_op jit(solution)/shard_map/ppermute | solution.py:330
  8.9 2.4 %collective-permute-done.2.refs_4_ = f32[2,32,256]{2,1,0:T(8,128)S(1)} collective-permute-done((f32[2,32,256]{2,1,0:T(8,128)S(1)}, f32[2,32,256]{2,1,0:T(8,128)S(1)}, u32[]{:S(2)}, u32[]{:S(2)}) %collective-permute-start.2) | collective-permute-done | bytes 65568 | tf_op jit(solution)/shard_map/ppermute | solution.py:330
  11.3 0.0 copy-done
  11.3 0.0 copy-start.1
  11.3 1.0 %copy-done.1 = bf16[4,256,256]{2,1,0:T(8,128)(2,1)S(1)} copy-done((bf16[4,256,256]{2,1,0:T(8,128)(2,1)S(1)}, bf16[4,256,256]{2,1,0:T(8,128)(2,1)}, u32[]{:S(2)}) %copy-start.1) | copy-done | bytes 524312
  12.4 0.0 copy-start.3
  12.4 0.0 copy-start.4
  12.4 0.7 %shard_map.78 = f32[32,24,128]{2,1,0:T(8,128)S(1)} custom-call(s32[1]{0:T(128)} %bitcast.refs_0_, f32[2,32,256]{2,1,0:T(8,128)S(1)} %get-tuple-element.12.refs_1_, f32[2,32,256]{2,1,0:T(8,128)S(1)} %collective-permute-done.refs_2_, f32[2,32,256]{2,1,0:T(8,128)S(1)} %collective-permute-done.1.refs_3_, f32[2,32,256]{2,1,0:T(8,128)S(1)} %collective-permute-done.2.refs_4_, ...), custom_call_target="tpu_custom_call" | custom-call | tf_op jit(solution)/shard_map/pallas_call | solution.py:313
  13.1 0.0 copy-start.2
  13.1 17.4 %all_to_all.10.refs_0_ = f32[32,24,128]{2,1,0:T(8,128)S(1)} all-to-all(f32[32,24,128]{2,1,0:T(8,128)S(1)} %shard_map.78), channel_id=1, replica_groups=mesh['row'=8,'col'=4] {'row','col'}, dimensions={0} | all-to-all | bytes 786432 | tf_op jit(solution)/shard_map/all_to_all | solution.py:369
  30.5 0.0 copy-done.3
  30.5 0.0 copy-done.4
  30.5 0.0 copy-done.2
  30.5 2.2 %shard_map.79 = f32[32,16,128]{2,1,0:T(8,128)S(1)} custom-call(f32[32,24,128]{2,1,0:T(8,128)S(1)} %all_to_all.10.refs_0_, f32[4,256,128]{2,1,0:T(8,128)S(1)} %get-tuple-element.4.refs_7_.refs_1_, f32[4,256,128]{2,1,0:T(8,128)S(1)} %get-tuple-element.5.refs_2_, bf16[4,256,256]{2,1,0:T(8,128)(2,1)S(1)} %copy-done, bf16[4,256,256]{2,1,0:T(8,128)(2,1)S(1)} %copy-done.2, ...), custom_call_target="tpu_custom_call" | custom-call | tf_op jit(solution)/shard_map/pallas_call | solution.py:313
  32.6 12.9 %all_to_all.11.refs_1_ = f32[32,16,128]{2,1,0:T(8,128)S(1)} all-to-all(f32[32,16,128]{2,1,0:T(8,128)S(1)} %shard_map.79), channel_id=1, replica_groups=mesh['row'=8,'col'=4] {'row','col'}, dimensions={0} | all-to-all | bytes 524288 | tf_op jit(solution)/shard_map/all_to_all | solution.py:388
  45.6 0.5 shard_map.80
  46.1 0.1 collective-permute-start.3
  46.2 1.4 %collective-permute-start.4 = (f32[2,32,256]{2,1,0:T(8,128)S(1)}, f32[2,32,256]{2,1,0:T(8,128)S(1)}, u32[]{:S(2)}, u32[]{:S(2)}) collective-permute-start(f32[2,32,256]{2,1,0:T(8,128)S(1)} %get-tuple-element.9), channel_id=1, source_target_pairs={{0,2},{1,3},{2,0},{3,1},{4,6},{5,7},{6,4},{7,5},{8,10},{9,11},{10,... | collective-permute-start | bytes 196616 | tf_op jit(solution)/shard_map/ppermute | solution.py:330
  47.6 2.1 %collective-permute-start.5 = (f32[2,32,256]{2,1,0:T(8,128)S(1)}, f32[2,32,256]{2,1,0:T(8,128)S(1)}, u32[]{:S(2)}, u32[]{:S(2)}) collective-permute-start(f32[2,32,256]{2,1,0:T(8,128)S(1)} %get-tuple-element.8), channel_id=1, source_target_pairs={{0,3},{1,2},{2,1},{3,0},{4,7},{5,6},{6,5},{7,4},{8,11},{9,10},{10,... | collective-permute-start | bytes 196616 | tf_op jit(solution)/shard_map/ppermute | solution.py:330
  49.7 1.0 %collective-permute-done.3 = f32[2,32,256]{2,1,0:T(8,128)S(1)} collective-permute-done((f32[2,32,256]{2,1,0:T(8,128)S(1)}, f32[2,32,256]{2,1,0:T(8,128)S(1)}, u32[]{:S(2)}, u32[]{:S(2)}) %collective-permute-start.3) | collective-permute-done | bytes 65568 | tf_op jit(solution)/shard_map/ppermute | solution.py:330
  50.8 0.5 collective-permute-done.4
  51.3 1.5 %collective-permute-done.5 = f32[2,32,256]{2,1,0:T(8,128)S(1)} collective-permute-done((f32[2,32,256]{2,1,0:T(8,128)S(1)}, f32[2,32,256]{2,1,0:T(8,128)S(1)}, u32[]{:S(2)}, u32[]{:S(2)}) %collective-permute-start.5) | collective-permute-done | bytes 65568 | tf_op jit(solution)/shard_map/ppermute | solution.py:330
  52.8 0.7 %fusion.9 = (f32[1,4,32,256]{3,2,1,0:T(8,128)}, f32[1,4,32,256]{3,2,1,0:T(8,128)}) fusion(f32[2,4,32,256]{3,2,1,0:T(8,128)S(1)} %bitcast_dynamic-update-slice_fusion), kind=kLoop, calls=%fused_computation.24 | loop fusion | bytes 524288 | tf_op jit(solution)/shard_map/slice | solution.py:407
  (7 shorter events, 0.1 us)
Async XLA Ops:
  0.6 10.7 %copy-start = (bf16[4,256,256]{2,1,0:T(8,128)(2,1)S(1)}, bf16[4,256,256]{2,1,0:T(8,128)(2,1)}, u32[]{:S(2)}) copy-start(bf16[4,256,256]{2,1,0:T(8,128)(2,1)} %constant.48.clone.refs_5_.refs_3_) | copy-start | bytes 1572868
  1.6 5.4 %collective-permute-start = (f32[2,32,256]{2,1,0:T(8,128)S(1)}, f32[2,32,256]{2,1,0:T(8,128)S(1)}, u32[]{:S(2)}, u32[]{:S(2)}) collective-permute-start(f32[2,32,256]{2,1,0:T(8,128)S(1)} %get-tuple-element.13), channel_id=1, source_target_pairs={{0,1},{1,0},{2,3},{3,2},{4,5},{5,4},{6,7},{7,6},{8,9},{9,8},{10,11... | collective-permute-start | bytes 196616 | tf_op jit(solution)/shard_map/ppermute | solution.py:330
  4.7 4.3 %collective-permute-start.1 = (f32[2,32,256]{2,1,0:T(8,128)S(1)}, f32[2,32,256]{2,1,0:T(8,128)S(1)}, u32[]{:S(2)}, u32[]{:S(2)}) collective-permute-start(f32[2,32,256]{2,1,0:T(8,128)S(1)} %get-tuple-element.14), channel_id=1, source_target_pairs={{0,2},{1,3},{2,0},{3,1},{4,6},{5,7},{6,4},{7,5},{8,10},{9,11},{10,... | collective-permute-start | bytes 196616 | tf_op jit(solution)/shard_map/ppermute | solution.py:330
  6.2 5.2 %collective-permute-start.2 = (f32[2,32,256]{2,1,0:T(8,128)S(1)}, f32[2,32,256]{2,1,0:T(8,128)S(1)}, u32[]{:S(2)}, u32[]{:S(2)}) collective-permute-start(f32[2,32,256]{2,1,0:T(8,128)S(1)} %get-tuple-element.11), channel_id=1, source_target_pairs={{0,3},{1,2},{2,1},{3,0},{4,7},{5,6},{6,5},{7,4},{8,11},{9,10},{10,... | collective-permute-start | bytes 196616 | tf_op jit(solution)/shard_map/ppermute | solution.py:330
  11.3 1.0 %copy-start.1 = (bf16[4,256,256]{2,1,0:T(8,128)(2,1)S(1)}, bf16[4,256,256]{2,1,0:T(8,128)(2,1)}, u32[]{:S(2)}) copy-start(bf16[4,256,256]{2,1,0:T(8,128)(2,1)} %constant.49.clone.refs_6_.refs_4_) | copy-start | bytes 1572868
  12.4 18.1 %copy-start.3 = (bf16[4,256,256]{2,1,0:T(8,128)(2,1)S(1)}, bf16[4,256,256]{2,1,0:T(8,128)(2,1)}, u32[]{:S(2)}) copy-start(bf16[4,256,256]{2,1,0:T(8,128)(2,1)} %constant.50.clone.refs_5_.refs_2_) | copy-start | bytes 1572868
  12.4 18.1 %copy-start.4 = (bf16[4,256,256]{2,1,0:T(8,128)(2,1)S(1)}, bf16[4,256,256]{2,1,0:T(8,128)(2,1)}, u32[]{:S(2)}) copy-start(bf16[4,256,256]{2,1,0:T(8,128)(2,1)} %constant.51.clone.refs_6_.refs_3_) | copy-start | bytes 1572868
  13.1 17.4 %copy-start.2 = (bf16[4,256,256]{2,1,0:T(8,128)(2,1)S(1)}, bf16[4,256,256]{2,1,0:T(8,128)(2,1)}, u32[]{:S(2)}) copy-start(bf16[4,256,256]{2,1,0:T(8,128)(2,1)} %constant.49.clone.refs_6_.refs_4_) | copy-start | bytes 1572868
  46.1 4.7 %collective-permute-start.3 = (f32[2,32,256]{2,1,0:T(8,128)S(1)}, f32[2,32,256]{2,1,0:T(8,128)S(1)}, u32[]{:S(2)}, u32[]{:S(2)}) collective-permute-start(f32[2,32,256]{2,1,0:T(8,128)S(1)} %get-tuple-element.10), channel_id=1, source_target_pairs={{0,1},{1,0},{2,3},{3,2},{4,5},{5,4},{6,7},{7,6},{8,9},{9,8},{10,11... | collective-permute-start | bytes 196616 | tf_op jit(solution)/shard_map/ppermute | solution.py:330
  46.2 5.0 %collective-permute-start.4 = (f32[2,32,256]{2,1,0:T(8,128)S(1)}, f32[2,32,256]{2,1,0:T(8,128)S(1)}, u32[]{:S(2)}, u32[]{:S(2)}) collective-permute-start(f32[2,32,256]{2,1,0:T(8,128)S(1)} %get-tuple-element.9), channel_id=1, source_target_pairs={{0,2},{1,3},{2,0},{3,1},{4,6},{5,7},{6,4},{7,5},{8,10},{9,11},{10,... | collective-permute-start | bytes 196616 | tf_op jit(solution)/shard_map/ppermute | solution.py:330
  47.6 5.2 %collective-permute-start.5 = (f32[2,32,256]{2,1,0:T(8,128)S(1)}, f32[2,32,256]{2,1,0:T(8,128)S(1)}, u32[]{:S(2)}, u32[]{:S(2)}) collective-permute-start(f32[2,32,256]{2,1,0:T(8,128)S(1)} %get-tuple-element.8), channel_id=1, source_target_pairs={{0,3},{1,2},{2,1},{3,0},{4,7},{5,6},{6,5},{7,4},{8,11},{9,10},{10,... | collective-permute-start | bytes 196616 | tf_op jit(solution)/shard_map/ppermute | solution.py:330

commit v2 on v1

--- a/solution.py
+++ b/solution.py
@@ -17,6 +17,7 @@
 SUBLANES = 8
 VMEM_LIMIT = 36 << 20
 VMEM = pl.BlockSpec(memory_space=pltpu.VMEM)
+HBM = pl.BlockSpec(memory_space=pltpu.HBM)
 SMEM = pl.BlockSpec(memory_space=pltpu.SMEM)
 
 
@@ -42,7 +43,7 @@
 def split_constant(matrices):
     high = matrices.astype(jnp.bfloat16)
     low = (matrices - high.astype(np.float64)).astype(jnp.bfloat16)
-    return jnp.asarray(high), jnp.asarray(low)
+    return jnp.asarray(np.stack([high, low]))
 
 
 def split_value(values):
@@ -161,7 +162,14 @@
     return angular * angular
 
 
-def tables_kernel(total_rows, total_cols, width, device_ref, growth_ref, forcing_ref):
+def tables_kernel(total_rows, total_cols, width, device_ref, *refs):
+    *matrix_refs, growth_ref, forcing_ref, loaded_ref, loaded_t_ref, semaphores = refs
+    copies = [
+        pltpu.make_async_copy(source, target, semaphores.at[index])
+        for index, (source, target) in enumerate(zip(matrix_refs, (loaded_ref, loaded_t_ref)))
+    ]
+    for copy in copies:
+        copy.start()
     radix = total_rows // LANES
     chunks = LANES // width
     device = device_ref[0]
@@ -184,10 +192,12 @@
             rows = slice(half * LANES, (half + 1) * LANES)
             growth_ref[index, rows, :] = growth * scale
             forcing_ref[index, rows, :] = (growth - 1.0) / linear * (scale * sign)
+    for copy in copies:
+        copy.wait()
 
 
 def forward_kernel(packed, place_ref, *refs):
-    *block_refs, high_ref, low_ref, _, out_ref, buffer_ref = refs
+    *block_refs, matrix_ref, out_ref, buffer_ref = refs
     count = len(block_refs)
     place = place_ref[0]
     for step, block_ref in enumerate(block_refs):
@@ -203,7 +213,7 @@
             tiles.append(jnp.concatenate([substrate, activator, substrate * activator * activator], axis=0))
     operands = paired(real_dft(tiles), 1)
     for index, operand in enumerate(operands):
-        product = dot_pairs(split_value(operand), (high_ref[index], low_ref[index]))
+        product = dot_pairs(split_value(operand), (matrix_ref[0, index], matrix_ref[1, index]))
         for half in range(2):
             tile = 2 * index + half
             spectrum = product[:, half * LANES : (half + 1) * LANES]
@@ -226,7 +236,7 @@
 
 def advance_kernel(packed, count, *refs):
     if packed:
-        in_ref, growth_ref, forcing_ref, high_ref, low_ref, high_t_ref, low_t_ref, out_ref = refs
+        in_ref, growth_ref, forcing_ref, matrix_ref, matrix_t_ref, out_ref = refs
         width = LANES // count
         radix = in_ref.shape[0] // count
         tiles = []
@@ -246,15 +256,15 @@
             own = jnp.concatenate(own_rows, axis=0)
             tiles.append(jnp.concatenate([own, jnp.concatenate(source_rows, axis=0)], axis=1))
     else:
-        own_ref, source_ref, growth_ref, forcing_ref, high_ref, low_ref, high_t_ref, low_t_ref, out_ref = refs
+        own_ref, source_ref, growth_ref, forcing_ref, matrix_ref, matrix_t_ref, out_ref = refs
         radix = own_ref.shape[0]
         tiles = [jnp.concatenate([own_ref[band], source_ref[band]], axis=1) for band in range(radix)]
     operands = paired(real_dft(tiles), 0)
     products = []
     for index, operand in enumerate(operands):
-        spectrum = dot_pairs((high_t_ref[index], low_t_ref[index]), split_value(operand))
+        spectrum = dot_pairs((matrix_t_ref[0, index], matrix_t_ref[1, index]), split_value(operand))
         advanced = growth_ref[index] * spectrum[:, :LANES] + forcing_ref[index] * spectrum[:, LANES:]
-        products.append(dot_pairs((high_ref[index], low_ref[index]), split_value(advanced)))
+        products.append(dot_pairs((matrix_ref[0, index], matrix_ref[1, index]), split_value(advanced)))
     bands = real_dft_transposed(unpaired(products, 0))
     for band, value in enumerate(bands):
         if not packed:
@@ -276,11 +286,11 @@
                 )
 
 
-def inverse_kernel(packed, count, shift, place_ref, in_ref, high_t_ref, low_t_ref, out_ref):
+def inverse_kernel(packed, count, shift, place_ref, in_ref, matrix_t_ref, *refs):
     place = place_ref[0]
-    radix = 2 * high_t_ref.shape[0]
-    height = out_ref.shape[2]
-    cols = out_ref.shape[3]
+    *out_refs, buffer_ref = refs
+    radix = 2 * matrix_t_ref.shape[1]
+    _, height, cols = out_refs[0].shape
     tiles = []
     for tile in range(radix):
         if not packed:
@@ -299,25 +309,61 @@
     products = []
     for index in range(radix // 2):
         operand = jnp.concatenate([tiles[2 * index], tiles[2 * index + 1]], axis=1)
-        products.append(dot_pairs(split_value(operand), (high_t_ref[index], low_t_ref[index])))
+        products.append(dot_pairs(split_value(operand), (matrix_t_ref[0, index], matrix_t_ref[1, index])))
     values = real_dft_transposed(unpaired(products, 1))
     per_target = cols // LANES
     for index, value in enumerate(values):
         target, tile = index // per_target, index % per_target
         part = slice(tile * LANES, (tile + 1) * LANES)
-        out_ref[place ^ target, 0, :, part] = value[:height] + shift
-        out_ref[place ^ target, 1, :, part] = value[height:]
-
-
-def call(kernel, out_shape, specs, operands, scratch=()):
+        buffer_ref[place ^ target, 0, :, part] = value[:height] + shift
+        buffer_ref[place ^ target, 1, :, part] = value[height:]
+    for step, out_ref in enumerate(out_refs):
+        out_ref[...] = buffer_ref[step]
+
+
+def start_all(copies):
+    for copy in copies:
+        copy.start()
+    for copy in copies:
+        copy.wait()
+
+
+def cut_kernel(place_ref, *refs):
+    *field_refs, semaphores = refs
+    in_refs, out_refs = field_refs[:2], field_refs[2:]
+    height = out_refs[0].shape[1]
+    copies = []
+    for step, out_ref in enumerate(out_refs):
+        rows = pl.ds((place_ref[0] ^ step) * height, height)
+        for field, in_ref in enumerate(in_refs):
+            copies.append(pltpu.make_async_copy(in_ref.at[rows], out_ref.at[field], semaphores.at[step, field]))
+    start_all(copies)
+
+
+def join_kernel(place_ref, *refs):
+    *block_refs, first_ref, second_ref, semaphores = refs
+    height = block_refs[0].shape[1]
+    copies = []
+    for step, block_ref in enumerate(block_refs):
+        rows = pl.ds((place_ref[0] ^ step) * height, height)
+        for field, out_ref in enumerate((first_ref, second_ref)):
+            copies.append(pltpu.make_async_copy(block_ref.at[field], out_ref.at[rows], semaphores.at[step, field]))
+    start_all(copies)
+
+
+def call(kernel, out_shape, specs, operands, scratch=(), out_spec=VMEM):
     return pl.pallas_call(
         kernel,
         out_shape=out_shape,
         in_specs=specs,
-        out_specs=jax.tree.map(lambda _: VMEM, out_shape),
+        out_specs=jax.tree.map(lambda _: out_spec, out_shape),
         scratch_shapes=list(scratch),
         compiler_params=pltpu.CompilerParams(vmem_limit_bytes=VMEM_LIMIT),
     )(*operands)
+
+
+def in_hbm(value):
+    return pltpu.with_memory_space_constraint(value, pltpu.HBM)
 
 
 def float_shape(*shape):
@@ -344,24 +390,32 @@
     places = place[None].astype(jnp.int32)
     devices = (lax.axis_index("row") * count + place)[None].astype(jnp.int32)
     matrices = basis_matrices(total_rows)
-    high, low = split_constant(matrices)
-    high_t, low_t = split_constant(np.swapaxes(matrices, 1, 2))
-
-    fields = jnp.stack([substrate, activator]).reshape(2, count, height, col_count)
+    forward = split_constant(matrices)
+    backward = split_constant(np.swapaxes(matrices, 1, 2))
+
+    block = float_shape(2, height, col_count)
     blocks = swap_blocks(
-        [lax.dynamic_index_in_dim(fields, place ^ step, 1, keepdims=False) for step in range(count)]
-    )
-    growth, forcing = call(
+        call(
+            cut_kernel,
+            [block] * count,
+            [SMEM] + [HBM] * 2,
+            (places, in_hbm(substrate), in_hbm(activator)),
+            [pltpu.SemaphoreType.DMA((count, 2))],
+        )
+    )
+    growth, forcing, forward, backward = call(
         lambda *refs: tables_kernel(total_rows, total_cols, width, *refs),
-        [float_shape(radix // 2, 2 * LANES, LANES)] * 2,
-        [SMEM],
-        (devices,),
+        [float_shape(radix // 2, 2 * LANES, LANES)] * 2
+        + [jax.ShapeDtypeStruct(constant.shape, constant.dtype) for constant in (forward, backward)],
+        [SMEM, HBM, HBM],
+        (devices, in_hbm(forward), in_hbm(backward)),
+        [pltpu.SemaphoreType.DMA((2,))],
     )
     spectra = call(
         lambda *refs: forward_kernel(packed, *refs),
         float_shape(bands * count, 3 * SUBLANES, LANES) if packed else float_shape(radix, 3 * height, LANES),
-        [SMEM] + [VMEM] * (count + 2) + [pl.BlockSpec(memory_space=pl.ANY)],
-        (places, *blocks, high, low, growth),
+        [SMEM] + [VMEM] * (count + 1),
+        (places, *blocks, forward),
         [pltpu.VMEM((count, 2, height, col_count), jnp.float32)],
     )
     axes = ("row", "col")
@@ -381,8 +435,8 @@
     advanced = call(
         lambda *refs: advance_kernel(packed, count, *refs),
         float_shape(bands * count, 2 * SUBLANES, LANES) if packed else float_shape(bands, row_count, LANES),
-        [VMEM] * (len(spectra) + 6),
-        (*spectra, growth, forcing, high, low, high_t, low_t),
+        [VMEM] * (len(spectra) + 4),
+        (*spectra, growth, forcing, forward, backward),
     )
     if packed:
         advanced = lax.all_to_all(advanced, axes, 0, 0, tiled=True)
@@ -393,18 +447,25 @@
         advanced = jnp.transpose(advanced.reshape(radix, LANES // width, 2, height, width), (0, 2, 3, 1, 4))
         advanced = advanced.reshape(radix, 2 * height, LANES)
     shift = FEED_RATE * math.expm1(-FEED_RATE * 0.5 * TIME_STEP) / -FEED_RATE
-    values = call(
-        lambda *refs: inverse_kernel(packed, count, shift, *refs),
-        float_shape(count, 2, height, col_count),
-        [SMEM] + [VMEM] * 3,
-        (places, advanced, high_t, low_t),
-    )
-    blocks = swap_blocks([values[step] for step in range(count)])
-    out = jnp.zeros((2, count, height, col_count), jnp.float32)
-    for step, block in enumerate(blocks):
-        out = lax.dynamic_update_index_in_dim(out, block, place ^ step, 1)
-    out = out.reshape(2, row_count, col_count)
-    return (out[0], out[1])
+    blocks = swap_blocks(
+        call(
+            lambda *refs: inverse_kernel(packed, count, shift, *refs),
+            [block] * count,
+            [SMEM] + [VMEM] * 2,
+            (places, advanced, backward),
+            [pltpu.VMEM((count, 2, height, col_count), jnp.float32)],
+        )
+    )
+    return tuple(
+        call(
+            join_kernel,
+            [float_shape(row_count, col_count)] * 2,
+            [SMEM] + [VMEM] * count,
+            (places, *blocks),
+            [pltpu.SemaphoreType.DMA((count, 2))],
+            HBM,
+        )
+    )
 
 
 def solution(mesh):

time: 53.8 us -> 52.6 us (0.978)
  Pallas kernels: 3.54 us -> 6.61 us
  local copies, waits for them, and re-layouts: 1.87 us -> 0 us
  waiting for transfers between devices: 7.94 us -> 6.64 us
  other arithmetic: 0.95 us -> 0 us
    pallas_call x4 -> x6, Pallas kernels: 3.54 us -> 6.61 us  [call(): pl.pallas_call(kernel, out_shape=out_shape, in_specs=specs, out_specs=jax...]
    ppermute x6, waiting for transfers between devices: 7.94 us -> 6.64 us  [swap_blocks(): lax.ppermute(blocks[step], 'col', [(s, s ^ step) for s in range(count)])]
    unnamed x10 -> x0, local copies, waits for them, and re-layouts: 1.06 us -> none
    squeeze x1 -> x0, other arithmetic: 0.95 us -> none  [on_device(): lax.dynamic_index_in_dim(fields, place ^ step, 1, keepdims=False)]
    slice x1 -> x0, local copies, waits for them, and re-layouts: 0.72 us -> none  [on_device(): return (out[0], out[1])]
  transfers between devices with their start and end apart: 6 -> 6, of which waited for: 6 -> 5; matrix products, arithmetic and copies ran while one was open for 0% -> 0% of each run, Pallas kernels for 0% -> 3%
where the time goes in v2:
time: 52.6 us; the launch traced here: 52.3 us
  blocking collectives  30.3 us (58%)
  starting transfers between devices  8.12 us (15%)
  waiting for transfers between devices  6.64 us (13%)
  Pallas kernels  6.61 us (13%)
  between operations  0.7 us (1%)
    all_to_all x1, blocking collectives, on_device(): spectra = (lax.all_to_all(spectra, axes, 0, 0, tiled=True),)  17.4 us
    all_to_all x1, blocking collectives, on_device(): advanced = lax.all_to_all(advanced, axes, 0, 0, tiled=True)  12.9 us
    ppermute x6, starting transfers between devices, swap_blocks(): lax.ppermute(blocks[step], 'col', [(s, s ^ step) for s in range(count)])  8.12 us
    ppermute x6, waiting for transfers between devices, swap_blocks(): lax.ppermute(blocks[step], 'col', [(s, s ^ step) for s in range(count)])  6.64 us
    pallas_call x6, Pallas kernels, call(): pl.pallas_call(kernel, out_shape=out_shape, in_specs=specs, out_specs=jax...  6.61 us
  transfers between devices with their start and end apart: 6, of which 5 were waited for; matrix products, arithmetic and copies ran while one was open for 0% of the time, Pallas kernels for 3%

profile of v2, /device:TPU:0, one launch (start us, length us, event | category | flops | bytes accessed | tf_op | source)
XLA Modules:
  0.0 52.3 jit_solution(15935098416246744636)
XLA Ops:
  0.6 0.9 %shard_map.59 = (f32[2,32,256]{2,1,0:T(8,128)S(1)}, f32[2,32,256]{2,1,0:T(8,128)S(1)}, f32[2,32,256]{2,1,0:T(8,128)S(1)}, f32[2,32,256]{2,1,0:T(8,128)S(1)}) custom-call(s32[1]{0:T(128)} %bitcast.place_ref.refs_0_, f32[128,256]{1,0:T(8,128)} %refs_0_.1, f32[128,256]{1,0:T(8,128)} %refs_1_.2), custom_call_target="tpu_custom_call" | custom-call | tf_op jit(solution)/shard_map/pallas_call | solution.py:355
  1.6 3.0 %collective-permute-start = (f32[2,32,256]{2,1,0:T(8,128)S(1)}, f32[2,32,256]{2,1,0:T(8,128)S(1)}, u32[]{:S(2)}, u32[]{:S(2)}) collective-permute-start(f32[2,32,256]{2,1,0:T(8,128)S(1)} %get-tuple-element.15), channel_id=1, source_target_pairs={{0,1},{1,0},{2,3},{3,2},{4,5},{5,4},{6,7},{7,6},{8,9},{9,8},{10,11... | collective-permute-start | bytes 196616 | tf_op jit(solution)/shard_map/ppermute | solution.py:376
  4.6 1.5 %collective-permute-start.1 = (f32[2,32,256]{2,1,0:T(8,128)S(1)}, f32[2,32,256]{2,1,0:T(8,128)S(1)}, u32[]{:S(2)}, u32[]{:S(2)}) collective-permute-start(f32[2,32,256]{2,1,0:T(8,128)S(1)} %get-tuple-element.16), channel_id=1, source_target_pairs={{0,2},{1,3},{2,0},{3,1},{4,6},{5,7},{6,4},{7,5},{8,10},{9,11},{10,... | collective-permute-start | bytes 196616 | tf_op jit(solution)/shard_map/ppermute | solution.py:376
  6.1 0.0 collective-permute-start.2
  6.2 1.6 %shard_map.60 = (f32[4,256,128]{2,1,0:T(8,128)S(1)}, f32[4,256,128]{2,1,0:T(8,128)S(1)}, bf16[2,4,256,256]{3,2,1,0:T(8,128)(2,1)S(1)}, bf16[2,4,256,256]{3,2,1,0:T(8,128)(2,1)S(1)}) custom-call(s32[1]{0:T(128)} %bitcast.1.refs_0_, bf16[2,4,256,256]{3,2,1,0:T(8,128)(2,1)} %constant.15.clone.refs_1_, bf16[2,4,256,256]{3,2,1,0:T(8,128)(2,1)} %constant.16.clone.refs_2_), custom_call_target="tpu_custom_call" | custom-call | tf_op jit(solution)/shard_map/pallas_call | solution.py:355
  7.7 0.0 collective-permute-done.refs_2_
  7.7 1.1 %collective-permute-done.1.refs_3_ = f32[2,32,256]{2,1,0:T(8,128)S(1)} collective-permute-done((f32[2,32,256]{2,1,0:T(8,128)S(1)}, f32[2,32,256]{2,1,0:T(8,128)S(1)}, u32[]{:S(2)}, u32[]{:S(2)}) %collective-permute-start.1) | collective-permute-done | bytes 65568 | tf_op jit(solution)/shard_map/ppermute | solution.py:376
  8.9 2.4 %collective-permute-done.2.refs_4_ = f32[2,32,256]{2,1,0:T(8,128)S(1)} collective-permute-done((f32[2,32,256]{2,1,0:T(8,128)S(1)}, f32[2,32,256]{2,1,0:T(8,128)S(1)}, u32[]{:S(2)}, u32[]{:S(2)}) %collective-permute-start.2) | collective-permute-done | bytes 65568 | tf_op jit(solution)/shard_map/ppermute | solution.py:376
  11.3 0.7 %shard_map.61 = f32[32,24,128]{2,1,0:T(8,128)S(1)} custom-call(s32[1]{0:T(128)} %bitcast.place_ref.refs_0_, f32[2,32,256]{2,1,0:T(8,128)S(1)} %get-tuple-element.14.refs_1_, f32[2,32,256]{2,1,0:T(8,128)S(1)} %collective-permute-done.refs_2_, f32[2,32,256]{2,1,0:T(8,128)S(1)} %collective-permute-done.1.refs_3_, ...), custom_call_target="tpu_custom_call" | custom-call | tf_op jit(solution)/shard_map/pallas_call | solution.py:355
  12.0 17.4 %all_to_all.10.refs_0_ = f32[32,24,128]{2,1,0:T(8,128)S(1)} all-to-all(f32[32,24,128]{2,1,0:T(8,128)S(1)} %shard_map.61), channel_id=1, replica_groups=mesh['row'=8,'col'=4] {'row','col'}, dimensions={0} | all-to-all | bytes 786432 | tf_op jit(solution)/shard_map/all_to_all | solution.py:423
  29.4 2.2 %shard_map.62 = f32[32,16,128]{2,1,0:T(8,128)S(1)} custom-call(f32[32,24,128]{2,1,0:T(8,128)S(1)} %all_to_all.10.refs_0_, f32[4,256,128]{2,1,0:T(8,128)S(1)} %get-tuple-element.19.refs_1_, f32[4,256,128]{2,1,0:T(8,128)S(1)} %get-tuple-element.20.refs_2_, bf16[2,4,256,256]{3,2,1,0:T(8,128)(2,1)S(1)} %get-tuple-element.18.refs_5_.refs_3_, ...), custom_call_target="tpu_custom_call" | custom-call | tf_op jit(solution)/shard_map/pallas_call | solution.py:355
  31.5 12.9 %all_to_all.11.refs_1_ = f32[32,16,128]{2,1,0:T(8,128)S(1)} all-to-all(f32[32,16,128]{2,1,0:T(8,128)S(1)} %shard_map.62), channel_id=1, replica_groups=mesh['row'=8,'col'=4] {'row','col'}, dimensions={0} | all-to-all | bytes 524288 | tf_op jit(solution)/shard_map/all_to_all | solution.py:442
  44.4 0.5 shard_map.63
  45.0 0.1 collective-permute-start.3
  45.0 1.4 %collective-permute-start.4 = (f32[2,32,256]{2,1,0:T(8,128)S(1)}, f32[2,32,256]{2,1,0:T(8,128)S(1)}, u32[]{:S(2)}, u32[]{:S(2)}) collective-permute-start(f32[2,32,256]{2,1,0:T(8,128)S(1)} %get-tuple-element.24), channel_id=1, source_target_pairs={{0,2},{1,3},{2,0},{3,1},{4,6},{5,7},{6,4},{7,5},{8,10},{9,11},{10,... | collective-permute-start | bytes 196616 | tf_op jit(solution)/shard_map/ppermute | solution.py:376
  46.4 2.1 %collective-permute-start.5 = (f32[2,32,256]{2,1,0:T(8,128)S(1)}, f32[2,32,256]{2,1,0:T(8,128)S(1)}, u32[]{:S(2)}, u32[]{:S(2)}) collective-permute-start(f32[2,32,256]{2,1,0:T(8,128)S(1)} %get-tuple-element.25), channel_id=1, source_target_pairs={{0,3},{1,2},{2,1},{3,0},{4,7},{5,6},{6,5},{7,4},{8,11},{9,10},{10,... | collective-permute-start | bytes 196616 | tf_op jit(solution)/shard_map/ppermute | solution.py:376
  48.5 1.2 %collective-permute-done.3.refs_1_ = f32[2,32,256]{2,1,0:T(8,128)S(1)} collective-permute-done((f32[2,32,256]{2,1,0:T(8,128)S(1)}, f32[2,32,256]{2,1,0:T(8,128)S(1)}, u32[]{:S(2)}, u32[]{:S(2)}) %collective-permute-start.3) | collective-permute-done | bytes 65568 | tf_op jit(solution)/shard_map/ppermute | solution.py:376
  49.8 0.3 collective-permute-done.4.refs_2_
  50.1 1.5 %collective-permute-done.5.refs_3_ = f32[2,32,256]{2,1,0:T(8,128)S(1)} collective-permute-done((f32[2,32,256]{2,1,0:T(8,128)S(1)}, f32[2,32,256]{2,1,0:T(8,128)S(1)}, u32[]{:S(2)}, u32[]{:S(2)}) %collective-permute-start.5) | collective-permute-done | bytes 65568 | tf_op jit(solution)/shard_map/ppermute | solution.py:376
  51.6 0.8 %shard_map.64 = (f32[128,256]{1,0:T(8,128)}, f32[128,256]{1,0:T(8,128)}) custom-call(s32[1]{0:T(128)} %bitcast.place_ref.refs_0_, f32[2,32,256]{2,1,0:T(8,128)S(1)} %get-tuple-element.22.refs_0_, f32[2,32,256]{2,1,0:T(8,128)S(1)} %collective-permute-done.3.refs_1_, f32[2,32,256]{2,1,0:T(8,128)S(1)} %collective-permute-done.4.refs_2_, ...), custom_call_target="tpu_custom_call" | custom-call | tf_op jit(solution)/shard_map/pallas_call | solution.py:355
Async XLA Ops:
  1.6 6.1 %collective-permute-start = (f32[2,32,256]{2,1,0:T(8,128)S(1)}, f32[2,32,256]{2,1,0:T(8,128)S(1)}, u32[]{:S(2)}, u32[]{:S(2)}) collective-permute-start(f32[2,32,256]{2,1,0:T(8,128)S(1)} %get-tuple-element.15), channel_id=1, source_target_pairs={{0,1},{1,0},{2,3},{3,2},{4,5},{5,4},{6,7},{7,6},{8,9},{9,8},{10,11... | collective-permute-start | bytes 196616 | tf_op jit(solution)/shard_map/ppermute | solution.py:376
  4.6 4.3 %collective-permute-start.1 = (f32[2,32,256]{2,1,0:T(8,128)S(1)}, f32[2,32,256]{2,1,0:T(8,128)S(1)}, u32[]{:S(2)}, u32[]{:S(2)}) collective-permute-start(f32[2,32,256]{2,1,0:T(8,128)S(1)} %get-tuple-element.16), channel_id=1, source_target_pairs={{0,2},{1,3},{2,0},{3,1},{4,6},{5,7},{6,4},{7,5},{8,10},{9,11},{10,... | collective-permute-start | bytes 196616 | tf_op jit(solution)/shard_map/ppermute | solution.py:376
  6.1 5.2 %collective-permute-start.2 = (f32[2,32,256]{2,1,0:T(8,128)S(1)}, f32[2,32,256]{2,1,0:T(8,128)S(1)}, u32[]{:S(2)}, u32[]{:S(2)}) collective-permute-start(f32[2,32,256]{2,1,0:T(8,128)S(1)} %get-tuple-element.17), channel_id=1, source_target_pairs={{0,3},{1,2},{2,1},{3,0},{4,7},{5,6},{6,5},{7,4},{8,11},{9,10},{10,... | collective-permute-start | bytes 196616 | tf_op jit(solution)/shard_map/ppermute | solution.py:376
  45.0 4.8 %collective-permute-start.3 = (f32[2,32,256]{2,1,0:T(8,128)S(1)}, f32[2,32,256]{2,1,0:T(8,128)S(1)}, u32[]{:S(2)}, u32[]{:S(2)}) collective-permute-start(f32[2,32,256]{2,1,0:T(8,128)S(1)} %get-tuple-element.23), channel_id=1, source_target_pairs={{0,1},{1,0},{2,3},{3,2},{4,5},{5,4},{6,7},{7,6},{8,9},{9,8},{10,11... | collective-permute-start | bytes 196616 | tf_op jit(solution)/shard_map/ppermute | solution.py:376
  45.0 5.0 %collective-permute-start.4 = (f32[2,32,256]{2,1,0:T(8,128)S(1)}, f32[2,32,256]{2,1,0:T(8,128)S(1)}, u32[]{:S(2)}, u32[]{:S(2)}) collective-permute-start(f32[2,32,256]{2,1,0:T(8,128)S(1)} %get-tuple-element.24), channel_id=1, source_target_pairs={{0,2},{1,3},{2,0},{3,1},{4,6},{5,7},{6,4},{7,5},{8,10},{9,11},{10,... | collective-permute-start | bytes 196616 | tf_op jit(solution)/shard_map/ppermute | solution.py:376
  46.4 5.2 %collective-permute-start.5 = (f32[2,32,256]{2,1,0:T(8,128)S(1)}, f32[2,32,256]{2,1,0:T(8,128)S(1)}, u32[]{:S(2)}, u32[]{:S(2)}) collective-permute-start(f32[2,32,256]{2,1,0:T(8,128)S(1)} %get-tuple-element.25), channel_id=1, source_target_pairs={{0,3},{1,2},{2,1},{3,0},{4,7},{5,6},{6,5},{7,4},{8,11},{9,10},{10,... | collective-permute-start | bytes 196616 | tf_op jit(solution)/shard_map/ppermute | solution.py:376

commit v3 on v2

--- a/solution.py
+++ b/solution.py
@@ -6,6 +6,7 @@
 from jax import lax
 from jax.experimental import pallas as pl
 from jax.experimental.pallas import tpu as pltpu
+from jax.sharding import Mesh
 from jax.sharding import PartitionSpec as P
 
 FEED_RATE = 0.037
@@ -14,6 +15,8 @@
 SUBSTRATE_DIFFUSION = 4e-07
 ACTIVATOR_DIFFUSION = 2e-07
 LANES = 128
+HALF = LANES // 2
+CORES = 2
 SUBLANES = 8
 VMEM_LIMIT = 36 << 20
 VMEM = pl.BlockSpec(memory_space=pltpu.VMEM)
@@ -163,7 +166,7 @@
 
 
 def tables_kernel(total_rows, total_cols, width, device_ref, *refs):
-    *matrix_refs, growth_ref, forcing_ref, loaded_ref, loaded_t_ref, semaphores = refs
+    *matrix_refs, table_ref, loaded_ref, loaded_t_ref, semaphores = refs
     copies = [
         pltpu.make_async_copy(source, target, semaphores.at[index])
         for index, (source, target) in enumerate(zip(matrix_refs, (loaded_ref, loaded_t_ref)))
@@ -178,7 +181,7 @@
     col_class = jnp.where(tile == 0, 0, jnp.where(tile == 1, total_cols // LANES // 2, tile // 2))
     col_squares = wave_squares(col_class, place * width + lane % width, total_cols)
     col_scale = jnp.where(tile < 2, 1.0 / total_cols, 2.0 / total_cols).astype(jnp.float32)
-    first = lane < width
+    first = lane % HALF < width
     diffusion = jnp.where(first, SUBSTRATE_DIFFUSION, ACTIVATOR_DIFFUSION).astype(jnp.float32)
     decay = jnp.where(first, FEED_RATE, FEED_RATE + KILL_RATE).astype(jnp.float32)
     sign = jnp.where(first, -1.0, 1.0).astype(jnp.float32)
@@ -190,8 +193,8 @@
             linear = -diffusion * (wave_squares(k1, k2, total_rows) + col_squares) - decay
             growth = jnp.exp(linear * (0.5 * TIME_STEP))
             rows = slice(half * LANES, (half + 1) * LANES)
-            growth_ref[index, rows, :] = growth * scale
-            forcing_ref[index, rows, :] = (growth - 1.0) / linear * (scale * sign)
+            forcing = (growth - 1.0) / linear * sign
+            table_ref[index, rows, :] = jnp.where(lane < HALF, growth, forcing) * scale
     for copy in copies:
         copy.wait()
 
@@ -234,37 +237,46 @@
                     )
 
 
-def advance_kernel(packed, count, *refs):
+def place_of(band, source, bands):
+    return (source * CORES + band % CORES) * (bands // CORES) + band // CORES
+
+
+def advance_kernel(packed, count, in_ref, table_ref, matrix_ref, matrix_t_ref, out_ref):
     if packed:
-        in_ref, growth_ref, forcing_ref, matrix_ref, matrix_t_ref, out_ref = refs
         width = LANES // count
         radix = in_ref.shape[0] // count
         tiles = []
         for band in range(radix):
-            own_rows, source_rows = [], []
+            rows = []
             for source in range(count):
-                block = in_ref[band * count + source]
+                block = in_ref[place_of(band, source, radix)]
                 turns = [
-                    [rolled(block[field * SUBLANES : (field + 1) * SUBLANES], -shift, width) for shift in range(count)]
+                    [rolled(block[field * SUBLANES : (field + 1) * SUBLANES], shift, width) for shift in range(count)]
                     for field in range(3)
                 ]
-                low_half = lane_chunk((SUBLANES, LANES), width) == 0
                 for group in range(count):
-                    near, next_near = group, (group - 1) % count
-                    own_rows.append(jnp.where(low_half, turns[0][near], turns[1][next_near]))
-                    source_rows.append(jnp.where(low_half, turns[2][near], turns[2][next_near]))
-            own = jnp.concatenate(own_rows, axis=0)
-            tiles.append(jnp.concatenate([own, jnp.concatenate(source_rows, axis=0)], axis=1))
+                    rows.append(
+                        pick_chunks(
+                            [turns[min(place, 2)][(place - group) % count] for place in range(count)], width
+                        )
+                    )
+            tiles.append(jnp.concatenate(rows, axis=0))
     else:
-        own_ref, source_ref, growth_ref, forcing_ref, matrix_ref, matrix_t_ref, out_ref = refs
-        radix = own_ref.shape[0]
-        tiles = [jnp.concatenate([own_ref[band], source_ref[band]], axis=1) for band in range(radix)]
+        radix = in_ref.shape[0]
+        tiles = [in_ref[band] for band in range(radix)]
     operands = paired(real_dft(tiles), 0)
+    low_half = lax.broadcasted_iota(jnp.int32, (2 * LANES, LANES), 1) < HALF
     products = []
     for index, operand in enumerate(operands):
-        spectrum = dot_pairs((matrix_t_ref[0, index], matrix_t_ref[1, index]), split_value(operand))
-        advanced = growth_ref[index] * spectrum[:, :LANES] + forcing_ref[index] * spectrum[:, LANES:]
-        products.append(dot_pairs((matrix_ref[0, index], matrix_ref[1, index]), split_value(advanced)))
+        high, low = split_value(operand)
+        both = dot(matrix_t_ref[0, index], jnp.concatenate([high, low], axis=1))
+        spectrum = both[:, :LANES] + (both[:, LANES:] + dot(matrix_t_ref[1, index], high))
+        scaled = table_ref[index] * spectrum
+        advanced = scaled + pltpu.roll(scaled, HALF, 1)
+        high = advanced.astype(jnp.bfloat16).astype(jnp.float32)
+        both = dot(matrix_ref[0, index], jnp.where(low_half, high, advanced - high).astype(jnp.bfloat16))
+        rest = dot(matrix_ref[1, index], high.astype(jnp.bfloat16))
+        products.append(both + (pltpu.roll(both, HALF, 1) + rest))
     bands = real_dft_transposed(unpaired(products, 0))
     for band, value in enumerate(bands):
         if not packed:
@@ -281,7 +293,7 @@
                     )
                     for group in range(count)
                 ]
-                out_ref[band * count + target, field * SUBLANES : (field + 1) * SUBLANES, :] = pick_chunks(
+                out_ref[place_of(band, target, radix), field * SUBLANES : (field + 1) * SUBLANES, :] = pick_chunks(
                     pieces, width
                 )
 
@@ -379,7 +391,7 @@
 
 def on_device(substrate, activator):
     row_count, col_count = substrate.shape
-    bands, count = lax.axis_size("row"), lax.axis_size("col")
+    bands, count = lax.axis_size("outer") * lax.axis_size("core"), lax.axis_size("col")
     total_rows, total_cols = row_count * bands, col_count * count
     height = row_count // count
     radix = total_cols // LANES
@@ -388,7 +400,8 @@
     packed = height == SUBLANES * count and width * count == LANES
     place = lax.axis_index("col")
     places = place[None].astype(jnp.int32)
-    devices = (lax.axis_index("row") * count + place)[None].astype(jnp.int32)
+    axes = ("col", "core", "outer")
+    devices = lax.axis_index(axes)[None].astype(jnp.int32)
     matrices = basis_matrices(total_rows)
     forward = split_constant(matrices)
     backward = split_constant(np.swapaxes(matrices, 1, 2))
@@ -403,9 +416,9 @@
             [pltpu.SemaphoreType.DMA((count, 2))],
         )
     )
-    growth, forcing, forward, backward = call(
+    table, forward, backward = call(
         lambda *refs: tables_kernel(total_rows, total_cols, width, *refs),
-        [float_shape(radix // 2, 2 * LANES, LANES)] * 2
+        [float_shape(radix // 2, 2 * LANES, LANES)]
         + [jax.ShapeDtypeStruct(constant.shape, constant.dtype) for constant in (forward, backward)],
         [SMEM, HBM, HBM],
         (devices, in_hbm(forward), in_hbm(backward)),
@@ -418,31 +431,28 @@
         (places, *blocks, forward),
         [pltpu.VMEM((count, 2, height, col_count), jnp.float32)],
     )
-    axes = ("row", "col")
     if packed:
-        spectra = (lax.all_to_all(spectra, axes, 0, 0, tiled=True),)
+        spectra = lax.all_to_all(spectra, axes, 0, 0, tiled=True)
     else:
         spectra = spectra.reshape(radix, 3, height, LANES // width, width)
         spectra = jnp.transpose(spectra, (0, 3, 1, 2, 4)).reshape(bands * count, -1)
         spectra = lax.all_to_all(spectra, axes, 0, 0, tiled=True)
-        spectra = jnp.transpose(spectra.reshape(bands, count, 3, height, width), (2, 0, 1, 3, 4))
+        spectra = spectra.reshape(count, CORES, bands // CORES, 3, height, width)
+        spectra = jnp.transpose(spectra, (3, 2, 1, 0, 4, 5))
         spectra = spectra.reshape(3, bands, row_count, width)
-        rest = jnp.zeros((bands, row_count, LANES - 2 * width), jnp.float32)
-        spectra = (
-            jnp.concatenate([spectra[0], spectra[1], rest], axis=2),
-            jnp.concatenate([spectra[2], spectra[2], rest], axis=2),
-        )
+        rest = jnp.zeros((bands, row_count, HALF - 2 * width), jnp.float32)
+        spectra = jnp.concatenate([spectra[0], spectra[1], rest, spectra[2], spectra[2], rest], axis=2)
     advanced = call(
         lambda *refs: advance_kernel(packed, count, *refs),
         float_shape(bands * count, 2 * SUBLANES, LANES) if packed else float_shape(bands, row_count, LANES),
-        [VMEM] * (len(spectra) + 4),
-        (*spectra, growth, forcing, forward, backward),
+        [VMEM] * 4,
+        (spectra, table, forward, backward),
     )
     if packed:
         advanced = lax.all_to_all(advanced, axes, 0, 0, tiled=True)
     else:
-        advanced = advanced[:, :, : 2 * width].reshape(bands, count, height, 2, width)
-        advanced = jnp.transpose(advanced, (0, 1, 3, 2, 4)).reshape(bands * count, -1)
+        advanced = advanced[:, :, : 2 * width].reshape(bands // CORES, CORES, count, height, 2, width)
+        advanced = jnp.transpose(advanced, (2, 1, 0, 4, 3, 5)).reshape(bands * count, -1)
         advanced = lax.all_to_all(advanced, axes, 0, 0, tiled=True)
         advanced = jnp.transpose(advanced.reshape(radix, LANES // width, 2, height, width), (0, 2, 3, 1, 4))
         advanced = advanced.reshape(radix, 2 * height, LANES)
@@ -469,8 +479,7 @@
 
 
 def solution(mesh):
-    in_specs = (P("row", "col"), P("row", "col"))
-    out_specs = (P("row", "col"), P("row", "col"))
-    return jax.shard_map(
-        on_device, mesh=mesh, in_specs=in_specs, out_specs=out_specs, check_vma=False
-    )
+    bands, count = mesh.shape["row"], mesh.shape["col"]
+    split = Mesh(mesh.devices.reshape(bands // CORES, CORES, count), ("outer", "core", "col"))
+    spec = P(("outer", "core"), "col")
+    return jax.shard_map(on_device, mesh=split, in_specs=(spec, spec), out_specs=(spec, spec), check_vma=False)

time: 52.6 us -> 51.9 us (0.987)
  blocking collectives: 30.3 us -> 29.5 us
    all_to_all x1, blocking collectives: 17.4 us -> 15.6 us  [on_device(): spectra = lax.all_to_all(spectra, axes, 0, 0, tiled=True)]
    all_to_all x1, blocking collectives: 12.9 us -> 13.8 us  [on_device(): advanced = lax.all_to_all(advanced, axes, 0, 0, tiled=True)]
where the time goes in v3:
time: 51.9 us; the launch traced here: 51.6 us
  blocking collectives  29.5 us (57%)
  starting transfers between devices  8.13 us (16%)
  waiting for transfers between devices  6.76 us (13%)
  Pallas kernels  6.6 us (13%)
  between operations  0.69 us (1%)
    all_to_all x1, blocking collectives, on_device(): spectra = lax.all_to_all(spectra, axes, 0, 0, tiled=True)  15.6 us
    all_to_all x1, blocking collectives, on_device(): advanced = lax.all_to_all(advanced, axes, 0, 0, tiled=True)  13.8 us
    ppermute x6, starting transfers between devices, swap_blocks(): lax.ppermute(blocks[step], 'col', [(s, s ^ step) for s in range(count)])  8.13 us
    ppermute x6, waiting for transfers between devices, swap_blocks(): lax.ppermute(blocks[step], 'col', [(s, s ^ step) for s in range(count)])  6.76 us
    pallas_call x6, Pallas kernels, call(): pl.pallas_call(kernel, out_shape=out_shape, in_specs=specs, out_specs=jax...  6.6 us
  transfers between devices with their start and end apart: 6, of which 5 were waited for; matrix products, arithmetic and copies ran while one was open for 0% of the time, Pallas kernels for 3%

profile of v3, /device:TPU:0, one launch (start us, length us, event | category | flops | bytes accessed | tf_op | source)
XLA Modules:
  0.0 51.6 jit_solution(15110072696317562950)
XLA Ops:
  0.6 0.9 %shard_map.59 = (f32[2,32,256]{2,1,0:T(8,128)S(1)}, f32[2,32,256]{2,1,0:T(8,128)S(1)}, f32[2,32,256]{2,1,0:T(8,128)S(1)}, f32[2,32,256]{2,1,0:T(8,128)S(1)}) custom-call(s32[1]{0:T(128)} %bitcast.place_ref.refs_0_, f32[128,256]{1,0:T(8,128)} %refs_0_.1, f32[128,256]{1,0:T(8,128)} %refs_1_.2), custom_call_target="tpu_custom_call" | custom-call | tf_op jit(solution)/shard_map/pallas_call | solution.py:367
  1.6 3.0 %collective-permute-start = (f32[2,32,256]{2,1,0:T(8,128)S(1)}, f32[2,32,256]{2,1,0:T(8,128)S(1)}, u32[]{:S(2)}, u32[]{:S(2)}) collective-permute-start(f32[2,32,256]{2,1,0:T(8,128)S(1)} %get-tuple-element.14), channel_id=1, source_target_pairs={{0,1},{1,0},{2,3},{3,2},{4,5},{5,4},{6,7},{7,6},{8,9},{9,8},{10,11... | collective-permute-start | bytes 196616 | tf_op jit(solution)/shard_map/ppermute | solution.py:388
  4.6 1.5 %collective-permute-start.1 = (f32[2,32,256]{2,1,0:T(8,128)S(1)}, f32[2,32,256]{2,1,0:T(8,128)S(1)}, u32[]{:S(2)}, u32[]{:S(2)}) collective-permute-start(f32[2,32,256]{2,1,0:T(8,128)S(1)} %get-tuple-element.15), channel_id=1, source_target_pairs={{0,2},{1,3},{2,0},{3,1},{4,6},{5,7},{6,4},{7,5},{8,10},{9,11},{10,... | collective-permute-start | bytes 196616 | tf_op jit(solution)/shard_map/ppermute | solution.py:388
  6.1 0.0 collective-permute-start.2
  6.2 1.6 %shard_map.60 = (f32[4,256,128]{2,1,0:T(8,128)S(1)}, bf16[2,4,256,256]{3,2,1,0:T(8,128)(2,1)S(1)}, bf16[2,4,256,256]{3,2,1,0:T(8,128)(2,1)S(1)}) custom-call(s32[1]{0:T(128)} %bitcast.1.refs_0_, bf16[2,4,256,256]{3,2,1,0:T(8,128)(2,1)} %constant.20.clone.refs_1_, bf16[2,4,256,256]{3,2,1,0:T(8,128)(2,1)} %constant.21.clone.refs_2_), custom_call_target="tpu_custom_call" | custom-call | tf_op jit(solution)/shard_map/pallas_call | solution.py:367
  7.7 0.0 collective-permute-done.refs_2_
  7.7 1.1 %collective-permute-done.1.refs_3_ = f32[2,32,256]{2,1,0:T(8,128)S(1)} collective-permute-done((f32[2,32,256]{2,1,0:T(8,128)S(1)}, f32[2,32,256]{2,1,0:T(8,128)S(1)}, u32[]{:S(2)}, u32[]{:S(2)}) %collective-permute-start.1) | collective-permute-done | bytes 65568 | tf_op jit(solution)/shard_map/ppermute | solution.py:388
  8.9 2.4 %collective-permute-done.2.refs_4_ = f32[2,32,256]{2,1,0:T(8,128)S(1)} collective-permute-done((f32[2,32,256]{2,1,0:T(8,128)S(1)}, f32[2,32,256]{2,1,0:T(8,128)S(1)}, u32[]{:S(2)}, u32[]{:S(2)}) %collective-permute-start.2) | collective-permute-done | bytes 65568 | tf_op jit(solution)/shard_map/ppermute | solution.py:388
  11.3 0.7 %shard_map.61 = f32[32,24,128]{2,1,0:T(8,128)S(1)} custom-call(s32[1]{0:T(128)} %bitcast.place_ref.refs_0_, f32[2,32,256]{2,1,0:T(8,128)S(1)} %get-tuple-element.13.refs_1_, f32[2,32,256]{2,1,0:T(8,128)S(1)} %collective-permute-done.refs_2_, f32[2,32,256]{2,1,0:T(8,128)S(1)} %collective-permute-done.1.refs_3_, ...), custom_call_target="tpu_custom_call" | custom-call | tf_op jit(solution)/shard_map/pallas_call | solution.py:367
  12.0 15.6 %all_to_all.10.refs_0_ = f32[32,24,128]{2,1,0:T(8,128)S(1)} all-to-all(f32[32,24,128]{2,1,0:T(8,128)S(1)} %shard_map.61), channel_id=1, replica_groups=mesh['outer'=4,'core'=2,'col'=4] {'col','core','outer'}, dimensions={0} | all-to-all | bytes 786432 | tf_op jit(solution)/shard_map/all_to_all | solution.py:435
  27.6 2.2 %shard_map.62 = f32[32,16,128]{2,1,0:T(8,128)S(1)} custom-call(f32[32,24,128]{2,1,0:T(8,128)S(1)} %all_to_all.10.refs_0_, f32[4,256,128]{2,1,0:T(8,128)S(1)} %get-tuple-element.18.refs_1_, bf16[2,4,256,256]{3,2,1,0:T(8,128)(2,1)S(1)} %get-tuple-element.17.refs_5_.refs_2_, bf16[2,4,256,256]{3,2,1,0:T(8,128)(2,1)S(1)} %get-tuple-element.19.refs_3_.refs_2_), custom_call_target="tpu_custom_call" | custom-call | tf_op jit(solution)/shard_map/pallas_call | solution.py:367
  29.8 13.8 %all_to_all.11.refs_1_ = f32[32,16,128]{2,1,0:T(8,128)S(1)} all-to-all(f32[32,16,128]{2,1,0:T(8,128)S(1)} %shard_map.62), channel_id=1, replica_groups=mesh['outer'=4,'core'=2,'col'=4] {'col','core','outer'}, dimensions={0} | all-to-all | bytes 524288 | tf_op jit(solution)/shard_map/all_to_all | solution.py:452
  43.6 0.5 shard_map.63
  44.1 1.0 %collective-permute-start.3 = (f32[2,32,256]{2,1,0:T(8,128)S(1)}, f32[2,32,256]{2,1,0:T(8,128)S(1)}, u32[]{:S(2)}, u32[]{:S(2)}) collective-permute-start(f32[2,32,256]{2,1,0:T(8,128)S(1)} %get-tuple-element.21), channel_id=1, source_target_pairs={{0,1},{1,0},{2,3},{3,2},{4,5},{5,4},{6,7},{7,6},{8,9},{9,8},{10,11... | collective-permute-start | bytes 196616 | tf_op jit(solution)/shard_map/ppermute | solution.py:388
  45.2 0.5 %collective-permute-start.4 = (f32[2,32,256]{2,1,0:T(8,128)S(1)}, f32[2,32,256]{2,1,0:T(8,128)S(1)}, u32[]{:S(2)}, u32[]{:S(2)}) collective-permute-start(f32[2,32,256]{2,1,0:T(8,128)S(1)} %get-tuple-element.22), channel_id=1, source_target_pairs={{0,2},{1,3},{2,0},{3,1},{4,6},{5,7},{6,4},{7,5},{8,10},{9,11},{10,... | collective-permute-start | bytes 196616 | tf_op jit(solution)/shard_map/ppermute | solution.py:388
  45.7 2.0 %collective-permute-start.5 = (f32[2,32,256]{2,1,0:T(8,128)S(1)}, f32[2,32,256]{2,1,0:T(8,128)S(1)}, u32[]{:S(2)}, u32[]{:S(2)}) collective-permute-start(f32[2,32,256]{2,1,0:T(8,128)S(1)} %get-tuple-element.23), channel_id=1, source_target_pairs={{0,3},{1,2},{2,1},{3,0},{4,7},{5,6},{6,5},{7,4},{8,11},{9,10},{10,... | collective-permute-start | bytes 196616 | tf_op jit(solution)/shard_map/ppermute | solution.py:388
  47.7 0.8 %collective-permute-done.3.refs_1_ = f32[2,32,256]{2,1,0:T(8,128)S(1)} collective-permute-done((f32[2,32,256]{2,1,0:T(8,128)S(1)}, f32[2,32,256]{2,1,0:T(8,128)S(1)}, u32[]{:S(2)}, u32[]{:S(2)}) %collective-permute-start.3) | collective-permute-done | bytes 65568 | tf_op jit(solution)/shard_map/ppermute | solution.py:388
  48.5 1.6 %collective-permute-done.4.refs_2_ = f32[2,32,256]{2,1,0:T(8,128)S(1)} collective-permute-done((f32[2,32,256]{2,1,0:T(8,128)S(1)}, f32[2,32,256]{2,1,0:T(8,128)S(1)}, u32[]{:S(2)}, u32[]{:S(2)}) %collective-permute-start.4) | collective-permute-done | bytes 65568 | tf_op jit(solution)/shard_map/ppermute | solution.py:388
  50.1 0.7 %collective-permute-done.5.refs_3_ = f32[2,32,256]{2,1,0:T(8,128)S(1)} collective-permute-done((f32[2,32,256]{2,1,0:T(8,128)S(1)}, f32[2,32,256]{2,1,0:T(8,128)S(1)}, u32[]{:S(2)}, u32[]{:S(2)}) %collective-permute-start.5) | collective-permute-done | bytes 65568 | tf_op jit(solution)/shard_map/ppermute | solution.py:388
  50.9 0.8 %shard_map.64 = (f32[128,256]{1,0:T(8,128)}, f32[128,256]{1,0:T(8,128)}) custom-call(s32[1]{0:T(128)} %bitcast.place_ref.refs_0_, f32[2,32,256]{2,1,0:T(8,128)S(1)} %get-tuple-element.20.refs_0_, f32[2,32,256]{2,1,0:T(8,128)S(1)} %collective-permute-done.3.refs_1_, f32[2,32,256]{2,1,0:T(8,128)S(1)} %collective-permute-done.4.refs_2_, ...), custom_call_target="tpu_custom_call" | custom-call | tf_op jit(solution)/shard_map/pallas_call | solution.py:367
Async XLA Ops:
  1.6 6.1 %collective-permute-start = (f32[2,32,256]{2,1,0:T(8,128)S(1)}, f32[2,32,256]{2,1,0:T(8,128)S(1)}, u32[]{:S(2)}, u32[]{:S(2)}) collective-permute-start(f32[2,32,256]{2,1,0:T(8,128)S(1)} %get-tuple-element.14), channel_id=1, source_target_pairs={{0,1},{1,0},{2,3},{3,2},{4,5},{5,4},{6,7},{7,6},{8,9},{9,8},{10,11... | collective-permute-start | bytes 196616 | tf_op jit(solution)/shard_map/ppermute | solution.py:388
  4.6 4.3 %collective-permute-start.1 = (f32[2,32,256]{2,1,0:T(8,128)S(1)}, f32[2,32,256]{2,1,0:T(8,128)S(1)}, u32[]{:S(2)}, u32[]{:S(2)}) collective-permute-start(f32[2,32,256]{2,1,0:T(8,128)S(1)} %get-tuple-element.15), channel_id=1, source_target_pairs={{0,2},{1,3},{2,0},{3,1},{4,6},{5,7},{6,4},{7,5},{8,10},{9,11},{10,... | collective-permute-start | bytes 196616 | tf_op jit(solution)/shard_map/ppermute | solution.py:388
  6.1 5.2 %collective-permute-start.2 = (f32[2,32,256]{2,1,0:T(8,128)S(1)}, f32[2,32,256]{2,1,0:T(8,128)S(1)}, u32[]{:S(2)}, u32[]{:S(2)}) collective-permute-start(f32[2,32,256]{2,1,0:T(8,128)S(1)} %get-tuple-element.16), channel_id=1, source_target_pairs={{0,3},{1,2},{2,1},{3,0},{4,7},{5,6},{6,5},{7,4},{8,11},{9,10},{10,... | collective-permute-start | bytes 196616 | tf_op jit(solution)/shard_map/ppermute | solution.py:388
  44.1 4.4 %collective-permute-start.3 = (f32[2,32,256]{2,1,0:T(8,128)S(1)}, f32[2,32,256]{2,1,0:T(8,128)S(1)}, u32[]{:S(2)}, u32[]{:S(2)}) collective-permute-start(f32[2,32,256]{2,1,0:T(8,128)S(1)} %get-tuple-element.21), channel_id=1, source_target_pairs={{0,1},{1,0},{2,3},{3,2},{4,5},{5,4},{6,7},{7,6},{8,9},{9,8},{10,11... | collective-permute-start | bytes 196616 | tf_op jit(solution)/shard_map/ppermute | solution.py:388
  45.2 5.0 %collective-permute-start.4 = (f32[2,32,256]{2,1,0:T(8,128)S(1)}, f32[2,32,256]{2,1,0:T(8,128)S(1)}, u32[]{:S(2)}, u32[]{:S(2)}) collective-permute-start(f32[2,32,256]{2,1,0:T(8,128)S(1)} %get-tuple-element.22), channel_id=1, source_target_pairs={{0,2},{1,3},{2,0},{3,1},{4,6},{5,7},{6,4},{7,5},{8,10},{9,11},{10,... | collective-permute-start | bytes 196616 | tf_op jit(solution)/shard_map/ppermute | solution.py:388
  45.7 5.2 %collective-permute-start.5 = (f32[2,32,256]{2,1,0:T(8,128)S(1)}, f32[2,32,256]{2,1,0:T(8,128)S(1)}, u32[]{:S(2)}, u32[]{:S(2)}) collective-permute-start(f32[2,32,256]{2,1,0:T(8,128)S(1)} %get-tuple-element.23), channel_id=1, source_target_pairs={{0,3},{1,2},{2,1},{3,0},{4,7},{5,6},{6,5},{7,4},{8,11},{9,10},{10,... | collective-permute-start | bytes 196616 | tf_op jit(solution)/shard_map/ppermute | solution.py:388

commit v4 on v3

--- a/solution.py
+++ b/solution.py
@@ -144,17 +144,26 @@
     return lax.broadcasted_iota(jnp.int32, shape, len(shape) - 1) // width
 
 
-def pick_chunks(pieces, width):
+def swap_chunks(pieces):
+    pieces = list(pieces)
+    count = len(pieces)
+    width = LANES // count
     chunk = lane_chunk(pieces[0].shape, width)
-    out = pieces[-1]
-    for index in range(len(pieces) - 2, -1, -1):
-        out = jnp.where(chunk == index, pieces[index], out)
-    return out
-
-
-def rolled(value, chunks, width):
-    shift = chunks * width % LANES
-    return pltpu.roll(value, shift, 1) if shift else value
+    step = count // 2
+    while step:
+        stays = chunk & step == 0
+        for first in range(count):
+            if first & step:
+                continue
+            near, far = pieces[first], pieces[first + step]
+            pieces[first] = jnp.where(stays, near, pltpu.roll(far, step * width, 1))
+            pieces[first + step] = jnp.where(stays, pltpu.roll(near, LANES - step * width, 1), far)
+        step //= 2
+    return pieces
+
+
+def sublane_rows(value, group):
+    return value[group * SUBLANES : (group + 1) * SUBLANES]
 
 
 def wave_squares(k1, k2, total):
@@ -223,18 +232,10 @@
             if not packed:
                 out_ref[tile] = spectrum
                 continue
-            width = LANES // count
-            turns = [rolled(spectrum, shift, width) for shift in range(count)]
-            for chunk in range(count):
-                for field in range(3):
-                    base = field * height
-                    pieces = [
-                        turns[(group - chunk) % count][base + group * SUBLANES : base + (group + 1) * SUBLANES]
-                        for group in range(count)
-                    ]
-                    out_ref[tile * count + chunk, field * SUBLANES : (field + 1) * SUBLANES, :] = pick_chunks(
-                        pieces, width
-                    )
+            for field in range(3):
+                part = spectrum[field * height : (field + 1) * height]
+                for chunk, piece in enumerate(swap_chunks([sublane_rows(part, group) for group in range(count)])):
+                    out_ref[tile * count + chunk, field * SUBLANES : (field + 1) * SUBLANES, :] = piece
 
 
 def place_of(band, source, bands):
@@ -243,59 +244,46 @@
 
 def advance_kernel(packed, count, in_ref, table_ref, matrix_ref, matrix_t_ref, out_ref):
     if packed:
-        width = LANES // count
         radix = in_ref.shape[0] // count
         tiles = []
         for band in range(radix):
             rows = []
             for source in range(count):
                 block = in_ref[place_of(band, source, radix)]
-                turns = [
-                    [rolled(block[field * SUBLANES : (field + 1) * SUBLANES], shift, width) for shift in range(count)]
-                    for field in range(3)
-                ]
-                for group in range(count):
-                    rows.append(
-                        pick_chunks(
-                            [turns[min(place, 2)][(place - group) % count] for place in range(count)], width
-                        )
-                    )
+                rows += swap_chunks([sublane_rows(block, min(field, 2)) for field in range(count)])
             tiles.append(jnp.concatenate(rows, axis=0))
     else:
         radix = in_ref.shape[0]
         tiles = [in_ref[band] for band in range(radix)]
     operands = paired(real_dft(tiles), 0)
     low_half = lax.broadcasted_iota(jnp.int32, (2 * LANES, LANES), 1) < HALF
-    products = []
+    scaled = []
     for index, operand in enumerate(operands):
         high, low = split_value(operand)
         both = dot(matrix_t_ref[0, index], jnp.concatenate([high, low], axis=1))
         spectrum = both[:, :LANES] + (both[:, LANES:] + dot(matrix_t_ref[1, index], high))
-        scaled = table_ref[index] * spectrum
-        advanced = scaled + pltpu.roll(scaled, HALF, 1)
+        scaled.append(table_ref[index] * spectrum)
+    products = []
+    for index, value in enumerate(scaled):
+        advanced = value + pltpu.roll(value, HALF, 1)
         high = advanced.astype(jnp.bfloat16).astype(jnp.float32)
         both = dot(matrix_ref[0, index], jnp.where(low_half, high, advanced - high).astype(jnp.bfloat16))
         rest = dot(matrix_ref[1, index], high.astype(jnp.bfloat16))
         products.append(both + (pltpu.roll(both, HALF, 1) + rest))
     bands = real_dft_transposed(unpaired(products, 0))
+    low_half = lane_chunk((SUBLANES, LANES), HALF) == 0
+    even = lane_chunk((SUBLANES, LANES), HALF // 2) % 2 == 0
     for band, value in enumerate(bands):
         if not packed:
             out_ref[band] = value
             continue
-        height = LANES // count
         for target in range(count):
-            for field in range(2):
-                pieces = [
-                    rolled(
-                        value[target * height + group * SUBLANES : target * height + (group + 1) * SUBLANES],
-                        group - field,
-                        width,
-                    )
-                    for group in range(count)
-                ]
-                out_ref[place_of(band, target, radix), field * SUBLANES : (field + 1) * SUBLANES, :] = pick_chunks(
-                    pieces, width
-                )
+            part = value[target * LANES // count : (target + 1) * LANES // count]
+            near = jnp.where(low_half, sublane_rows(part, 0), sublane_rows(part, 2))
+            far = jnp.where(low_half, sublane_rows(part, 1), sublane_rows(part, 3))
+            place = place_of(band, target, radix)
+            out_ref[place, :SUBLANES, :] = jnp.where(even, near, pltpu.roll(far, HALF // 2, 1))
+            out_ref[place, SUBLANES:, :] = jnp.where(even, pltpu.roll(near, LANES - HALF // 2, 1), far)
 
 
 def inverse_kernel(packed, count, shift, place_ref, in_ref, matrix_t_ref, *refs):
@@ -308,15 +296,9 @@
         if not packed:
             tiles.append(in_ref[tile])
             continue
-        width = LANES // count
-        turns = [[rolled(in_ref[tile * count + chunk], step, width) for step in range(count)] for chunk in range(count)]
         rows = []
         for field in range(2):
-            part = slice(field * SUBLANES, (field + 1) * SUBLANES)
-            for group in range(count):
-                rows.append(
-                    pick_chunks([turns[chunk][(chunk - group) % count][part] for chunk in range(count)], width)
-                )
+            rows += swap_chunks([sublane_rows(in_ref[tile * count + chunk], field) for chunk in range(count)])
         tiles.append(jnp.concatenate(rows, axis=0))
     products = []
     for index in range(radix // 2):
@@ -397,7 +379,7 @@
     radix = total_cols // LANES
     width = total_cols // (bands * count)
     assert row_count == LANES and total_rows == total_cols and count & (count - 1) == 0
-    packed = height == SUBLANES * count and width * count == LANES
+    packed = count == 4 and height == SUBLANES * count and width * count == LANES
     place = lax.axis_index("col")
     places = place[None].astype(jnp.int32)
     axes = ("col", "core", "outer")

time: 51.9 us -> 50.8 us (0.979)
  Pallas kernels: 6.6 us -> 5.52 us
    pallas_call x6, Pallas kernels: 6.6 us -> 5.52 us  [call(): pl.pallas_call(kernel, out_shape=out_shape, in_specs=specs, out_specs=jax...]
where the time goes in v4:
time: 50.8 us; the launch traced here: 50.6 us
  blocking collectives  29.5 us (58%)
  starting transfers between devices  8.13 us (16%)
  waiting for transfers between devices  6.76 us (13%)
  Pallas kernels  5.52 us (11%)
  between operations  0.69 us (1%)
    all_to_all x1, blocking collectives, on_device(): spectra = lax.all_to_all(spectra, axes, 0, 0, tiled=True)  15.6 us
    all_to_all x1, blocking collectives, on_device(): advanced = lax.all_to_all(advanced, axes, 0, 0, tiled=True)  13.8 us
    ppermute x6, starting transfers between devices, swap_blocks(): lax.ppermute(blocks[step], 'col', [(s, s ^ step) for s in range(count)])  8.13 us
    ppermute x6, waiting for transfers between devices, swap_blocks(): lax.ppermute(blocks[step], 'col', [(s, s ^ step) for s in range(count)])  6.76 us
    pallas_call x6, Pallas kernels, call(): pl.pallas_call(kernel, out_shape=out_shape, in_specs=specs, out_specs=jax...  5.52 us
  transfers between devices with their start and end apart: 6, of which 5 were waited for; matrix products, arithmetic and copies ran while one was open for 0% of the time, Pallas kernels for 3%

profile of v4, /device:TPU:0, one launch (start us, length us, event | category | flops | bytes accessed | tf_op | source)
XLA Modules:
  0.0 50.6 jit_solution(16668979571447976702)
XLA Ops:
  0.6 0.9 %shard_map.59 = (f32[2,32,256]{2,1,0:T(8,128)S(1)}, f32[2,32,256]{2,1,0:T(8,128)S(1)}, f32[2,32,256]{2,1,0:T(8,128)S(1)}, f32[2,32,256]{2,1,0:T(8,128)S(1)}) custom-call(s32[1]{0:T(128)} %bitcast.place_ref.refs_0_, f32[128,256]{1,0:T(8,128)} %refs_0_.1, f32[128,256]{1,0:T(8,128)} %refs_1_.2), custom_call_target="tpu_custom_call" | custom-call | tf_op jit(solution)/shard_map/pallas_call | solution.py:349
  1.6 3.0 %collective-permute-start = (f32[2,32,256]{2,1,0:T(8,128)S(1)}, f32[2,32,256]{2,1,0:T(8,128)S(1)}, u32[]{:S(2)}, u32[]{:S(2)}) collective-permute-start(f32[2,32,256]{2,1,0:T(8,128)S(1)} %get-tuple-element.14), channel_id=1, source_target_pairs={{0,1},{1,0},{2,3},{3,2},{4,5},{5,4},{6,7},{7,6},{8,9},{9,8},{10,11... | collective-permute-start | bytes 196616 | tf_op jit(solution)/shard_map/ppermute | solution.py:370
  4.6 1.5 %collective-permute-start.1 = (f32[2,32,256]{2,1,0:T(8,128)S(1)}, f32[2,32,256]{2,1,0:T(8,128)S(1)}, u32[]{:S(2)}, u32[]{:S(2)}) collective-permute-start(f32[2,32,256]{2,1,0:T(8,128)S(1)} %get-tuple-element.15), channel_id=1, source_target_pairs={{0,2},{1,3},{2,0},{3,1},{4,6},{5,7},{6,4},{7,5},{8,10},{9,11},{10,... | collective-permute-start | bytes 196616 | tf_op jit(solution)/shard_map/ppermute | solution.py:370
  6.1 0.0 collective-permute-start.2
  6.2 1.6 %shard_map.60 = (f32[4,256,128]{2,1,0:T(8,128)S(1)}, bf16[2,4,256,256]{3,2,1,0:T(8,128)(2,1)S(1)}, bf16[2,4,256,256]{3,2,1,0:T(8,128)(2,1)S(1)}) custom-call(s32[1]{0:T(128)} %bitcast.1.refs_0_, bf16[2,4,256,256]{3,2,1,0:T(8,128)(2,1)} %constant.20.clone.refs_1_, bf16[2,4,256,256]{3,2,1,0:T(8,128)(2,1)} %constant.21.clone.refs_2_), custom_call_target="tpu_custom_call" | custom-call | tf_op jit(solution)/shard_map/pallas_call | solution.py:349
  7.7 0.0 collective-permute-done.refs_2_
  7.7 1.1 %collective-permute-done.1.refs_3_ = f32[2,32,256]{2,1,0:T(8,128)S(1)} collective-permute-done((f32[2,32,256]{2,1,0:T(8,128)S(1)}, f32[2,32,256]{2,1,0:T(8,128)S(1)}, u32[]{:S(2)}, u32[]{:S(2)}) %collective-permute-start.1) | collective-permute-done | bytes 65568 | tf_op jit(solution)/shard_map/ppermute | solution.py:370
  8.9 2.4 %collective-permute-done.2.refs_4_ = f32[2,32,256]{2,1,0:T(8,128)S(1)} collective-permute-done((f32[2,32,256]{2,1,0:T(8,128)S(1)}, f32[2,32,256]{2,1,0:T(8,128)S(1)}, u32[]{:S(2)}, u32[]{:S(2)}) %collective-permute-start.2) | collective-permute-done | bytes 65568 | tf_op jit(solution)/shard_map/ppermute | solution.py:370
  11.3 0.6 %shard_map.61 = f32[32,24,128]{2,1,0:T(8,128)S(1)} custom-call(s32[1]{0:T(128)} %bitcast.place_ref.refs_0_, f32[2,32,256]{2,1,0:T(8,128)S(1)} %get-tuple-element.13.refs_1_, f32[2,32,256]{2,1,0:T(8,128)S(1)} %collective-permute-done.refs_2_, f32[2,32,256]{2,1,0:T(8,128)S(1)} %collective-permute-done.1.refs_3_, ...), custom_call_target="tpu_custom_call" | custom-call | tf_op jit(solution)/shard_map/pallas_call | solution.py:349
  11.9 15.6 %all_to_all.10.refs_0_ = f32[32,24,128]{2,1,0:T(8,128)S(1)} all-to-all(f32[32,24,128]{2,1,0:T(8,128)S(1)} %shard_map.61), channel_id=1, replica_groups=mesh['outer'=4,'core'=2,'col'=4] {'col','core','outer'}, dimensions={0} | all-to-all | bytes 786432 | tf_op jit(solution)/shard_map/all_to_all | solution.py:417
  27.5 1.2 %shard_map.62 = f32[32,16,128]{2,1,0:T(8,128)S(1)} custom-call(f32[32,24,128]{2,1,0:T(8,128)S(1)} %all_to_all.10.refs_0_, f32[4,256,128]{2,1,0:T(8,128)S(1)} %get-tuple-element.18.refs_1_, bf16[2,4,256,256]{3,2,1,0:T(8,128)(2,1)S(1)} %get-tuple-element.17.refs_5_.refs_2_, bf16[2,4,256,256]{3,2,1,0:T(8,128)(2,1)S(1)} %get-tuple-element.19.refs_3_.refs_2_), custom_call_target="tpu_custom_call" | custom-call | tf_op jit(solution)/shard_map/pallas_call | solution.py:349
  28.7 13.8 %all_to_all.11.refs_1_ = f32[32,16,128]{2,1,0:T(8,128)S(1)} all-to-all(f32[32,16,128]{2,1,0:T(8,128)S(1)} %shard_map.62), channel_id=1, replica_groups=mesh['outer'=4,'core'=2,'col'=4] {'col','core','outer'}, dimensions={0} | all-to-all | bytes 524288 | tf_op jit(solution)/shard_map/all_to_all | solution.py:434
  42.5 0.5 shard_map.63
  43.1 1.1 %collective-permute-start.3 = (f32[2,32,256]{2,1,0:T(8,128)S(1)}, f32[2,32,256]{2,1,0:T(8,128)S(1)}, u32[]{:S(2)}, u32[]{:S(2)}) collective-permute-start(f32[2,32,256]{2,1,0:T(8,128)S(1)} %get-tuple-element.21), channel_id=1, source_target_pairs={{0,1},{1,0},{2,3},{3,2},{4,5},{5,4},{6,7},{7,6},{8,9},{9,8},{10,11... | collective-permute-start | bytes 196616 | tf_op jit(solution)/shard_map/ppermute | solution.py:370
  44.1 0.5 %collective-permute-start.4 = (f32[2,32,256]{2,1,0:T(8,128)S(1)}, f32[2,32,256]{2,1,0:T(8,128)S(1)}, u32[]{:S(2)}, u32[]{:S(2)}) collective-permute-start(f32[2,32,256]{2,1,0:T(8,128)S(1)} %get-tuple-element.22), channel_id=1, source_target_pairs={{0,2},{1,3},{2,0},{3,1},{4,6},{5,7},{6,4},{7,5},{8,10},{9,11},{10,... | collective-permute-start | bytes 196616 | tf_op jit(solution)/shard_map/ppermute | solution.py:370
  44.6 2.0 %collective-permute-start.5 = (f32[2,32,256]{2,1,0:T(8,128)S(1)}, f32[2,32,256]{2,1,0:T(8,128)S(1)}, u32[]{:S(2)}, u32[]{:S(2)}) collective-permute-start(f32[2,32,256]{2,1,0:T(8,128)S(1)} %get-tuple-element.23), channel_id=1, source_target_pairs={{0,3},{1,2},{2,1},{3,0},{4,7},{5,6},{6,5},{7,4},{8,11},{9,10},{10,... | collective-permute-start | bytes 196616 | tf_op jit(solution)/shard_map/ppermute | solution.py:370
  46.6 0.8 %collective-permute-done.3.refs_1_ = f32[2,32,256]{2,1,0:T(8,128)S(1)} collective-permute-done((f32[2,32,256]{2,1,0:T(8,128)S(1)}, f32[2,32,256]{2,1,0:T(8,128)S(1)}, u32[]{:S(2)}, u32[]{:S(2)}) %collective-permute-start.3) | collective-permute-done | bytes 65568 | tf_op jit(solution)/shard_map/ppermute | solution.py:370
  47.5 1.6 %collective-permute-done.4.refs_2_ = f32[2,32,256]{2,1,0:T(8,128)S(1)} collective-permute-done((f32[2,32,256]{2,1,0:T(8,128)S(1)}, f32[2,32,256]{2,1,0:T(8,128)S(1)}, u32[]{:S(2)}, u32[]{:S(2)}) %collective-permute-start.4) | collective-permute-done | bytes 65568 | tf_op jit(solution)/shard_map/ppermute | solution.py:370
  49.1 0.7 %collective-permute-done.5.refs_3_ = f32[2,32,256]{2,1,0:T(8,128)S(1)} collective-permute-done((f32[2,32,256]{2,1,0:T(8,128)S(1)}, f32[2,32,256]{2,1,0:T(8,128)S(1)}, u32[]{:S(2)}, u32[]{:S(2)}) %collective-permute-start.5) | collective-permute-done | bytes 65568 | tf_op jit(solution)/shard_map/ppermute | solution.py:370
  49.8 0.8 %shard_map.64 = (f32[128,256]{1,0:T(8,128)}, f32[128,256]{1,0:T(8,128)}) custom-call(s32[1]{0:T(128)} %bitcast.place_ref.refs_0_, f32[2,32,256]{2,1,0:T(8,128)S(1)} %get-tuple-element.20.refs_0_, f32[2,32,256]{2,1,0:T(8,128)S(1)} %collective-permute-done.3.refs_1_, f32[2,32,256]{2,1,0:T(8,128)S(1)} %collective-permute-done.4.refs_2_, ...), custom_call_target="tpu_custom_call" | custom-call | tf_op jit(solution)/shard_map/pallas_call | solution.py:349
Async XLA Ops:
  1.6 6.1 %collective-permute-start = (f32[2,32,256]{2,1,0:T(8,128)S(1)}, f32[2,32,256]{2,1,0:T(8,128)S(1)}, u32[]{:S(2)}, u32[]{:S(2)}) collective-permute-start(f32[2,32,256]{2,1,0:T(8,128)S(1)} %get-tuple-element.14), channel_id=1, source_target_pairs={{0,1},{1,0},{2,3},{3,2},{4,5},{5,4},{6,7},{7,6},{8,9},{9,8},{10,11... | collective-permute-start | bytes 196616 | tf_op jit(solution)/shard_map/ppermute | solution.py:370
  4.6 4.3 %collective-permute-start.1 = (f32[2,32,256]{2,1,0:T(8,128)S(1)}, f32[2,32,256]{2,1,0:T(8,128)S(1)}, u32[]{:S(2)}, u32[]{:S(2)}) collective-permute-start(f32[2,32,256]{2,1,0:T(8,128)S(1)} %get-tuple-element.15), channel_id=1, source_target_pairs={{0,2},{1,3},{2,0},{3,1},{4,6},{5,7},{6,4},{7,5},{8,10},{9,11},{10,... | collective-permute-start | bytes 196616 | tf_op jit(solution)/shard_map/ppermute | solution.py:370
  6.1 5.2 %collective-permute-start.2 = (f32[2,32,256]{2,1,0:T(8,128)S(1)}, f32[2,32,256]{2,1,0:T(8,128)S(1)}, u32[]{:S(2)}, u32[]{:S(2)}) collective-permute-start(f32[2,32,256]{2,1,0:T(8,128)S(1)} %get-tuple-element.16), channel_id=1, source_target_pairs={{0,3},{1,2},{2,1},{3,0},{4,7},{5,6},{6,5},{7,4},{8,11},{9,10},{10,... | collective-permute-start | bytes 196616 | tf_op jit(solution)/shard_map/ppermute | solution.py:370
  43.1 4.4 %collective-permute-start.3 = (f32[2,32,256]{2,1,0:T(8,128)S(1)}, f32[2,32,256]{2,1,0:T(8,128)S(1)}, u32[]{:S(2)}, u32[]{:S(2)}) collective-permute-start(f32[2,32,256]{2,1,0:T(8,128)S(1)} %get-tuple-element.21), channel_id=1, source_target_pairs={{0,1},{1,0},{2,3},{3,2},{4,5},{5,4},{6,7},{7,6},{8,9},{9,8},{10,11... | collective-permute-start | bytes 196616 | tf_op jit(solution)/shard_map/ppermute | solution.py:370
  44.1 5.0 %collective-permute-start.4 = (f32[2,32,256]{2,1,0:T(8,128)S(1)}, f32[2,32,256]{2,1,0:T(8,128)S(1)}, u32[]{:S(2)}, u32[]{:S(2)}) collective-permute-start(f32[2,32,256]{2,1,0:T(8,128)S(1)} %get-tuple-element.22), channel_id=1, source_target_pairs={{0,2},{1,3},{2,0},{3,1},{4,6},{5,7},{6,4},{7,5},{8,10},{9,11},{10,... | collective-permute-start | bytes 196616 | tf_op jit(solution)/shard_map/ppermute | solution.py:370
  44.6 5.2 %collective-permute-start.5 = (f32[2,32,256]{2,1,0:T(8,128)S(1)}, f32[2,32,256]{2,1,0:T(8,128)S(1)}, u32[]{:S(2)}, u32[]{:S(2)}) collective-permute-start(f32[2,32,256]{2,1,0:T(8,128)S(1)} %get-tuple-element.23), channel_id=1, source_target_pairs={{0,3},{1,2},{2,1},{3,0},{4,7},{5,6},{6,5},{7,4},{8,11},{9,10},{10,... | collective-permute-start | bytes 196616 | tf_op jit(solution)/shard_map/ppermute | solution.py:370

commit v5 on v4

--- a/solution.py
+++ b/solution.py
@@ -60,7 +60,9 @@
 
 
 def dot_pairs(left, right):
-    return dot(left[0], right[0]) + (dot(left[0], right[1]) + dot(left[1], right[0]))
+    height = left[0].shape[0]
+    both = dot(jnp.concatenate(left, axis=0), right[0])
+    return both[:height] + (both[height:] + dot(left[0], right[1]))
 
 
 def turn(value, k, period, sign):
@@ -212,7 +214,7 @@
     *block_refs, matrix_ref, out_ref, buffer_ref = refs
     count = len(block_refs)
     place = place_ref[0]
-    for step, block_ref in enumerate(block_refs):
+    for step, block_ref in zip(steps(count), block_refs):
         buffer_ref[place ^ step] = block_ref[...]
     cols = buffer_ref.shape[-1]
     height = buffer_ref.shape[2]
@@ -311,8 +313,12 @@
         part = slice(tile * LANES, (tile + 1) * LANES)
         buffer_ref[place ^ target, 0, :, part] = value[:height] + shift
         buffer_ref[place ^ target, 1, :, part] = value[height:]
-    for step, out_ref in enumerate(out_refs):
+    for step, out_ref in zip(steps(count), out_refs):
         out_ref[...] = buffer_ref[step]
+
+
+def steps(count):
+    return [0, count - 1] + list(range(1, count - 1))
 
 
 def start_all(copies):
@@ -327,10 +333,10 @@
     in_refs, out_refs = field_refs[:2], field_refs[2:]
     height = out_refs[0].shape[1]
     copies = []
-    for step, out_ref in enumerate(out_refs):
+    for index, (step, out_ref) in enumerate(zip(steps(len(out_refs)), out_refs)):
         rows = pl.ds((place_ref[0] ^ step) * height, height)
         for field, in_ref in enumerate(in_refs):
-            copies.append(pltpu.make_async_copy(in_ref.at[rows], out_ref.at[field], semaphores.at[step, field]))
+            copies.append(pltpu.make_async_copy(in_ref.at[rows], out_ref.at[field], semaphores.at[index, field]))
     start_all(copies)
 
 
@@ -338,10 +344,10 @@
     *block_refs, first_ref, second_ref, semaphores = refs
     height = block_refs[0].shape[1]
     copies = []
-    for step, block_ref in enumerate(block_refs):
+    for index, (step, block_ref) in enumerate(zip(steps(len(block_refs)), block_refs)):
         rows = pl.ds((place_ref[0] ^ step) * height, height)
         for field, out_ref in enumerate((first_ref, second_ref)):
-            copies.append(pltpu.make_async_copy(block_ref.at[field], out_ref.at[rows], semaphores.at[step, field]))
+            copies.append(pltpu.make_async_copy(block_ref.at[field], out_ref.at[rows], semaphores.at[index, field]))
     start_all(copies)
 
 
@@ -367,7 +373,8 @@
 def swap_blocks(blocks):
     count = len(blocks)
     return [blocks[0]] + [
-        lax.ppermute(blocks[step], "col", [(s, s ^ step) for s in range(count)]) for step in range(1, count)
+        lax.ppermute(block, "col", [(s, s ^ step) for s in range(count)])
+        for step, block in list(zip(steps(count), blocks))[1:]
     ]
 
 

time: 50.8 us -> 50.8 us (level)
  waiting for transfers between devices: 6.76 us -> 5.84 us
  blocking collectives: 29.5 us -> 30.4 us
    all_to_all x1, blocking collectives: 15.6 us -> 16.5 us  [on_device(): spectra = lax.all_to_all(spectra, axes, 0, 0, tiled=True)]
    ppermute x6, waiting for transfers between devices: 6.76 us -> 5.84 us  [swap_blocks(): lax.ppermute(block, 'col', [(s, s ^ step) for s in range(count)])]
  transfers between devices with their start and end apart: 6 -> 6, of which waited for: 5 -> 6; matrix products, arithmetic and copies ran while one was open for 0% -> 0% of each run, Pallas kernels for 3% -> 3%
where the time goes in v5:
time: 50.8 us; the launch traced here: 50.6 us
  blocking collectives  30.4 us (60%)
  starting transfers between devices  8.18 us (16%)
  waiting for transfers between devices  5.84 us (11%)
  Pallas kernels  5.47 us (11%)
  between operations  0.68 us (1%)
    all_to_all x1, blocking collectives, on_device(): spectra = lax.all_to_all(spectra, axes, 0, 0, tiled=True)  16.5 us
    all_to_all x1, blocking collectives, on_device(): advanced = lax.all_to_all(advanced, axes, 0, 0, tiled=True)  13.8 us
    ppermute x6, starting transfers between devices, swap_blocks(): lax.ppermute(block, 'col', [(s, s ^ step) for s in range(count)])  8.18 us
    ppermute x6, waiting for transfers between devices, swap_blocks(): lax.ppermute(block, 'col', [(s, s ^ step) for s in range(count)])  5.84 us
    pallas_call x6, Pallas kernels, call(): pl.pallas_call(kernel, out_shape=out_shape, in_specs=specs, out_specs=jax...  5.47 us
  transfers between devices with their start and end apart: 6, of which 6 were waited for; matrix products, arithmetic and copies ran while one was open for 0% of the time, Pallas kernels for 3%

profile of v5, /device:TPU:0, one launch (start us, length us, event | category | flops | bytes accessed | tf_op | source)
XLA Modules:
  0.0 50.6 jit_solution(10361976785075505081)
XLA Ops:
  0.6 0.9 %shard_map.59 = (f32[2,32,256]{2,1,0:T(8,128)S(1)}, f32[2,32,256]{2,1,0:T(8,128)S(1)}, f32[2,32,256]{2,1,0:T(8,128)S(1)}, f32[2,32,256]{2,1,0:T(8,128)S(1)}) custom-call(s32[1]{0:T(128)} %bitcast.place_ref.refs_0_, f32[128,256]{1,0:T(8,128)} %refs_0_.1, f32[128,256]{1,0:T(8,128)} %refs_1_.2), custom_call_target="tpu_custom_call" | custom-call | tf_op jit(solution)/shard_map/pallas_call | solution.py:355
  1.6 4.0 %collective-permute-start = (f32[2,32,256]{2,1,0:T(8,128)S(1)}, f32[2,32,256]{2,1,0:T(8,128)S(1)}, u32[]{:S(2)}, u32[]{:S(2)}) collective-permute-start(f32[2,32,256]{2,1,0:T(8,128)S(1)} %get-tuple-element.14), channel_id=1, source_target_pairs={{0,3},{1,2},{2,1},{3,0},{4,7},{5,6},{6,5},{7,4},{8,11},{9,10},{10,... | collective-permute-start | bytes 196616 | tf_op jit(solution)/shard_map/ppermute | solution.py:376
  5.6 0.5 %collective-permute-start.1 = (f32[2,32,256]{2,1,0:T(8,128)S(1)}, f32[2,32,256]{2,1,0:T(8,128)S(1)}, u32[]{:S(2)}, u32[]{:S(2)}) collective-permute-start(f32[2,32,256]{2,1,0:T(8,128)S(1)} %get-tuple-element.15), channel_id=1, source_target_pairs={{0,1},{1,0},{2,3},{3,2},{4,5},{5,4},{6,7},{7,6},{8,9},{9,8},{10,11... | collective-permute-start | bytes 196616 | tf_op jit(solution)/shard_map/ppermute | solution.py:376
  6.1 0.1 collective-permute-start.2
  6.2 1.6 %shard_map.60 = (f32[4,256,128]{2,1,0:T(8,128)S(1)}, bf16[2,4,256,256]{3,2,1,0:T(8,128)(2,1)S(1)}, bf16[2,4,256,256]{3,2,1,0:T(8,128)(2,1)S(1)}) custom-call(s32[1]{0:T(128)} %bitcast.1.refs_0_, bf16[2,4,256,256]{3,2,1,0:T(8,128)(2,1)} %constant.20.clone.refs_1_, bf16[2,4,256,256]{3,2,1,0:T(8,128)(2,1)} %constant.21.clone.refs_2_), custom_call_target="tpu_custom_call" | custom-call | tf_op jit(solution)/shard_map/pallas_call | solution.py:355
  7.8 0.2 collective-permute-done.refs_2_
  8.0 1.9 %collective-permute-done.1.refs_3_ = f32[2,32,256]{2,1,0:T(8,128)S(1)} collective-permute-done((f32[2,32,256]{2,1,0:T(8,128)S(1)}, f32[2,32,256]{2,1,0:T(8,128)S(1)}, u32[]{:S(2)}, u32[]{:S(2)}) %collective-permute-start.1) | collective-permute-done | bytes 65568 | tf_op jit(solution)/shard_map/ppermute | solution.py:376
  9.8 0.5 %collective-permute-done.2.refs_4_ = f32[2,32,256]{2,1,0:T(8,128)S(1)} collective-permute-done((f32[2,32,256]{2,1,0:T(8,128)S(1)}, f32[2,32,256]{2,1,0:T(8,128)S(1)}, u32[]{:S(2)}, u32[]{:S(2)}) %collective-permute-start.2) | collective-permute-done | bytes 65568 | tf_op jit(solution)/shard_map/ppermute | solution.py:376
  10.4 0.6 %shard_map.61 = f32[32,24,128]{2,1,0:T(8,128)S(1)} custom-call(s32[1]{0:T(128)} %bitcast.place_ref.refs_0_, f32[2,32,256]{2,1,0:T(8,128)S(1)} %get-tuple-element.13.refs_1_, f32[2,32,256]{2,1,0:T(8,128)S(1)} %collective-permute-done.refs_2_, f32[2,32,256]{2,1,0:T(8,128)S(1)} %collective-permute-done.1.refs_3_, ...), custom_call_target="tpu_custom_call" | custom-call | tf_op jit(solution)/shard_map/pallas_call | solution.py:355
  11.0 16.5 %all_to_all.10.refs_0_ = f32[32,24,128]{2,1,0:T(8,128)S(1)} all-to-all(f32[32,24,128]{2,1,0:T(8,128)S(1)} %shard_map.61), channel_id=1, replica_groups=mesh['outer'=4,'core'=2,'col'=4] {'col','core','outer'}, dimensions={0} | all-to-all | bytes 786432 | tf_op jit(solution)/shard_map/all_to_all | solution.py:424
  27.5 1.2 %shard_map.62 = f32[32,16,128]{2,1,0:T(8,128)S(1)} custom-call(f32[32,24,128]{2,1,0:T(8,128)S(1)} %all_to_all.10.refs_0_, f32[4,256,128]{2,1,0:T(8,128)S(1)} %get-tuple-element.18.refs_1_, bf16[2,4,256,256]{3,2,1,0:T(8,128)(2,1)S(1)} %get-tuple-element.17.refs_5_.refs_2_, bf16[2,4,256,256]{3,2,1,0:T(8,128)(2,1)S(1)} %get-tuple-element.19.refs_3_.refs_2_), custom_call_target="tpu_custom_call" | custom-call | tf_op jit(solution)/shard_map/pallas_call | solution.py:355
  28.7 13.8 %all_to_all.11.refs_1_ = f32[32,16,128]{2,1,0:T(8,128)S(1)} all-to-all(f32[32,16,128]{2,1,0:T(8,128)S(1)} %shard_map.62), channel_id=1, replica_groups=mesh['outer'=4,'core'=2,'col'=4] {'col','core','outer'}, dimensions={0} | all-to-all | bytes 524288 | tf_op jit(solution)/shard_map/all_to_all | solution.py:441
  42.5 0.5 shard_map.63
  43.0 1.0 %collective-permute-start.3 = (f32[2,32,256]{2,1,0:T(8,128)S(1)}, f32[2,32,256]{2,1,0:T(8,128)S(1)}, u32[]{:S(2)}, u32[]{:S(2)}) collective-permute-start(f32[2,32,256]{2,1,0:T(8,128)S(1)} %get-tuple-element.21), channel_id=1, source_target_pairs={{0,3},{1,2},{2,1},{3,0},{4,7},{5,6},{6,5},{7,4},{8,11},{9,10},{10,... | collective-permute-start | bytes 196616 | tf_op jit(solution)/shard_map/ppermute | solution.py:376
  44.0 1.5 %collective-permute-start.4 = (f32[2,32,256]{2,1,0:T(8,128)S(1)}, f32[2,32,256]{2,1,0:T(8,128)S(1)}, u32[]{:S(2)}, u32[]{:S(2)}) collective-permute-start(f32[2,32,256]{2,1,0:T(8,128)S(1)} %get-tuple-element.22), channel_id=1, source_target_pairs={{0,1},{1,0},{2,3},{3,2},{4,5},{5,4},{6,7},{7,6},{8,9},{9,8},{10,11... | collective-permute-start | bytes 196616 | tf_op jit(solution)/shard_map/ppermute | solution.py:376
  45.5 1.0 %collective-permute-start.5 = (f32[2,32,256]{2,1,0:T(8,128)S(1)}, f32[2,32,256]{2,1,0:T(8,128)S(1)}, u32[]{:S(2)}, u32[]{:S(2)}) collective-permute-start(f32[2,32,256]{2,1,0:T(8,128)S(1)} %get-tuple-element.23), channel_id=1, source_target_pairs={{0,2},{1,3},{2,0},{3,1},{4,6},{5,7},{6,4},{7,5},{8,10},{9,11},{10,... | collective-permute-start | bytes 196616 | tf_op jit(solution)/shard_map/ppermute | solution.py:376
  46.5 2.4 %collective-permute-done.3.refs_1_ = f32[2,32,256]{2,1,0:T(8,128)S(1)} collective-permute-done((f32[2,32,256]{2,1,0:T(8,128)S(1)}, f32[2,32,256]{2,1,0:T(8,128)S(1)}, u32[]{:S(2)}, u32[]{:S(2)}) %collective-permute-start.3) | collective-permute-done | bytes 65568 | tf_op jit(solution)/shard_map/ppermute | solution.py:376
  48.9 0.2 collective-permute-done.4.refs_2_
  49.2 0.6 %collective-permute-done.5.refs_3_ = f32[2,32,256]{2,1,0:T(8,128)S(1)} collective-permute-done((f32[2,32,256]{2,1,0:T(8,128)S(1)}, f32[2,32,256]{2,1,0:T(8,128)S(1)}, u32[]{:S(2)}, u32[]{:S(2)}) %collective-permute-start.5) | collective-permute-done | bytes 65568 | tf_op jit(solution)/shard_map/ppermute | solution.py:376
  49.8 0.8 %shard_map.64 = (f32[128,256]{1,0:T(8,128)}, f32[128,256]{1,0:T(8,128)}) custom-call(s32[1]{0:T(128)} %bitcast.place_ref.refs_0_, f32[2,32,256]{2,1,0:T(8,128)S(1)} %get-tuple-element.20.refs_0_, f32[2,32,256]{2,1,0:T(8,128)S(1)} %collective-permute-done.3.refs_1_, f32[2,32,256]{2,1,0:T(8,128)S(1)} %collective-permute-done.4.refs_2_, ...), custom_call_target="tpu_custom_call" | custom-call | tf_op jit(solution)/shard_map/pallas_call | solution.py:355
Async XLA Ops:
  1.6 6.4 %collective-permute-start = (f32[2,32,256]{2,1,0:T(8,128)S(1)}, f32[2,32,256]{2,1,0:T(8,128)S(1)}, u32[]{:S(2)}, u32[]{:S(2)}) collective-permute-start(f32[2,32,256]{2,1,0:T(8,128)S(1)} %get-tuple-element.14), channel_id=1, source_target_pairs={{0,3},{1,2},{2,1},{3,0},{4,7},{5,6},{6,5},{7,4},{8,11},{9,10},{10,... | collective-permute-start | bytes 196616 | tf_op jit(solution)/shard_map/ppermute | solution.py:376
  5.6 4.3 %collective-permute-start.1 = (f32[2,32,256]{2,1,0:T(8,128)S(1)}, f32[2,32,256]{2,1,0:T(8,128)S(1)}, u32[]{:S(2)}, u32[]{:S(2)}) collective-permute-start(f32[2,32,256]{2,1,0:T(8,128)S(1)} %get-tuple-element.15), channel_id=1, source_target_pairs={{0,1},{1,0},{2,3},{3,2},{4,5},{5,4},{6,7},{7,6},{8,9},{9,8},{10,11... | collective-permute-start | bytes 196616 | tf_op jit(solution)/shard_map/ppermute | solution.py:376
  6.1 4.3 %collective-permute-start.2 = (f32[2,32,256]{2,1,0:T(8,128)S(1)}, f32[2,32,256]{2,1,0:T(8,128)S(1)}, u32[]{:S(2)}, u32[]{:S(2)}) collective-permute-start(f32[2,32,256]{2,1,0:T(8,128)S(1)} %get-tuple-element.16), channel_id=1, source_target_pairs={{0,2},{1,3},{2,0},{3,1},{4,6},{5,7},{6,4},{7,5},{8,10},{9,11},{10,... | collective-permute-start | bytes 196616 | tf_op jit(solution)/shard_map/ppermute | solution.py:376
  43.0 5.9 %collective-permute-start.3 = (f32[2,32,256]{2,1,0:T(8,128)S(1)}, f32[2,32,256]{2,1,0:T(8,128)S(1)}, u32[]{:S(2)}, u32[]{:S(2)}) collective-permute-start(f32[2,32,256]{2,1,0:T(8,128)S(1)} %get-tuple-element.21), channel_id=1, source_target_pairs={{0,3},{1,2},{2,1},{3,0},{4,7},{5,6},{6,5},{7,4},{8,11},{9,10},{10,... | collective-permute-start | bytes 196616 | tf_op jit(solution)/shard_map/ppermute | solution.py:376
  44.0 5.1 %collective-permute-start.4 = (f32[2,32,256]{2,1,0:T(8,128)S(1)}, f32[2,32,256]{2,1,0:T(8,128)S(1)}, u32[]{:S(2)}, u32[]{:S(2)}) collective-permute-start(f32[2,32,256]{2,1,0:T(8,128)S(1)} %get-tuple-element.22), channel_id=1, source_target_pairs={{0,1},{1,0},{2,3},{3,2},{4,5},{5,4},{6,7},{7,6},{8,9},{9,8},{10,11... | collective-permute-start | bytes 196616 | tf_op jit(solution)/shard_map/ppermute | solution.py:376
  45.5 4.3 %collective-permute-start.5 = (f32[2,32,256]{2,1,0:T(8,128)S(1)}, f32[2,32,256]{2,1,0:T(8,128)S(1)}, u32[]{:S(2)}, u32[]{:S(2)}) collective-permute-start(f32[2,32,256]{2,1,0:T(8,128)S(1)} %get-tuple-element.23), channel_id=1, source_target_pairs={{0,2},{1,3},{2,0},{3,1},{4,6},{5,7},{6,4},{7,5},{8,10},{9,11},{10,... | collective-permute-start | bytes 196616 | tf_op jit(solution)/shard_map/ppermute | solution.py:376

commit v6 on v5

--- a/solution.py
+++ b/solution.py
@@ -17,6 +17,8 @@
 LANES = 128
 HALF = LANES // 2
 CORES = 2
+PAIR = 2
+COL = ("col_high", "col_low")
 SUBLANES = 8
 VMEM_LIMIT = 36 << 20
 VMEM = pl.BlockSpec(memory_space=pltpu.VMEM)
@@ -241,7 +243,9 @@
 
 
 def place_of(band, source, bands):
-    return (source * CORES + band % CORES) * (bands // CORES) + band // CORES
+    outer, core = band // CORES, band % CORES
+    high, low = source // PAIR, source % PAIR
+    return ((high * CORES + core) * PAIR + low) * (bands // CORES) + outer
 
 
 def advance_kernel(packed, count, in_ref, table_ref, matrix_ref, matrix_t_ref, out_ref):
@@ -373,23 +377,23 @@
 def swap_blocks(blocks):
     count = len(blocks)
     return [blocks[0]] + [
-        lax.ppermute(block, "col", [(s, s ^ step) for s in range(count)])
+        lax.ppermute(block, COL, [(s, s ^ step) for s in range(count)])
         for step, block in list(zip(steps(count), blocks))[1:]
     ]
 
 
 def on_device(substrate, activator):
     row_count, col_count = substrate.shape
-    bands, count = lax.axis_size("outer") * lax.axis_size("core"), lax.axis_size("col")
+    bands, count = lax.axis_size("outer") * lax.axis_size("core"), lax.axis_size(COL)
     total_rows, total_cols = row_count * bands, col_count * count
     height = row_count // count
     radix = total_cols // LANES
     width = total_cols // (bands * count)
     assert row_count == LANES and total_rows == total_cols and count & (count - 1) == 0
     packed = count == 4 and height == SUBLANES * count and width * count == LANES
-    place = lax.axis_index("col")
+    place = lax.axis_index(COL)
     places = place[None].astype(jnp.int32)
-    axes = ("col", "core", "outer")
+    axes = ("col_high", "core", "col_low", "outer")
     devices = lax.axis_index(axes)[None].astype(jnp.int32)
     matrices = basis_matrices(total_rows)
     forward = split_constant(matrices)
@@ -426,8 +430,8 @@
         spectra = spectra.reshape(radix, 3, height, LANES // width, width)
         spectra = jnp.transpose(spectra, (0, 3, 1, 2, 4)).reshape(bands * count, -1)
         spectra = lax.all_to_all(spectra, axes, 0, 0, tiled=True)
-        spectra = spectra.reshape(count, CORES, bands // CORES, 3, height, width)
-        spectra = jnp.transpose(spectra, (3, 2, 1, 0, 4, 5))
+        spectra = spectra.reshape(count // PAIR, CORES, PAIR, bands // CORES, 3, height, width)
+        spectra = jnp.transpose(spectra, (4, 3, 1, 0, 2, 5, 6))
         spectra = spectra.reshape(3, bands, row_count, width)
         rest = jnp.zeros((bands, row_count, HALF - 2 * width), jnp.float32)
         spectra = jnp.concatenate([spectra[0], spectra[1], rest, spectra[2], spectra[2], rest], axis=2)
@@ -440,8 +444,8 @@
     if packed:
         advanced = lax.all_to_all(advanced, axes, 0, 0, tiled=True)
     else:
-        advanced = advanced[:, :, : 2 * width].reshape(bands // CORES, CORES, count, height, 2, width)
-        advanced = jnp.transpose(advanced, (2, 1, 0, 4, 3, 5)).reshape(bands * count, -1)
+        advanced = advanced[:, :, : 2 * width].reshape(bands // CORES, CORES, count // PAIR, PAIR, height, 2, width)
+        advanced = jnp.transpose(advanced, (2, 1, 3, 0, 5, 4, 6)).reshape(bands * count, -1)
         advanced = lax.all_to_all(advanced, axes, 0, 0, tiled=True)
         advanced = jnp.transpose(advanced.reshape(radix, LANES // width, 2, height, width), (0, 2, 3, 1, 4))
         advanced = advanced.reshape(radix, 2 * height, LANES)
@@ -469,6 +473,6 @@
 
 def solution(mesh):
     bands, count = mesh.shape["row"], mesh.shape["col"]
-    split = Mesh(mesh.devices.reshape(bands // CORES, CORES, count), ("outer", "core", "col"))
-    spec = P(("outer", "core"), "col")
+    split = Mesh(mesh.devices.reshape(bands // CORES, CORES, count // PAIR, PAIR), ("outer", "core") + COL)
+    spec = P(("outer", "core"), COL)
     return jax.shard_map(on_device, mesh=split, in_specs=(spec, spec), out_specs=(spec, spec), check_vma=False)

time: 50.8 us -> 50.9 us (level)
    all_to_all x1, blocking collectives: 16.5 us -> 17.9 us  [on_device(): spectra = lax.all_to_all(spectra, axes, 0, 0, tiled=True)]
    all_to_all x1, blocking collectives: 13.8 us -> 12.6 us  [on_device(): advanced = lax.all_to_all(advanced, axes, 0, 0, tiled=True)]
  transfers between devices with their start and end apart: 6 -> 6, of which waited for: 6 -> 5; matrix products, arithmetic and copies ran while one was open for 0% -> 0% of each run, Pallas kernels for 3% -> 3%
where the time goes in v6:
time: 50.9 us; the launch traced here: 50.6 us
  blocking collectives  30.5 us (60%)
  starting transfers between devices  8.18 us (16%)
  waiting for transfers between devices  5.74 us (11%)
  Pallas kernels  5.47 us (11%)
  between operations  0.68 us (1%)
    all_to_all x1, blocking collectives, on_device(): spectra = lax.all_to_all(spectra, axes, 0, 0, tiled=True)  17.9 us
    all_to_all x1, blocking collectives, on_device(): advanced = lax.all_to_all(advanced, axes, 0, 0, tiled=True)  12.6 us
    ppermute x6, starting transfers between devices, swap_blocks(): lax.ppermute(block, COL, [(s, s ^ step) for s in range(count)])  8.18 us
    ppermute x6, waiting for transfers between devices, swap_blocks(): lax.ppermute(block, COL, [(s, s ^ step) for s in range(count)])  5.74 us
    pallas_call x6, Pallas kernels, call(): pl.pallas_call(kernel, out_shape=out_shape, in_specs=specs, out_specs=jax...  5.47 us
  transfers between devices with their start and end apart: 6, of which 5 were waited for; matrix products, arithmetic and copies ran while one was open for 0% of the time, Pallas kernels for 3%

profile of v6, /device:TPU:0, one launch (start us, length us, event | category | flops | bytes accessed | tf_op | source)
XLA Modules:
  0.0 50.6 jit_solution(8446153594772902733)
XLA Ops:
  0.6 0.9 %shard_map.59 = (f32[2,32,256]{2,1,0:T(8,128)S(1)}, f32[2,32,256]{2,1,0:T(8,128)S(1)}, f32[2,32,256]{2,1,0:T(8,128)S(1)}, f32[2,32,256]{2,1,0:T(8,128)S(1)}) custom-call(s32[1]{0:T(128)} %bitcast.place_ref.refs_0_, f32[128,256]{1,0:T(8,128)} %refs_0_.1, f32[128,256]{1,0:T(8,128)} %refs_1_.2), custom_call_target="tpu_custom_call" | custom-call | tf_op jit(solution)/shard_map/pallas_call | solution.py:359
  1.6 4.0 %collective-permute-start = (f32[2,32,256]{2,1,0:T(8,128)S(1)}, f32[2,32,256]{2,1,0:T(8,128)S(1)}, u32[]{:S(2)}, u32[]{:S(2)}) collective-permute-start(f32[2,32,256]{2,1,0:T(8,128)S(1)} %get-tuple-element.14), channel_id=1, source_target_pairs={{0,3},{1,2},{2,1},{3,0},{4,7},{5,6},{6,5},{7,4},{8,11},{9,10},{10,... | collective-permute-start | bytes 196616 | tf_op jit(solution)/shard_map/ppermute | solution.py:380
  5.6 0.5 %collective-permute-start.1 = (f32[2,32,256]{2,1,0:T(8,128)S(1)}, f32[2,32,256]{2,1,0:T(8,128)S(1)}, u32[]{:S(2)}, u32[]{:S(2)}) collective-permute-start(f32[2,32,256]{2,1,0:T(8,128)S(1)} %get-tuple-element.15), channel_id=1, source_target_pairs={{0,1},{1,0},{2,3},{3,2},{4,5},{5,4},{6,7},{7,6},{8,9},{9,8},{10,11... | collective-permute-start | bytes 196616 | tf_op jit(solution)/shard_map/ppermute | solution.py:380
  6.1 0.1 collective-permute-start.2
  6.2 1.6 %shard_map.60 = (f32[4,256,128]{2,1,0:T(8,128)S(1)}, bf16[2,4,256,256]{3,2,1,0:T(8,128)(2,1)S(1)}, bf16[2,4,256,256]{3,2,1,0:T(8,128)(2,1)S(1)}) custom-call(s32[1]{0:T(128)} %bitcast.1.refs_0_, bf16[2,4,256,256]{3,2,1,0:T(8,128)(2,1)} %constant.26.clone.refs_1_, bf16[2,4,256,256]{3,2,1,0:T(8,128)(2,1)} %constant.27.clone.refs_2_), custom_call_target="tpu_custom_call" | custom-call | tf_op jit(solution)/shard_map/pallas_call | solution.py:359
  7.8 0.2 collective-permute-done.refs_2_
  8.0 1.9 %collective-permute-done.1.refs_3_ = f32[2,32,256]{2,1,0:T(8,128)S(1)} collective-permute-done((f32[2,32,256]{2,1,0:T(8,128)S(1)}, f32[2,32,256]{2,1,0:T(8,128)S(1)}, u32[]{:S(2)}, u32[]{:S(2)}) %collective-permute-start.1) | collective-permute-done | bytes 65568 | tf_op jit(solution)/shard_map/ppermute | solution.py:380
  9.8 0.5 %collective-permute-done.2.refs_4_ = f32[2,32,256]{2,1,0:T(8,128)S(1)} collective-permute-done((f32[2,32,256]{2,1,0:T(8,128)S(1)}, f32[2,32,256]{2,1,0:T(8,128)S(1)}, u32[]{:S(2)}, u32[]{:S(2)}) %collective-permute-start.2) | collective-permute-done | bytes 65568 | tf_op jit(solution)/shard_map/ppermute | solution.py:380
  10.4 0.6 %shard_map.61 = f32[32,24,128]{2,1,0:T(8,128)S(1)} custom-call(s32[1]{0:T(128)} %bitcast.place_ref.refs_0_, f32[2,32,256]{2,1,0:T(8,128)S(1)} %get-tuple-element.13.refs_1_, f32[2,32,256]{2,1,0:T(8,128)S(1)} %collective-permute-done.refs_2_, f32[2,32,256]{2,1,0:T(8,128)S(1)} %collective-permute-done.1.refs_3_, ...), custom_call_target="tpu_custom_call" | custom-call | tf_op jit(solution)/shard_map/pallas_call | solution.py:359
  11.0 17.9 %all_to_all.10.refs_0_ = f32[32,24,128]{2,1,0:T(8,128)S(1)} all-to-all(f32[32,24,128]{2,1,0:T(8,128)S(1)} %shard_map.61), channel_id=1, replica_groups=mesh['outer'=4,'core'=2,'col_high'=2,'col_low'=2] {'col_high','core','co..., dimensions={0} | all-to-all | bytes 786432 | tf_op jit(solution)/shard_map/all_to_all | solution.py:428
  28.9 1.2 %shard_map.62 = f32[32,16,128]{2,1,0:T(8,128)S(1)} custom-call(f32[32,24,128]{2,1,0:T(8,128)S(1)} %all_to_all.10.refs_0_, f32[4,256,128]{2,1,0:T(8,128)S(1)} %get-tuple-element.18.refs_1_, bf16[2,4,256,256]{3,2,1,0:T(8,128)(2,1)S(1)} %get-tuple-element.17.refs_5_.refs_2_, bf16[2,4,256,256]{3,2,1,0:T(8,128)(2,1)S(1)} %get-tuple-element.19.refs_3_.refs_2_), custom_call_target="tpu_custom_call" | custom-call | tf_op jit(solution)/shard_map/pallas_call | solution.py:359
  30.1 12.6 %all_to_all.11.refs_1_ = f32[32,16,128]{2,1,0:T(8,128)S(1)} all-to-all(f32[32,16,128]{2,1,0:T(8,128)S(1)} %shard_map.62), channel_id=1, replica_groups=mesh['outer'=4,'core'=2,'col_high'=2,'col_low'=2] {'col_high','core','co..., dimensions={0} | all-to-all | bytes 524288 | tf_op jit(solution)/shard_map/all_to_all | solution.py:445
  42.7 0.5 shard_map.63
  43.2 0.8 %collective-permute-start.3 = (f32[2,32,256]{2,1,0:T(8,128)S(1)}, f32[2,32,256]{2,1,0:T(8,128)S(1)}, u32[]{:S(2)}, u32[]{:S(2)}) collective-permute-start(f32[2,32,256]{2,1,0:T(8,128)S(1)} %get-tuple-element.21), channel_id=1, source_target_pairs={{0,3},{1,2},{2,1},{3,0},{4,7},{5,6},{6,5},{7,4},{8,11},{9,10},{10,... | collective-permute-start | bytes 196616 | tf_op jit(solution)/shard_map/ppermute | solution.py:380
  43.9 1.7 %collective-permute-start.4 = (f32[2,32,256]{2,1,0:T(8,128)S(1)}, f32[2,32,256]{2,1,0:T(8,128)S(1)}, u32[]{:S(2)}, u32[]{:S(2)}) collective-permute-start(f32[2,32,256]{2,1,0:T(8,128)S(1)} %get-tuple-element.22), channel_id=1, source_target_pairs={{0,1},{1,0},{2,3},{3,2},{4,5},{5,4},{6,7},{7,6},{8,9},{9,8},{10,11... | collective-permute-start | bytes 196616 | tf_op jit(solution)/shard_map/ppermute | solution.py:380
  45.6 1.1 %collective-permute-start.5 = (f32[2,32,256]{2,1,0:T(8,128)S(1)}, f32[2,32,256]{2,1,0:T(8,128)S(1)}, u32[]{:S(2)}, u32[]{:S(2)}) collective-permute-start(f32[2,32,256]{2,1,0:T(8,128)S(1)} %get-tuple-element.23), channel_id=1, source_target_pairs={{0,2},{1,3},{2,0},{3,1},{4,6},{5,7},{6,4},{7,5},{8,10},{9,11},{10,... | collective-permute-start | bytes 196616 | tf_op jit(solution)/shard_map/ppermute | solution.py:380
  46.7 2.2 %collective-permute-done.3.refs_1_ = f32[2,32,256]{2,1,0:T(8,128)S(1)} collective-permute-done((f32[2,32,256]{2,1,0:T(8,128)S(1)}, f32[2,32,256]{2,1,0:T(8,128)S(1)}, u32[]{:S(2)}, u32[]{:S(2)}) %collective-permute-start.3) | collective-permute-done | bytes 65568 | tf_op jit(solution)/shard_map/ppermute | solution.py:380
  48.9 0.0 collective-permute-done.4.refs_2_
  48.9 0.9 %collective-permute-done.5.refs_3_ = f32[2,32,256]{2,1,0:T(8,128)S(1)} collective-permute-done((f32[2,32,256]{2,1,0:T(8,128)S(1)}, f32[2,32,256]{2,1,0:T(8,128)S(1)}, u32[]{:S(2)}, u32[]{:S(2)}) %collective-permute-start.5) | collective-permute-done | bytes 65568 | tf_op jit(solution)/shard_map/ppermute | solution.py:380
  49.9 0.8 %shard_map.64 = (f32[128,256]{1,0:T(8,128)}, f32[128,256]{1,0:T(8,128)}) custom-call(s32[1]{0:T(128)} %bitcast.place_ref.refs_0_, f32[2,32,256]{2,1,0:T(8,128)S(1)} %get-tuple-element.20.refs_0_, f32[2,32,256]{2,1,0:T(8,128)S(1)} %collective-permute-done.3.refs_1_, f32[2,32,256]{2,1,0:T(8,128)S(1)} %collective-permute-done.4.refs_2_, ...), custom_call_target="tpu_custom_call" | custom-call | tf_op jit(solution)/shard_map/pallas_call | solution.py:359
Async XLA Ops:
  1.6 6.4 %collective-permute-start = (f32[2,32,256]{2,1,0:T(8,128)S(1)}, f32[2,32,256]{2,1,0:T(8,128)S(1)}, u32[]{:S(2)}, u32[]{:S(2)}) collective-permute-start(f32[2,32,256]{2,1,0:T(8,128)S(1)} %get-tuple-element.14), channel_id=1, source_target_pairs={{0,3},{1,2},{2,1},{3,0},{4,7},{5,6},{6,5},{7,4},{8,11},{9,10},{10,... | collective-permute-start | bytes 196616 | tf_op jit(solution)/shard_map/ppermute | solution.py:380
  5.6 4.3 %collective-permute-start.1 = (f32[2,32,256]{2,1,0:T(8,128)S(1)}, f32[2,32,256]{2,1,0:T(8,128)S(1)}, u32[]{:S(2)}, u32[]{:S(2)}) collective-permute-start(f32[2,32,256]{2,1,0:T(8,128)S(1)} %get-tuple-element.15), channel_id=1, source_target_pairs={{0,1},{1,0},{2,3},{3,2},{4,5},{5,4},{6,7},{7,6},{8,9},{9,8},{10,11... | collective-permute-start | bytes 196616 | tf_op jit(solution)/shard_map/ppermute | solution.py:380
  6.1 4.3 %collective-permute-start.2 = (f32[2,32,256]{2,1,0:T(8,128)S(1)}, f32[2,32,256]{2,1,0:T(8,128)S(1)}, u32[]{:S(2)}, u32[]{:S(2)}) collective-permute-start(f32[2,32,256]{2,1,0:T(8,128)S(1)} %get-tuple-element.16), channel_id=1, source_target_pairs={{0,2},{1,3},{2,0},{3,1},{4,6},{5,7},{6,4},{7,5},{8,10},{9,11},{10,... | collective-permute-start | bytes 196616 | tf_op jit(solution)/shard_map/ppermute | solution.py:380
  43.2 5.8 %collective-permute-start.3 = (f32[2,32,256]{2,1,0:T(8,128)S(1)}, f32[2,32,256]{2,1,0:T(8,128)S(1)}, u32[]{:S(2)}, u32[]{:S(2)}) collective-permute-start(f32[2,32,256]{2,1,0:T(8,128)S(1)} %get-tuple-element.21), channel_id=1, source_target_pairs={{0,3},{1,2},{2,1},{3,0},{4,7},{5,6},{6,5},{7,4},{8,11},{9,10},{10,... | collective-permute-start | bytes 196616 | tf_op jit(solution)/shard_map/ppermute | solution.py:380
  43.9 5.0 %collective-permute-start.4 = (f32[2,32,256]{2,1,0:T(8,128)S(1)}, f32[2,32,256]{2,1,0:T(8,128)S(1)}, u32[]{:S(2)}, u32[]{:S(2)}) collective-permute-start(f32[2,32,256]{2,1,0:T(8,128)S(1)} %get-tuple-element.22), channel_id=1, source_target_pairs={{0,1},{1,0},{2,3},{3,2},{4,5},{5,4},{6,7},{7,6},{8,9},{9,8},{10,11... | collective-permute-start | bytes 196616 | tf_op jit(solution)/shard_map/ppermute | solution.py:380
  45.6 4.3 %collective-permute-start.5 = (f32[2,32,256]{2,1,0:T(8,128)S(1)}, f32[2,32,256]{2,1,0:T(8,128)S(1)}, u32[]{:S(2)}, u32[]{:S(2)}) collective-permute-start(f32[2,32,256]{2,1,0:T(8,128)S(1)} %get-tuple-element.23), channel_id=1, source_target_pairs={{0,2},{1,3},{2,0},{3,1},{4,6},{5,7},{6,4},{7,5},{8,10},{9,11},{10,... | collective-permute-start | bytes 196616 | tf_op jit(solution)/shard_map/ppermute | solution.py:380

commit v7 on v5

--- a/solution.py
+++ b/solution.py
@@ -17,11 +17,11 @@
 LANES = 128
 HALF = LANES // 2
 CORES = 2
+AXES = ("col", "core", "outer")
 SUBLANES = 8
 VMEM_LIMIT = 36 << 20
 VMEM = pl.BlockSpec(memory_space=pltpu.VMEM)
 HBM = pl.BlockSpec(memory_space=pltpu.HBM)
-SMEM = pl.BlockSpec(memory_space=pltpu.SMEM)
 
 
 def basis_matrices(total):
@@ -176,7 +176,7 @@
     return angular * angular
 
 
-def tables_kernel(total_rows, total_cols, width, device_ref, *refs):
+def tables_kernel(total_rows, total_cols, width, *refs):
     *matrix_refs, table_ref, loaded_ref, loaded_t_ref, semaphores = refs
     copies = [
         pltpu.make_async_copy(source, target, semaphores.at[index])
@@ -186,7 +186,7 @@
         copy.start()
     radix = total_rows // LANES
     chunks = LANES // width
-    device = device_ref[0]
+    device = lax.axis_index(AXES)
     tile, place = device // chunks, device % chunks
     lane = lax.broadcasted_iota(jnp.int32, (1, LANES), 1)
     col_class = jnp.where(tile == 0, 0, jnp.where(tile == 1, total_cols // LANES // 2, tile // 2))
@@ -210,10 +210,10 @@
         copy.wait()
 
 
-def forward_kernel(packed, place_ref, *refs):
+def forward_kernel(packed, *refs):
     *block_refs, matrix_ref, out_ref, buffer_ref = refs
     count = len(block_refs)
-    place = place_ref[0]
+    place = lax.axis_index("col")
     for step, block_ref in zip(steps(count), block_refs):
         buffer_ref[place ^ step] = block_ref[...]
     cols = buffer_ref.shape[-1]
@@ -288,8 +288,8 @@
             out_ref[place, SUBLANES:, :] = jnp.where(even, pltpu.roll(near, LANES - HALF // 2, 1), far)
 
 
-def inverse_kernel(packed, count, shift, place_ref, in_ref, matrix_t_ref, *refs):
-    place = place_ref[0]
+def inverse_kernel(packed, count, shift, in_ref, matrix_t_ref, *refs):
+    place = lax.axis_index("col")
     *out_refs, buffer_ref = refs
     radix = 2 * matrix_t_ref.shape[1]
     _, height, cols = out_refs[0].shape
@@ -328,24 +328,24 @@
         copy.wait()
 
 
-def cut_kernel(place_ref, *refs):
+def cut_kernel(*refs):
     *field_refs, semaphores = refs
     in_refs, out_refs = field_refs[:2], field_refs[2:]
     height = out_refs[0].shape[1]
     copies = []
     for index, (step, out_ref) in enumerate(zip(steps(len(out_refs)), out_refs)):
-        rows = pl.ds((place_ref[0] ^ step) * height, height)
+        rows = pl.ds((lax.axis_index("col") ^ step) * height, height)
         for field, in_ref in enumerate(in_refs):
             copies.append(pltpu.make_async_copy(in_ref.at[rows], out_ref.at[field], semaphores.at[index, field]))
     start_all(copies)
 
 
-def join_kernel(place_ref, *refs):
+def join_kernel(*refs):
     *block_refs, first_ref, second_ref, semaphores = refs
     height = block_refs[0].shape[1]
     copies = []
     for index, (step, block_ref) in enumerate(zip(steps(len(block_refs)), block_refs)):
-        rows = pl.ds((place_ref[0] ^ step) * height, height)
+        rows = pl.ds((lax.axis_index("col") ^ step) * height, height)
         for field, out_ref in enumerate((first_ref, second_ref)):
             copies.append(pltpu.make_async_copy(block_ref.at[field], out_ref.at[rows], semaphores.at[index, field]))
     start_all(copies)
@@ -387,10 +387,6 @@
     width = total_cols // (bands * count)
     assert row_count == LANES and total_rows == total_cols and count & (count - 1) == 0
     packed = count == 4 and height == SUBLANES * count and width * count == LANES
-    place = lax.axis_index("col")
-    places = place[None].astype(jnp.int32)
-    axes = ("col", "core", "outer")
-    devices = lax.axis_index(axes)[None].astype(jnp.int32)
     matrices = basis_matrices(total_rows)
     forward = split_constant(matrices)
     backward = split_constant(np.swapaxes(matrices, 1, 2))
@@ -400,8 +396,8 @@
         call(
             cut_kernel,
             [block] * count,
-            [SMEM] + [HBM] * 2,
-            (places, in_hbm(substrate), in_hbm(activator)),
+            [HBM] * 2,
+            (in_hbm(substrate), in_hbm(activator)),
             [pltpu.SemaphoreType.DMA((count, 2))],
         )
     )
@@ -409,23 +405,23 @@
         lambda *refs: tables_kernel(total_rows, total_cols, width, *refs),
         [float_shape(radix // 2, 2 * LANES, LANES)]
         + [jax.ShapeDtypeStruct(constant.shape, constant.dtype) for constant in (forward, backward)],
-        [SMEM, HBM, HBM],
-        (devices, in_hbm(forward), in_hbm(backward)),
+        [HBM, HBM],
+        (in_hbm(forward), in_hbm(backward)),
         [pltpu.SemaphoreType.DMA((2,))],
     )
     spectra = call(
         lambda *refs: forward_kernel(packed, *refs),
         float_shape(bands * count, 3 * SUBLANES, LANES) if packed else float_shape(radix, 3 * height, LANES),
-        [SMEM] + [VMEM] * (count + 1),
-        (places, *blocks, forward),
+        [VMEM] * (count + 1),
+        (*blocks, forward),
         [pltpu.VMEM((count, 2, height, col_count), jnp.float32)],
     )
     if packed:
-        spectra = lax.all_to_all(spectra, axes, 0, 0, tiled=True)
+        spectra = lax.all_to_all(spectra, AXES, 0, 0, tiled=True)
     else:
         spectra = spectra.reshape(radix, 3, height, LANES // width, width)
         spectra = jnp.transpose(spectra, (0, 3, 1, 2, 4)).reshape(bands * count, -1)
-        spectra = lax.all_to_all(spectra, axes, 0, 0, tiled=True)
+        spectra = lax.all_to_all(spectra, AXES, 0, 0, tiled=True)
         spectra = spectra.reshape(count, CORES, bands // CORES, 3, height, width)
         spectra = jnp.transpose(spectra, (3, 2, 1, 0, 4, 5))
         spectra = spectra.reshape(3, bands, row_count, width)
@@ -438,11 +434,11 @@
         (spectra, table, forward, backward),
     )
     if packed:
-        advanced = lax.all_to_all(advanced, axes, 0, 0, tiled=True)
+        advanced = lax.all_to_all(advanced, AXES, 0, 0, tiled=True)
     else:
         advanced = advanced[:, :, : 2 * width].reshape(bands // CORES, CORES, count, height, 2, width)
         advanced = jnp.transpose(advanced, (2, 1, 0, 4, 3, 5)).reshape(bands * count, -1)
-        advanced = lax.all_to_all(advanced, axes, 0, 0, tiled=True)
+        advanced = lax.all_to_all(advanced, AXES, 0, 0, tiled=True)
         advanced = jnp.transpose(advanced.reshape(radix, LANES // width, 2, height, width), (0, 2, 3, 1, 4))
         advanced = advanced.reshape(radix, 2 * height, LANES)
     shift = FEED_RATE * math.expm1(-FEED_RATE * 0.5 * TIME_STEP) / -FEED_RATE
@@ -450,8 +446,8 @@
         call(
             lambda *refs: inverse_kernel(packed, count, shift, *refs),
             [block] * count,
-            [SMEM] + [VMEM] * 2,
-            (places, advanced, backward),
+            [VMEM] * 2,
+            (advanced, backward),
             [pltpu.VMEM((count, 2, height, col_count), jnp.float32)],
         )
     )
@@ -459,8 +455,8 @@
         call(
             join_kernel,
             [float_shape(row_count, col_count)] * 2,
-            [SMEM] + [VMEM] * count,
-            (places, *blocks),
+            [VMEM] * count,
+            (*blocks,),
             [pltpu.SemaphoreType.DMA((count, 2))],
             HBM,
         )

time: 50.8 us -> 50.8 us (level)
  no operation moved by 1% of the time
where the time goes in v7:
time: 50.8 us; the launch traced here: 50.5 us
  blocking collectives  30.4 us (60%)
  starting transfers between devices  8.18 us (16%)
  waiting for transfers between devices  5.84 us (11%)
  Pallas kernels  5.47 us (11%)
  between operations  0.67 us (1%)
    all_to_all x1, blocking collectives, on_device(): spectra = lax.all_to_all(spectra, AXES, 0, 0, tiled=True)  16.5 us
    all_to_all x1, blocking collectives, on_device(): advanced = lax.all_to_all(advanced, AXES, 0, 0, tiled=True)  13.8 us
    ppermute x6, starting transfers between devices, swap_blocks(): lax.ppermute(block, 'col', [(s, s ^ step) for s in range(count)])  8.18 us
    ppermute x6, waiting for transfers between devices, swap_blocks(): lax.ppermute(block, 'col', [(s, s ^ step) for s in range(count)])  5.84 us
    pallas_call x6, Pallas kernels, call(): pl.pallas_call(kernel, out_shape=out_shape, in_specs=specs, out_specs=jax...  5.47 us
  transfers between devices with their start and end apart: 6, of which 6 were waited for; matrix products, arithmetic and copies ran while one was open for 0% of the time, Pallas kernels for 3%

profile of v7, /device:TPU:0, one launch (start us, length us, event | category | flops | bytes accessed | tf_op | source)
XLA Modules:
  0.0 50.5 jit_solution(13851256590996005865)
XLA Ops:
  0.6 1.0 %shard_map.59 = (f32[2,32,256]{2,1,0:T(8,128)S(1)}, f32[2,32,256]{2,1,0:T(8,128)S(1)}, f32[2,32,256]{2,1,0:T(8,128)S(1)}, f32[2,32,256]{2,1,0:T(8,128)S(1)}) custom-call(f32[128,256]{1,0:T(8,128)} %refs_0_.2, f32[128,256]{1,0:T(8,128)} %refs_1_.2), custom_call_target="tpu_custom_call" | custom-call | tf_op jit(solution)/shard_map/pallas_call | solution.py:355
  1.6 4.0 %collective-permute-start = (f32[2,32,256]{2,1,0:T(8,128)S(1)}, f32[2,32,256]{2,1,0:T(8,128)S(1)}, u32[]{:S(2)}, u32[]{:S(2)}) collective-permute-start(f32[2,32,256]{2,1,0:T(8,128)S(1)} %get-tuple-element.14), channel_id=1, source_target_pairs={{0,3},{1,2},{2,1},{3,0},{4,7},{5,6},{6,5},{7,4},{8,11},{9,10},{10,... | collective-permute-start | bytes 196616 | tf_op jit(solution)/shard_map/ppermute | solution.py:376
  5.6 0.5 %collective-permute-start.1 = (f32[2,32,256]{2,1,0:T(8,128)S(1)}, f32[2,32,256]{2,1,0:T(8,128)S(1)}, u32[]{:S(2)}, u32[]{:S(2)}) collective-permute-start(f32[2,32,256]{2,1,0:T(8,128)S(1)} %get-tuple-element.15), channel_id=1, source_target_pairs={{0,1},{1,0},{2,3},{3,2},{4,5},{5,4},{6,7},{7,6},{8,9},{9,8},{10,11... | collective-permute-start | bytes 196616 | tf_op jit(solution)/shard_map/ppermute | solution.py:376
  6.1 0.1 collective-permute-start.2
  6.2 1.6 %shard_map.60 = (f32[4,256,128]{2,1,0:T(8,128)S(1)}, bf16[2,4,256,256]{3,2,1,0:T(8,128)(2,1)S(1)}, bf16[2,4,256,256]{3,2,1,0:T(8,128)(2,1)S(1)}) custom-call(bf16[2,4,256,256]{3,2,1,0:T(8,128)(2,1)} %constant.4.clone.refs_0_, bf16[2,4,256,256]{3,2,1,0:T(8,128)(2,1)} %constant.5.clone.refs_1_), custom_call_target="tpu_custom_call" | custom-call | tf_op jit(solution)/shard_map/pallas_call | solution.py:355
  7.8 0.2 collective-permute-done.refs_1_
  8.0 1.9 %collective-permute-done.1.refs_2_ = f32[2,32,256]{2,1,0:T(8,128)S(1)} collective-permute-done((f32[2,32,256]{2,1,0:T(8,128)S(1)}, f32[2,32,256]{2,1,0:T(8,128)S(1)}, u32[]{:S(2)}, u32[]{:S(2)}) %collective-permute-start.1) | collective-permute-done | bytes 65568 | tf_op jit(solution)/shard_map/ppermute | solution.py:376
  9.8 0.5 %collective-permute-done.2.refs_3_ = f32[2,32,256]{2,1,0:T(8,128)S(1)} collective-permute-done((f32[2,32,256]{2,1,0:T(8,128)S(1)}, f32[2,32,256]{2,1,0:T(8,128)S(1)}, u32[]{:S(2)}, u32[]{:S(2)}) %collective-permute-start.2) | collective-permute-done | bytes 65568 | tf_op jit(solution)/shard_map/ppermute | solution.py:376
  10.4 0.6 %shard_map.61 = f32[32,24,128]{2,1,0:T(8,128)S(1)} custom-call(f32[2,32,256]{2,1,0:T(8,128)S(1)} %get-tuple-element.13.refs_0_, f32[2,32,256]{2,1,0:T(8,128)S(1)} %collective-permute-done.refs_1_, f32[2,32,256]{2,1,0:T(8,128)S(1)} %collective-permute-done.1.refs_2_, f32[2,32,256]{2,1,0:T(8,128)S(1)} %collective-permute-done.2.refs_3_, ...), custom_call_target="tpu_custom_call" | custom-call | tf_op jit(solution)/shard_map/pallas_call | solution.py:355
  11.0 16.5 %all_to_all.10.refs_0_ = f32[32,24,128]{2,1,0:T(8,128)S(1)} all-to-all(f32[32,24,128]{2,1,0:T(8,128)S(1)} %shard_map.61), channel_id=1, replica_groups=mesh['outer'=4,'core'=2,'col'=4] {'col','core','outer'}, dimensions={0} | all-to-all | bytes 786432 | tf_op jit(solution)/shard_map/all_to_all | solution.py:420
  27.5 1.1 %shard_map.62 = f32[32,16,128]{2,1,0:T(8,128)S(1)} custom-call(f32[32,24,128]{2,1,0:T(8,128)S(1)} %all_to_all.10.refs_0_, f32[4,256,128]{2,1,0:T(8,128)S(1)} %get-tuple-element.18.refs_1_, bf16[2,4,256,256]{3,2,1,0:T(8,128)(2,1)S(1)} %get-tuple-element.17.refs_4_.refs_2_, bf16[2,4,256,256]{3,2,1,0:T(8,128)(2,1)S(1)} %get-tuple-element.19.refs_3_.refs_1_), custom_call_target="tpu_custom_call" | custom-call | tf_op jit(solution)/shard_map/pallas_call | solution.py:355
  28.7 13.8 %all_to_all.11.refs_0_ = f32[32,16,128]{2,1,0:T(8,128)S(1)} all-to-all(f32[32,16,128]{2,1,0:T(8,128)S(1)} %shard_map.62), channel_id=1, replica_groups=mesh['outer'=4,'core'=2,'col'=4] {'col','core','outer'}, dimensions={0} | all-to-all | bytes 524288 | tf_op jit(solution)/shard_map/all_to_all | solution.py:437
  42.5 0.5 shard_map.63
  43.0 1.0 %collective-permute-start.3 = (f32[2,32,256]{2,1,0:T(8,128)S(1)}, f32[2,32,256]{2,1,0:T(8,128)S(1)}, u32[]{:S(2)}, u32[]{:S(2)}) collective-permute-start(f32[2,32,256]{2,1,0:T(8,128)S(1)} %get-tuple-element.21), channel_id=1, source_target_pairs={{0,3},{1,2},{2,1},{3,0},{4,7},{5,6},{6,5},{7,4},{8,11},{9,10},{10,... | collective-permute-start | bytes 196616 | tf_op jit(solution)/shard_map/ppermute | solution.py:376
  44.0 1.5 %collective-permute-start.4 = (f32[2,32,256]{2,1,0:T(8,128)S(1)}, f32[2,32,256]{2,1,0:T(8,128)S(1)}, u32[]{:S(2)}, u32[]{:S(2)}) collective-permute-start(f32[2,32,256]{2,1,0:T(8,128)S(1)} %get-tuple-element.22), channel_id=1, source_target_pairs={{0,1},{1,0},{2,3},{3,2},{4,5},{5,4},{6,7},{7,6},{8,9},{9,8},{10,11... | collective-permute-start | bytes 196616 | tf_op jit(solution)/shard_map/ppermute | solution.py:376
  45.5 1.0 %collective-permute-start.5 = (f32[2,32,256]{2,1,0:T(8,128)S(1)}, f32[2,32,256]{2,1,0:T(8,128)S(1)}, u32[]{:S(2)}, u32[]{:S(2)}) collective-permute-start(f32[2,32,256]{2,1,0:T(8,128)S(1)} %get-tuple-element.23), channel_id=1, source_target_pairs={{0,2},{1,3},{2,0},{3,1},{4,6},{5,7},{6,4},{7,5},{8,10},{9,11},{10,... | collective-permute-start | bytes 196616 | tf_op jit(solution)/shard_map/ppermute | solution.py:376
  46.5 2.4 %collective-permute-done.3.refs_1_ = f32[2,32,256]{2,1,0:T(8,128)S(1)} collective-permute-done((f32[2,32,256]{2,1,0:T(8,128)S(1)}, f32[2,32,256]{2,1,0:T(8,128)S(1)}, u32[]{:S(2)}, u32[]{:S(2)}) %collective-permute-start.3) | collective-permute-done | bytes 65568 | tf_op jit(solution)/shard_map/ppermute | solution.py:376
  48.9 0.2 collective-permute-done.4.refs_2_
  49.2 0.6 %collective-permute-done.5.refs_3_ = f32[2,32,256]{2,1,0:T(8,128)S(1)} collective-permute-done((f32[2,32,256]{2,1,0:T(8,128)S(1)}, f32[2,32,256]{2,1,0:T(8,128)S(1)}, u32[]{:S(2)}, u32[]{:S(2)}) %collective-permute-start.5) | collective-permute-done | bytes 65568 | tf_op jit(solution)/shard_map/ppermute | solution.py:376
  49.8 0.8 %shard_map.64 = (f32[128,256]{1,0:T(8,128)}, f32[128,256]{1,0:T(8,128)}) custom-call(f32[2,32,256]{2,1,0:T(8,128)S(1)} %get-tuple-element.20.refs_0_, f32[2,32,256]{2,1,0:T(8,128)S(1)} %collective-permute-done.3.refs_1_, f32[2,32,256]{2,1,0:T(8,128)S(1)} %collective-permute-done.4.refs_2_, f32[2,32,256]{2,1,0:T(8,128)S(1)} %collective-permute-done.5.refs_3_), custom_call_target="tpu_custom_call" | custom-call | tf_op jit(solution)/shard_map/pallas_call | solution.py:355
Async XLA Ops:
  1.6 6.4 %collective-permute-start = (f32[2,32,256]{2,1,0:T(8,128)S(1)}, f32[2,32,256]{2,1,0:T(8,128)S(1)}, u32[]{:S(2)}, u32[]{:S(2)}) collective-permute-start(f32[2,32,256]{2,1,0:T(8,128)S(1)} %get-tuple-element.14), channel_id=1, source_target_pairs={{0,3},{1,2},{2,1},{3,0},{4,7},{5,6},{6,5},{7,4},{8,11},{9,10},{10,... | collective-permute-start | bytes 196616 | tf_op jit(solution)/shard_map/ppermute | solution.py:376
  5.6 4.3 %collective-permute-start.1 = (f32[2,32,256]{2,1,0:T(8,128)S(1)}, f32[2,32,256]{2,1,0:T(8,128)S(1)}, u32[]{:S(2)}, u32[]{:S(2)}) collective-permute-start(f32[2,32,256]{2,1,0:T(8,128)S(1)} %get-tuple-element.15), channel_id=1, source_target_pairs={{0,1},{1,0},{2,3},{3,2},{4,5},{5,4},{6,7},{7,6},{8,9},{9,8},{10,11... | collective-permute-start | bytes 196616 | tf_op jit(solution)/shard_map/ppermute | solution.py:376
  6.1 4.3 %collective-permute-start.2 = (f32[2,32,256]{2,1,0:T(8,128)S(1)}, f32[2,32,256]{2,1,0:T(8,128)S(1)}, u32[]{:S(2)}, u32[]{:S(2)}) collective-permute-start(f32[2,32,256]{2,1,0:T(8,128)S(1)} %get-tuple-element.16), channel_id=1, source_target_pairs={{0,2},{1,3},{2,0},{3,1},{4,6},{5,7},{6,4},{7,5},{8,10},{9,11},{10,... | collective-permute-start | bytes 196616 | tf_op jit(solution)/shard_map/ppermute | solution.py:376
  43.0 5.9 %collective-permute-start.3 = (f32[2,32,256]{2,1,0:T(8,128)S(1)}, f32[2,32,256]{2,1,0:T(8,128)S(1)}, u32[]{:S(2)}, u32[]{:S(2)}) collective-permute-start(f32[2,32,256]{2,1,0:T(8,128)S(1)} %get-tuple-element.21), channel_id=1, source_target_pairs={{0,3},{1,2},{2,1},{3,0},{4,7},{5,6},{6,5},{7,4},{8,11},{9,10},{10,... | collective-permute-start | bytes 196616 | tf_op jit(solution)/shard_map/ppermute | solution.py:376
  44.0 5.1 %collective-permute-start.4 = (f32[2,32,256]{2,1,0:T(8,128)S(1)}, f32[2,32,256]{2,1,0:T(8,128)S(1)}, u32[]{:S(2)}, u32[]{:S(2)}) collective-permute-start(f32[2,32,256]{2,1,0:T(8,128)S(1)} %get-tuple-element.22), channel_id=1, source_target_pairs={{0,1},{1,0},{2,3},{3,2},{4,5},{5,4},{6,7},{7,6},{8,9},{9,8},{10,11... | collective-permute-start | bytes 196616 | tf_op jit(solution)/shard_map/ppermute | solution.py:376
  45.5 4.3 %collective-permute-start.5 = (f32[2,32,256]{2,1,0:T(8,128)S(1)}, f32[2,32,256]{2,1,0:T(8,128)S(1)}, u32[]{:S(2)}, u32[]{:S(2)}) collective-permute-start(f32[2,32,256]{2,1,0:T(8,128)S(1)} %get-tuple-element.23), channel_id=1, source_target_pairs={{0,2},{1,3},{2,0},{3,1},{4,6},{5,7},{6,4},{7,5},{8,10},{9,11},{10,... | collective-permute-start | bytes 196616 | tf_op jit(solution)/shard_map/ppermute | solution.py:376

commit v8 on v7

--- a/solution.py
+++ b/solution.py
@@ -341,14 +341,16 @@
 
 
 def join_kernel(*refs):
-    *block_refs, first_ref, second_ref, semaphores = refs
+    *block_refs, first_ref, second_ref, buffer_ref, semaphores = refs
     height = block_refs[0].shape[1]
-    copies = []
-    for index, (step, block_ref) in enumerate(zip(steps(len(block_refs)), block_refs)):
-        rows = pl.ds((lax.axis_index("col") ^ step) * height, height)
-        for field, out_ref in enumerate((first_ref, second_ref)):
-            copies.append(pltpu.make_async_copy(block_ref.at[field], out_ref.at[rows], semaphores.at[index, field]))
-    start_all(copies)
+    for step, block_ref in zip(steps(len(block_refs)), block_refs):
+        buffer_ref[:, pl.ds((lax.axis_index("col") ^ step) * height, height), :] = block_ref[...]
+    start_all(
+        [
+            pltpu.make_async_copy(buffer_ref.at[field], out_ref, semaphores.at[field])
+            for field, out_ref in enumerate((first_ref, second_ref))
+        ]
+    )
 
 
 def call(kernel, out_shape, specs, operands, scratch=(), out_spec=VMEM):
@@ -457,7 +459,7 @@
             [float_shape(row_count, col_count)] * 2,
             [VMEM] * count,
             (*blocks,),
-            [pltpu.SemaphoreType.DMA((count, 2))],
+            [pltpu.VMEM((2, row_count, col_count), jnp.float32), pltpu.SemaphoreType.DMA((2,))],
             HBM,
         )
     )

time: 50.8 us -> 50.8 us (level)
  no operation moved by 1% of the time
where the time goes in v8:
time: 50.8 us; the launch traced here: 50.5 us
  blocking collectives  30.4 us (60%)
  starting transfers between devices  8.18 us (16%)
  waiting for transfers between devices  5.84 us (11%)
  Pallas kernels  5.45 us (11%)
  between operations  0.67 us (1%)
    all_to_all x1, blocking collectives, on_device(): spectra = lax.all_to_all(spectra, AXES, 0, 0, tiled=True)  16.5 us
    all_to_all x1, blocking collectives, on_device(): advanced = lax.all_to_all(advanced, AXES, 0, 0, tiled=True)  13.8 us
    ppermute x6, starting transfers between devices, swap_blocks(): lax.ppermute(block, 'col', [(s, s ^ step) for s in range(count)])  8.18 us
    ppermute x6, waiting for transfers between devices, swap_blocks(): lax.ppermute(block, 'col', [(s, s ^ step) for s in range(count)])  5.84 us
    pallas_call x6, Pallas kernels, call(): pl.pallas_call(kernel, out_shape=out_shape, in_specs=specs, out_specs=jax...  5.45 us
  transfers between devices with their start and end apart: 6, of which 6 were waited for; matrix products, arithmetic and copies ran while one was open for 0% of the time, Pallas kernels for 3%

profile of v8, /device:TPU:0, one launch (start us, length us, event | category | flops | bytes accessed | tf_op | source)
XLA Modules:
  0.0 50.5 jit_solution(7065843680199170852)
XLA Ops:
  0.6 1.0 %shard_map.59 = (f32[2,32,256]{2,1,0:T(8,128)S(1)}, f32[2,32,256]{2,1,0:T(8,128)S(1)}, f32[2,32,256]{2,1,0:T(8,128)S(1)}, f32[2,32,256]{2,1,0:T(8,128)S(1)}) custom-call(f32[128,256]{1,0:T(8,128)} %refs_0_.2, f32[128,256]{1,0:T(8,128)} %refs_1_.2), custom_call_target="tpu_custom_call" | custom-call | tf_op jit(solution)/shard_map/pallas_call | solution.py:357
  1.6 4.0 %collective-permute-start = (f32[2,32,256]{2,1,0:T(8,128)S(1)}, f32[2,32,256]{2,1,0:T(8,128)S(1)}, u32[]{:S(2)}, u32[]{:S(2)}) collective-permute-start(f32[2,32,256]{2,1,0:T(8,128)S(1)} %get-tuple-element.14), channel_id=1, source_target_pairs={{0,3},{1,2},{2,1},{3,0},{4,7},{5,6},{6,5},{7,4},{8,11},{9,10},{10,... | collective-permute-start | bytes 196616 | tf_op jit(solution)/shard_map/ppermute | solution.py:378
  5.6 0.5 %collective-permute-start.1 = (f32[2,32,256]{2,1,0:T(8,128)S(1)}, f32[2,32,256]{2,1,0:T(8,128)S(1)}, u32[]{:S(2)}, u32[]{:S(2)}) collective-permute-start(f32[2,32,256]{2,1,0:T(8,128)S(1)} %get-tuple-element.15), channel_id=1, source_target_pairs={{0,1},{1,0},{2,3},{3,2},{4,5},{5,4},{6,7},{7,6},{8,9},{9,8},{10,11... | collective-permute-start | bytes 196616 | tf_op jit(solution)/shard_map/ppermute | solution.py:378
  6.1 0.1 collective-permute-start.2
  6.2 1.6 %shard_map.60 = (f32[4,256,128]{2,1,0:T(8,128)S(1)}, bf16[2,4,256,256]{3,2,1,0:T(8,128)(2,1)S(1)}, bf16[2,4,256,256]{3,2,1,0:T(8,128)(2,1)S(1)}) custom-call(bf16[2,4,256,256]{3,2,1,0:T(8,128)(2,1)} %constant.4.clone.refs_0_, bf16[2,4,256,256]{3,2,1,0:T(8,128)(2,1)} %constant.5.clone.refs_1_), custom_call_target="tpu_custom_call" | custom-call | tf_op jit(solution)/shard_map/pallas_call | solution.py:357
  7.8 0.2 collective-permute-done.refs_1_
  8.0 1.9 %collective-permute-done.1.refs_2_ = f32[2,32,256]{2,1,0:T(8,128)S(1)} collective-permute-done((f32[2,32,256]{2,1,0:T(8,128)S(1)}, f32[2,32,256]{2,1,0:T(8,128)S(1)}, u32[]{:S(2)}, u32[]{:S(2)}) %collective-permute-start.1) | collective-permute-done | bytes 65568 | tf_op jit(solution)/shard_map/ppermute | solution.py:378
  9.8 0.5 %collective-permute-done.2.refs_3_ = f32[2,32,256]{2,1,0:T(8,128)S(1)} collective-permute-done((f32[2,32,256]{2,1,0:T(8,128)S(1)}, f32[2,32,256]{2,1,0:T(8,128)S(1)}, u32[]{:S(2)}, u32[]{:S(2)}) %collective-permute-start.2) | collective-permute-done | bytes 65568 | tf_op jit(solution)/shard_map/ppermute | solution.py:378
  10.4 0.6 %shard_map.61 = f32[32,24,128]{2,1,0:T(8,128)S(1)} custom-call(f32[2,32,256]{2,1,0:T(8,128)S(1)} %get-tuple-element.13.refs_0_, f32[2,32,256]{2,1,0:T(8,128)S(1)} %collective-permute-done.refs_1_, f32[2,32,256]{2,1,0:T(8,128)S(1)} %collective-permute-done.1.refs_2_, f32[2,32,256]{2,1,0:T(8,128)S(1)} %collective-permute-done.2.refs_3_, ...), custom_call_target="tpu_custom_call" | custom-call | tf_op jit(solution)/shard_map/pallas_call | solution.py:357
  11.0 16.5 %all_to_all.10.refs_0_ = f32[32,24,128]{2,1,0:T(8,128)S(1)} all-to-all(f32[32,24,128]{2,1,0:T(8,128)S(1)} %shard_map.61), channel_id=1, replica_groups=mesh['outer'=4,'core'=2,'col'=4] {'col','core','outer'}, dimensions={0} | all-to-all | bytes 786432 | tf_op jit(solution)/shard_map/all_to_all | solution.py:422
  27.5 1.1 %shard_map.62 = f32[32,16,128]{2,1,0:T(8,128)S(1)} custom-call(f32[32,24,128]{2,1,0:T(8,128)S(1)} %all_to_all.10.refs_0_, f32[4,256,128]{2,1,0:T(8,128)S(1)} %get-tuple-element.18.refs_1_, bf16[2,4,256,256]{3,2,1,0:T(8,128)(2,1)S(1)} %get-tuple-element.17.refs_4_.refs_2_, bf16[2,4,256,256]{3,2,1,0:T(8,128)(2,1)S(1)} %get-tuple-element.19.refs_3_.refs_1_), custom_call_target="tpu_custom_call" | custom-call | tf_op jit(solution)/shard_map/pallas_call | solution.py:357
  28.7 13.8 %all_to_all.11.refs_0_ = f32[32,16,128]{2,1,0:T(8,128)S(1)} all-to-all(f32[32,16,128]{2,1,0:T(8,128)S(1)} %shard_map.62), channel_id=1, replica_groups=mesh['outer'=4,'core'=2,'col'=4] {'col','core','outer'}, dimensions={0} | all-to-all | bytes 524288 | tf_op jit(solution)/shard_map/all_to_all | solution.py:439
  42.5 0.5 shard_map.63
  43.0 1.0 %collective-permute-start.3 = (f32[2,32,256]{2,1,0:T(8,128)S(1)}, f32[2,32,256]{2,1,0:T(8,128)S(1)}, u32[]{:S(2)}, u32[]{:S(2)}) collective-permute-start(f32[2,32,256]{2,1,0:T(8,128)S(1)} %get-tuple-element.21), channel_id=1, source_target_pairs={{0,3},{1,2},{2,1},{3,0},{4,7},{5,6},{6,5},{7,4},{8,11},{9,10},{10,... | collective-permute-start | bytes 196616 | tf_op jit(solution)/shard_map/ppermute | solution.py:378
  44.0 1.5 %collective-permute-start.4 = (f32[2,32,256]{2,1,0:T(8,128)S(1)}, f32[2,32,256]{2,1,0:T(8,128)S(1)}, u32[]{:S(2)}, u32[]{:S(2)}) collective-permute-start(f32[2,32,256]{2,1,0:T(8,128)S(1)} %get-tuple-element.22), channel_id=1, source_target_pairs={{0,1},{1,0},{2,3},{3,2},{4,5},{5,4},{6,7},{7,6},{8,9},{9,8},{10,11... | collective-permute-start | bytes 196616 | tf_op jit(solution)/shard_map/ppermute | solution.py:378
  45.5 1.0 %collective-permute-start.5 = (f32[2,32,256]{2,1,0:T(8,128)S(1)}, f32[2,32,256]{2,1,0:T(8,128)S(1)}, u32[]{:S(2)}, u32[]{:S(2)}) collective-permute-start(f32[2,32,256]{2,1,0:T(8,128)S(1)} %get-tuple-element.23), channel_id=1, source_target_pairs={{0,2},{1,3},{2,0},{3,1},{4,6},{5,7},{6,4},{7,5},{8,10},{9,11},{10,... | collective-permute-start | bytes 196616 | tf_op jit(solution)/shard_map/ppermute | solution.py:378
  46.5 2.4 %collective-permute-done.3.refs_1_ = f32[2,32,256]{2,1,0:T(8,128)S(1)} collective-permute-done((f32[2,32,256]{2,1,0:T(8,128)S(1)}, f32[2,32,256]{2,1,0:T(8,128)S(1)}, u32[]{:S(2)}, u32[]{:S(2)}) %collective-permute-start.3) | collective-permute-done | bytes 65568 | tf_op jit(solution)/shard_map/ppermute | solution.py:378
  48.9 0.2 collective-permute-done.4.refs_2_
  49.2 0.6 %collective-permute-done.5.refs_3_ = f32[2,32,256]{2,1,0:T(8,128)S(1)} collective-permute-done((f32[2,32,256]{2,1,0:T(8,128)S(1)}, f32[2,32,256]{2,1,0:T(8,128)S(1)}, u32[]{:S(2)}, u32[]{:S(2)}) %collective-permute-start.5) | collective-permute-done | bytes 65568 | tf_op jit(solution)/shard_map/ppermute | solution.py:378
  49.8 0.7 %shard_map.64 = (f32[128,256]{1,0:T(8,128)}, f32[128,256]{1,0:T(8,128)}) custom-call(f32[2,32,256]{2,1,0:T(8,128)S(1)} %get-tuple-element.20.refs_0_, f32[2,32,256]{2,1,0:T(8,128)S(1)} %collective-permute-done.3.refs_1_, f32[2,32,256]{2,1,0:T(8,128)S(1)} %collective-permute-done.4.refs_2_, f32[2,32,256]{2,1,0:T(8,128)S(1)} %collective-permute-done.5.refs_3_), custom_call_target="tpu_custom_call" | custom-call | tf_op jit(solution)/shard_map/pallas_call | solution.py:357
Async XLA Ops:
  1.6 6.4 %collective-permute-start = (f32[2,32,256]{2,1,0:T(8,128)S(1)}, f32[2,32,256]{2,1,0:T(8,128)S(1)}, u32[]{:S(2)}, u32[]{:S(2)}) collective-permute-start(f32[2,32,256]{2,1,0:T(8,128)S(1)} %get-tuple-element.14), channel_id=1, source_target_pairs={{0,3},{1,2},{2,1},{3,0},{4,7},{5,6},{6,5},{7,4},{8,11},{9,10},{10,... | collective-permute-start | bytes 196616 | tf_op jit(solution)/shard_map/ppermute | solution.py:378
  5.6 4.3 %collective-permute-start.1 = (f32[2,32,256]{2,1,0:T(8,128)S(1)}, f32[2,32,256]{2,1,0:T(8,128)S(1)}, u32[]{:S(2)}, u32[]{:S(2)}) collective-permute-start(f32[2,32,256]{2,1,0:T(8,128)S(1)} %get-tuple-element.15), channel_id=1, source_target_pairs={{0,1},{1,0},{2,3},{3,2},{4,5},{5,4},{6,7},{7,6},{8,9},{9,8},{10,11... | collective-permute-start | bytes 196616 | tf_op jit(solution)/shard_map/ppermute | solution.py:378
  6.1 4.3 %collective-permute-start.2 = (f32[2,32,256]{2,1,0:T(8,128)S(1)}, f32[2,32,256]{2,1,0:T(8,128)S(1)}, u32[]{:S(2)}, u32[]{:S(2)}) collective-permute-start(f32[2,32,256]{2,1,0:T(8,128)S(1)} %get-tuple-element.16), channel_id=1, source_target_pairs={{0,2},{1,3},{2,0},{3,1},{4,6},{5,7},{6,4},{7,5},{8,10},{9,11},{10,... | collective-permute-start | bytes 196616 | tf_op jit(solution)/shard_map/ppermute | solution.py:378
  43.0 5.9 %collective-permute-start.3 = (f32[2,32,256]{2,1,0:T(8,128)S(1)}, f32[2,32,256]{2,1,0:T(8,128)S(1)}, u32[]{:S(2)}, u32[]{:S(2)}) collective-permute-start(f32[2,32,256]{2,1,0:T(8,128)S(1)} %get-tuple-element.21), channel_id=1, source_target_pairs={{0,3},{1,2},{2,1},{3,0},{4,7},{5,6},{6,5},{7,4},{8,11},{9,10},{10,... | collective-permute-start | bytes 196616 | tf_op jit(solution)/shard_map/ppermute | solution.py:378
  44.0 5.1 %collective-permute-start.4 = (f32[2,32,256]{2,1,0:T(8,128)S(1)}, f32[2,32,256]{2,1,0:T(8,128)S(1)}, u32[]{:S(2)}, u32[]{:S(2)}) collective-permute-start(f32[2,32,256]{2,1,0:T(8,128)S(1)} %get-tuple-element.22), channel_id=1, source_target_pairs={{0,1},{1,0},{2,3},{3,2},{4,5},{5,4},{6,7},{7,6},{8,9},{9,8},{10,11... | collective-permute-start | bytes 196616 | tf_op jit(solution)/shard_map/ppermute | solution.py:378
  45.5 4.3 %collective-permute-start.5 = (f32[2,32,256]{2,1,0:T(8,128)S(1)}, f32[2,32,256]{2,1,0:T(8,128)S(1)}, u32[]{:S(2)}, u32[]{:S(2)}) collective-permute-start(f32[2,32,256]{2,1,0:T(8,128)S(1)} %get-tuple-element.23), channel_id=1, source_target_pairs={{0,2},{1,3},{2,0},{3,1},{4,6},{5,7},{6,4},{7,5},{8,10},{9,11},{10,... | collective-permute-start | bytes 196616 | tf_op jit(solution)/shard_map/ppermute | solution.py:378

commit v9 on v7

--- a/solution.py
+++ b/solution.py
@@ -318,7 +318,7 @@
 
 
 def steps(count):
-    return [0, count - 1] + list(range(1, count - 1))
+    return [0] + list(range(count - 1, 0, -1))
 
 
 def start_all(copies):

time: 50.8 us -> 50.8 us (level)
  transfers between devices with their start and end apart: 6 -> 6, of which waited for: 6 -> 5; matrix products, arithmetic and copies ran while one was open for 0% -> 0% of each run, Pallas kernels for 3% -> 3%
where the time goes in v9:
time: 50.8 us; the launch traced here: 50.5 us
  blocking collectives  30.4 us (60%)
  starting transfers between devices  8.18 us (16%)
  waiting for transfers between devices  5.79 us (11%)
  Pallas kernels  5.47 us (11%)
  between operations  0.67 us (1%)
    all_to_all x1, blocking collectives, on_device(): spectra = lax.all_to_all(spectra, AXES, 0, 0, tiled=True)  16.6 us
    all_to_all x1, blocking collectives, on_device(): advanced = lax.all_to_all(advanced, AXES, 0, 0, tiled=True)  13.8 us
    ppermute x6, starting transfers between devices, swap_blocks(): lax.ppermute(block, 'col', [(s, s ^ step) for s in range(count)])  8.18 us
    ppermute x6, waiting for transfers between devices, swap_blocks(): lax.ppermute(block, 'col', [(s, s ^ step) for s in range(count)])  5.79 us
    pallas_call x6, Pallas kernels, call(): pl.pallas_call(kernel, out_shape=out_shape, in_specs=specs, out_specs=jax...  5.47 us
  transfers between devices with their start and end apart: 6, of which 5 were waited for; matrix products, arithmetic and copies ran while one was open for 0% of the time, Pallas kernels for 3%

profile of v9, /device:TPU:0, one launch (start us, length us, event | category | flops | bytes accessed | tf_op | source)
XLA Modules:
  0.0 50.5 jit_solution(9418100409418458245)
XLA Ops:
  0.6 1.0 %shard_map.59 = (f32[2,32,256]{2,1,0:T(8,128)S(1)}, f32[2,32,256]{2,1,0:T(8,128)S(1)}, f32[2,32,256]{2,1,0:T(8,128)S(1)}, f32[2,32,256]{2,1,0:T(8,128)S(1)}) custom-call(f32[128,256]{1,0:T(8,128)} %refs_0_.2, f32[128,256]{1,0:T(8,128)} %refs_1_.2), custom_call_target="tpu_custom_call" | custom-call | tf_op jit(solution)/shard_map/pallas_call | solution.py:355
  1.6 4.0 %collective-permute-start = (f32[2,32,256]{2,1,0:T(8,128)S(1)}, f32[2,32,256]{2,1,0:T(8,128)S(1)}, u32[]{:S(2)}, u32[]{:S(2)}) collective-permute-start(f32[2,32,256]{2,1,0:T(8,128)S(1)} %get-tuple-element.14), channel_id=1, source_target_pairs={{0,3},{1,2},{2,1},{3,0},{4,7},{5,6},{6,5},{7,4},{8,11},{9,10},{10,... | collective-permute-start | bytes 196616 | tf_op jit(solution)/shard_map/ppermute | solution.py:376
  5.6 0.5 %collective-permute-start.1 = (f32[2,32,256]{2,1,0:T(8,128)S(1)}, f32[2,32,256]{2,1,0:T(8,128)S(1)}, u32[]{:S(2)}, u32[]{:S(2)}) collective-permute-start(f32[2,32,256]{2,1,0:T(8,128)S(1)} %get-tuple-element.15), channel_id=1, source_target_pairs={{0,2},{1,3},{2,0},{3,1},{4,6},{5,7},{6,4},{7,5},{8,10},{9,11},{10,... | collective-permute-start | bytes 196616 | tf_op jit(solution)/shard_map/ppermute | solution.py:376
  6.1 0.1 collective-permute-start.2
  6.2 1.6 %shard_map.60 = (f32[4,256,128]{2,1,0:T(8,128)S(1)}, bf16[2,4,256,256]{3,2,1,0:T(8,128)(2,1)S(1)}, bf16[2,4,256,256]{3,2,1,0:T(8,128)(2,1)S(1)}) custom-call(bf16[2,4,256,256]{3,2,1,0:T(8,128)(2,1)} %constant.4.clone.refs_0_, bf16[2,4,256,256]{3,2,1,0:T(8,128)(2,1)} %constant.5.clone.refs_1_), custom_call_target="tpu_custom_call" | custom-call | tf_op jit(solution)/shard_map/pallas_call | solution.py:355
  7.8 0.0 collective-permute-done.refs_1_
  7.8 2.0 %collective-permute-done.1.refs_2_ = f32[2,32,256]{2,1,0:T(8,128)S(1)} collective-permute-done((f32[2,32,256]{2,1,0:T(8,128)S(1)}, f32[2,32,256]{2,1,0:T(8,128)S(1)}, u32[]{:S(2)}, u32[]{:S(2)}) %collective-permute-start.1) | collective-permute-done | bytes 65568 | tf_op jit(solution)/shard_map/ppermute | solution.py:376
  9.8 0.5 %collective-permute-done.2.refs_3_ = f32[2,32,256]{2,1,0:T(8,128)S(1)} collective-permute-done((f32[2,32,256]{2,1,0:T(8,128)S(1)}, f32[2,32,256]{2,1,0:T(8,128)S(1)}, u32[]{:S(2)}, u32[]{:S(2)}) %collective-permute-start.2) | collective-permute-done | bytes 65568 | tf_op jit(solution)/shard_map/ppermute | solution.py:376
  10.3 0.6 %shard_map.61 = f32[32,24,128]{2,1,0:T(8,128)S(1)} custom-call(f32[2,32,256]{2,1,0:T(8,128)S(1)} %get-tuple-element.13.refs_0_, f32[2,32,256]{2,1,0:T(8,128)S(1)} %collective-permute-done.refs_1_, f32[2,32,256]{2,1,0:T(8,128)S(1)} %collective-permute-done.1.refs_2_, f32[2,32,256]{2,1,0:T(8,128)S(1)} %collective-permute-done.2.refs_3_, ...), custom_call_target="tpu_custom_call" | custom-call | tf_op jit(solution)/shard_map/pallas_call | solution.py:355
  10.9 16.6 %all_to_all.10.refs_0_ = f32[32,24,128]{2,1,0:T(8,128)S(1)} all-to-all(f32[32,24,128]{2,1,0:T(8,128)S(1)} %shard_map.61), channel_id=1, replica_groups=mesh['outer'=4,'core'=2,'col'=4] {'col','core','outer'}, dimensions={0} | all-to-all | bytes 786432 | tf_op jit(solution)/shard_map/all_to_all | solution.py:420
  27.5 1.1 %shard_map.62 = f32[32,16,128]{2,1,0:T(8,128)S(1)} custom-call(f32[32,24,128]{2,1,0:T(8,128)S(1)} %all_to_all.10.refs_0_, f32[4,256,128]{2,1,0:T(8,128)S(1)} %get-tuple-element.18.refs_1_, bf16[2,4,256,256]{3,2,1,0:T(8,128)(2,1)S(1)} %get-tuple-element.17.refs_4_.refs_2_, bf16[2,4,256,256]{3,2,1,0:T(8,128)(2,1)S(1)} %get-tuple-element.19.refs_3_.refs_1_), custom_call_target="tpu_custom_call" | custom-call | tf_op jit(solution)/shard_map/pallas_call | solution.py:355
  28.7 13.8 %all_to_all.11.refs_0_ = f32[32,16,128]{2,1,0:T(8,128)S(1)} all-to-all(f32[32,16,128]{2,1,0:T(8,128)S(1)} %shard_map.62), channel_id=1, replica_groups=mesh['outer'=4,'core'=2,'col'=4] {'col','core','outer'}, dimensions={0} | all-to-all | bytes 524288 | tf_op jit(solution)/shard_map/all_to_all | solution.py:437
  42.5 0.5 shard_map.63
  43.0 1.0 %collective-permute-start.3 = (f32[2,32,256]{2,1,0:T(8,128)S(1)}, f32[2,32,256]{2,1,0:T(8,128)S(1)}, u32[]{:S(2)}, u32[]{:S(2)}) collective-permute-start(f32[2,32,256]{2,1,0:T(8,128)S(1)} %get-tuple-element.21), channel_id=1, source_target_pairs={{0,3},{1,2},{2,1},{3,0},{4,7},{5,6},{6,5},{7,4},{8,11},{9,10},{10,... | collective-permute-start | bytes 196616 | tf_op jit(solution)/shard_map/ppermute | solution.py:376
  44.0 1.5 %collective-permute-start.4 = (f32[2,32,256]{2,1,0:T(8,128)S(1)}, f32[2,32,256]{2,1,0:T(8,128)S(1)}, u32[]{:S(2)}, u32[]{:S(2)}) collective-permute-start(f32[2,32,256]{2,1,0:T(8,128)S(1)} %get-tuple-element.22), channel_id=1, source_target_pairs={{0,2},{1,3},{2,0},{3,1},{4,6},{5,7},{6,4},{7,5},{8,10},{9,11},{10,... | collective-permute-start | bytes 196616 | tf_op jit(solution)/shard_map/ppermute | solution.py:376
  45.5 1.0 %collective-permute-start.5 = (f32[2,32,256]{2,1,0:T(8,128)S(1)}, f32[2,32,256]{2,1,0:T(8,128)S(1)}, u32[]{:S(2)}, u32[]{:S(2)}) collective-permute-start(f32[2,32,256]{2,1,0:T(8,128)S(1)} %get-tuple-element.23), channel_id=1, source_target_pairs={{0,1},{1,0},{2,3},{3,2},{4,5},{5,4},{6,7},{7,6},{8,9},{9,8},{10,11... | collective-permute-start | bytes 196616 | tf_op jit(solution)/shard_map/ppermute | solution.py:376
  46.5 2.3 %collective-permute-done.3.refs_1_ = f32[2,32,256]{2,1,0:T(8,128)S(1)} collective-permute-done((f32[2,32,256]{2,1,0:T(8,128)S(1)}, f32[2,32,256]{2,1,0:T(8,128)S(1)}, u32[]{:S(2)}, u32[]{:S(2)}) %collective-permute-start.3) | collective-permute-done | bytes 65568 | tf_op jit(solution)/shard_map/ppermute | solution.py:376
  48.8 0.6 %collective-permute-done.4.refs_2_ = f32[2,32,256]{2,1,0:T(8,128)S(1)} collective-permute-done((f32[2,32,256]{2,1,0:T(8,128)S(1)}, f32[2,32,256]{2,1,0:T(8,128)S(1)}, u32[]{:S(2)}, u32[]{:S(2)}) %collective-permute-start.4) | collective-permute-done | bytes 65568 | tf_op jit(solution)/shard_map/ppermute | solution.py:376
  49.4 0.4 collective-permute-done.5.refs_3_
  49.8 0.8 %shard_map.64 = (f32[128,256]{1,0:T(8,128)}, f32[128,256]{1,0:T(8,128)}) custom-call(f32[2,32,256]{2,1,0:T(8,128)S(1)} %get-tuple-element.20.refs_0_, f32[2,32,256]{2,1,0:T(8,128)S(1)} %collective-permute-done.3.refs_1_, f32[2,32,256]{2,1,0:T(8,128)S(1)} %collective-permute-done.4.refs_2_, f32[2,32,256]{2,1,0:T(8,128)S(1)} %collective-permute-done.5.refs_3_), custom_call_target="tpu_custom_call" | custom-call | tf_op jit(solution)/shard_map/pallas_call | solution.py:355
Async XLA Ops:
  1.6 6.2 %collective-permute-start = (f32[2,32,256]{2,1,0:T(8,128)S(1)}, f32[2,32,256]{2,1,0:T(8,128)S(1)}, u32[]{:S(2)}, u32[]{:S(2)}) collective-permute-start(f32[2,32,256]{2,1,0:T(8,128)S(1)} %get-tuple-element.14), channel_id=1, source_target_pairs={{0,3},{1,2},{2,1},{3,0},{4,7},{5,6},{6,5},{7,4},{8,11},{9,10},{10,... | collective-permute-start | bytes 196616 | tf_op jit(solution)/shard_map/ppermute | solution.py:376
  5.6 4.3 %collective-permute-start.1 = (f32[2,32,256]{2,1,0:T(8,128)S(1)}, f32[2,32,256]{2,1,0:T(8,128)S(1)}, u32[]{:S(2)}, u32[]{:S(2)}) collective-permute-start(f32[2,32,256]{2,1,0:T(8,128)S(1)} %get-tuple-element.15), channel_id=1, source_target_pairs={{0,2},{1,3},{2,0},{3,1},{4,6},{5,7},{6,4},{7,5},{8,10},{9,11},{10,... | collective-permute-start | bytes 196616 | tf_op jit(solution)/shard_map/ppermute | solution.py:376
  6.1 4.3 %collective-permute-start.2 = (f32[2,32,256]{2,1,0:T(8,128)S(1)}, f32[2,32,256]{2,1,0:T(8,128)S(1)}, u32[]{:S(2)}, u32[]{:S(2)}) collective-permute-start(f32[2,32,256]{2,1,0:T(8,128)S(1)} %get-tuple-element.16), channel_id=1, source_target_pairs={{0,1},{1,0},{2,3},{3,2},{4,5},{5,4},{6,7},{7,6},{8,9},{9,8},{10,11... | collective-permute-start | bytes 196616 | tf_op jit(solution)/shard_map/ppermute | solution.py:376
  43.0 5.8 %collective-permute-start.3 = (f32[2,32,256]{2,1,0:T(8,128)S(1)}, f32[2,32,256]{2,1,0:T(8,128)S(1)}, u32[]{:S(2)}, u32[]{:S(2)}) collective-permute-start(f32[2,32,256]{2,1,0:T(8,128)S(1)} %get-tuple-element.21), channel_id=1, source_target_pairs={{0,3},{1,2},{2,1},{3,0},{4,7},{5,6},{6,5},{7,4},{8,11},{9,10},{10,... | collective-permute-start | bytes 196616 | tf_op jit(solution)/shard_map/ppermute | solution.py:376
  44.0 5.4 %collective-permute-start.4 = (f32[2,32,256]{2,1,0:T(8,128)S(1)}, f32[2,32,256]{2,1,0:T(8,128)S(1)}, u32[]{:S(2)}, u32[]{:S(2)}) collective-permute-start(f32[2,32,256]{2,1,0:T(8,128)S(1)} %get-tuple-element.22), channel_id=1, source_target_pairs={{0,2},{1,3},{2,0},{3,1},{4,6},{5,7},{6,4},{7,5},{8,10},{9,11},{10,... | collective-permute-start | bytes 196616 | tf_op jit(solution)/shard_map/ppermute | solution.py:376
  45.5 4.3 %collective-permute-start.5 = (f32[2,32,256]{2,1,0:T(8,128)S(1)}, f32[2,32,256]{2,1,0:T(8,128)S(1)}, u32[]{:S(2)}, u32[]{:S(2)}) collective-permute-start(f32[2,32,256]{2,1,0:T(8,128)S(1)} %get-tuple-element.23), channel_id=1, source_target_pairs={{0,1},{1,0},{2,3},{3,2},{4,5},{5,4},{6,7},{7,6},{8,9},{9,8},{10,11... | collective-permute-start | bytes 196616 | tf_op jit(solution)/shard_map/ppermute | solution.py:376
